TPU v7x, 32 devices: a whole 2x2x4 slice. The times are simulated.
32 devices in a mesh: groups: 2 (over y), rows: 4 (over z), cols: 4 (over x, core).
Axes of the slice: x: 2, y: 2, z: 4, core: 2. Of those that a mesh axis runs over, the one named last changes fastest.
Arguments:
- alignment_features: float32 [128, 32, 64], P(('groups', 'rows'), 'cols'), parts along dimension 0, may hold values from -6 to 6
- affine_factor: float32 [64], replicated, may hold values from 0.25 to 1.75
- affine_offset: float32 [64], replicated, may hold values from -3 to 3
- first_projector: bfloat16 [64, 32], replicated, may hold values from -0.75 to 0.75
- second_projector: bfloat16 [64, 32], replicated, may hold values from -0.75 to 0.75
- final_projector: bfloat16 [1024, 128], replicated, may hold values from -0.75 to 0.75
- additive_term: float32 [128], replicated, may hold values from -3 to 3
- adjoint_update: bfloat16 [128, 64, 128], P(('groups', 'rows'), 'cols'), parts along dimension 0, may hold values from -6 to 6
Outputs:
- residue_update: bfloat16 [128, 64, 128], P(('groups', 'rows'), 'cols'), parts along dimension 0
- alignment_slope: float32 [128, 32, 64], P(('groups', 'rows'), 'cols'), parts along dimension 0
- final_projector_slope: float32 [2048, 128], P(('groups', 'rows', 'cols')), parts along dimension 0
- first_projector_slope: float32 [128, 32], P('groups'), parts along dimension 0
- second_projector_slope: float32 [128, 32], P('groups'), parts along dimension 0
There are 2 independent parts, one for each index of `groups`. A program takes and returns all parts, laid end to end along the dimension named above; an argument that names none is the same for every part. Nothing has to cross between parts.
All inputs are finite; a program needn't handle non-finite values.
Results may differ from a plain program's by a relative error of at most 0.0061.
Values may be sent and summed in bfloat16 or wider, within the bound.
No kernel may reach another device: no remote copies, remote signals or barrier semaphores. Data moves between devices by JAX's collectives and lax.ppermute only.
A program may use at most 64 MiB of HBM per device.

v0:
```python
import jax
import jax.numpy as jnp
from jax import lax
from jax.sharding import PartitionSpec as P


def layernorm_parts(alignment_features, affine_factor, affine_offset):
    centered_alignment = alignment_features - jnp.mean(alignment_features, axis=-1, keepdims=True)
    reciprocal_spread = lax.rsqrt(
        jnp.mean(centered_alignment * centered_alignment, axis=-1, keepdims=True) + 1e-05
    )
    zscored_alignment = centered_alignment * reciprocal_spread
    return (
        zscored_alignment,
        reciprocal_spread,
        (zscored_alignment * affine_factor + affine_offset).astype(jnp.bfloat16),
    )


def local(
    alignment_features,
    affine_factor,
    affine_offset,
    first_projector,
    second_projector,
    final_projector,
    additive_term,
    adjoint_update,
):
    zscored_alignment, reciprocal_spread, unit_alignment = layernorm_parts(
        alignment_features, affine_factor, affine_offset
    )
    first_factor_here = jnp.dot(
        unit_alignment, first_projector, preferred_element_type=jnp.float32
    ).astype(jnp.bfloat16)
    second_factor_here = jnp.dot(
        unit_alignment, second_projector, preferred_element_type=jnp.float32
    ).astype(jnp.bfloat16)
    tokens, quarter, chans = first_factor_here.shape
    left_flat = first_factor_here.reshape(tokens, quarter * chans)
    right_flat = second_factor_here.reshape(tokens, quarter * chans)
    left_wide, right_wide = (
        lax.all_gather(left_flat, "cols", axis=1, tiled=True),
        lax.all_gather(right_flat, "cols", axis=1, tiled=True),
    )
    left_rows = left_wide.reshape(tokens, -1, chans)
    right_all = lax.all_gather(right_wide, "rows", axis=0, tiled=True)
    block = right_all.shape[0] // lax.axis_size("cols")
    right_cols = lax.dynamic_slice_in_dim(
        right_all, lax.axis_index("cols") * block, block, 0
    ).reshape(block, -1, chans)
    seqs = left_rows.shape[1]
    multiplier = 1.0 / seqs
    pair_ch = adjoint_update.shape[2]
    step_rows = 4
    rounds = tokens // step_rows
    first_tile_list = left_rows.reshape(rounds, step_rows, seqs, chans)
    cot_blocks = adjoint_update.reshape(rounds, step_rows, block, pair_ch)

    def advance(carry, inputs):
        right_acc, out_acc = carry
        left_slab, cot_slab = inputs
        outer = (
            jnp.einsum("isc,jsd->ijcd", left_slab, right_cols, preferred_element_type=jnp.float32)
            * multiplier
        ).astype(jnp.bfloat16)
        flat = outer.reshape(step_rows * block, chans * chans)
        cot_flat = cot_slab.reshape(step_rows * block, pair_ch)
        update = (
            jnp.dot(flat, final_projector, preferred_element_type=jnp.float32) + additive_term
        ).astype(jnp.bfloat16)
        outer_grad = jnp.dot(
            cot_flat, final_projector.T, preferred_element_type=jnp.float32
        ).astype(jnp.bfloat16)
        outer_grad = outer_grad.reshape(step_rows, block, chans, chans)
        left_piece = (
            jnp.einsum("ijcd,jsd->isc", outer_grad, right_cols, preferred_element_type=jnp.float32)
            * multiplier
        )
        right_acc = (
            right_acc
            + jnp.einsum("ijcd,isc->jsd", outer_grad, left_slab, preferred_element_type=jnp.float32)
            * multiplier
        )
        out_acc = out_acc + jnp.einsum(
            "fk,fe->ke", flat, cot_flat, preferred_element_type=jnp.float32
        )
        return ((right_acc, out_acc), (update.reshape(step_rows, block, pair_ch), left_piece))

    beginning_position = (
        jnp.zeros((block, seqs, chans), jnp.float32),
        jnp.zeros((chans * chans, pair_ch), jnp.float32),
    )
    (right_part, out_term), (updates, left_pieces) = lax.scan(
        advance, beginning_position, (first_tile_list, cot_blocks)
    )
    residue_update = updates.reshape(tokens, block, pair_ch)
    left_part = left_pieces.reshape(tokens, seqs * chans)
    first_adjoint = lax.psum_scatter(left_part, "cols", scatter_dimension=1, tiled=True).reshape(
        tokens, quarter, chans
    )
    moved = lax.all_to_all(
        right_part.reshape(block, seqs * chans), "cols", split_axis=1, concat_axis=0, tiled=True
    )
    right_back = lax.psum_scatter(moved, "rows", scatter_dimension=0, tiled=True).reshape(
        tokens, quarter, chans
    )
    final_projector_slope = lax.psum_scatter(
        out_term, ("rows", "cols"), scatter_dimension=0, tiled=True
    )
    unit_broadcast = unit_alignment.astype(jnp.float32)
    high = lax.Precision.HIGHEST
    left_term = jnp.einsum("tsk,tsc->kc", unit_broadcast, first_adjoint, precision=high)
    right_term = jnp.einsum("tsk,tsc->kc", unit_broadcast, right_back, precision=high)
    first_projector_slope, second_projector_slope = lax.psum(
        (left_term, right_term), ("rows", "cols")
    )
    unit_adjoint = jnp.einsum(
        "tsc,kc->tsk", first_adjoint, first_projector.astype(jnp.float32), precision=high
    )
    unit_adjoint = unit_adjoint + jnp.einsum(
        "tsc,kc->tsk", right_back, second_projector.astype(jnp.float32), precision=high
    )
    scaled_alignment = unit_adjoint * affine_factor
    alignment_slope = reciprocal_spread * (
        scaled_alignment
        - jnp.mean(scaled_alignment, axis=-1, keepdims=True)
        - zscored_alignment * jnp.mean(scaled_alignment * zscored_alignment, axis=-1, keepdims=True)
    )
    return (
        residue_update,
        alignment_slope,
        final_projector_slope,
        first_projector_slope,
        second_projector_slope,
    )


def solution(mesh):
    in_specs = (
        P(("groups", "rows"), "cols", None),
        P(),
        P(),
        P(),
        P(),
        P(),
        P(),
        P(("groups", "rows"), "cols", None),
    )
    out_specs = (
        P(("groups", "rows"), "cols", None),
        P(("groups", "rows"), "cols", None),
        P(("groups", "rows", "cols"), None),
        P("groups", None),
        P("groups", None),
    )
    return jax.shard_map(local, mesh=mesh, in_specs=in_specs, out_specs=out_specs, check_vma=False)
```

profile of v0, /device:TPU:0, one launch (start us, length us, event | category | flops | bytes accessed | tf_op | source)
XLA Modules:
  0.0 162.5 jit_solution(4833273838013963649)
XLA Ops:
  7.3 0.9 reduce_sum.36
  8.5 0.6 copy-done.6
  9.5 6.4 %all_gather.10 = bf16[16,1024]{1,0:T(8,128)(2,1)S(1)} all-gather(bf16[16,256]{1,0:T(8,128)(2,1)S(1)} %reshape.76), channel_id=1, replica_groups=mesh['groups'=2,'rows'=4,'cols'=4] {'cols'}, dimensions={1}, use_global_device_ids=true | all-gather | bytes 40960 | tf_op jit(solution)/shard_map/all_gather | solution.py:44
  16.1 5.4 %all_gather.9 = bf16[16,1024]{1,0:T(8,128)(2,1)S(1)} all-gather(bf16[16,256]{1,0:T(8,128)(2,1)S(1)} %reshape.74), channel_id=1, replica_groups=mesh['groups'=2,'rows'=4,'cols'=4] {'cols'}, dimensions={1}, use_global_device_ids=true | all-gather | bytes 40960 | tf_op jit(solution)/shard_map/all_gather | solution.py:43
  21.7 13.8 %all_gather.11 = bf16[64,1024]{1,0:T(8,128)(2,1)S(1)} all-gather(bf16[16,1024]{1,0:T(8,128)(2,1)S(1)} %all_gather.10), channel_id=1, replica_groups=mesh['groups'=2,'rows'=4,'cols'=4] {'rows'}, dimensions={0}, use_global_device_ids=true | all-gather | bytes 163840 | tf_op jit(solution)/shard_map/all_gather | solution.py:47
  35.7 0.6 copy-done.5
  36.3 16.0 %while.17 = (s32[]{:T(128)}, f32[16,32,32]{2,1,0:T(8,128)S(1)}, f32[1024,128]{1,0:T(8,128)S(1)}, bf16[4,4,16,128]{3,2,1,0:T(8,128)(2,1)}, f32[4,4,32,32]{3,2,1,0...) while((s32[]{:T(128)}, f32[16,32,32]{2,1,0:T(8,128)S(1)}, ...), condition=%wide.region_3.4_spmd.clone, body=%wide.region_2.3_spmd.clone.sunk | while | flops 63442944 | bytes 4129432 | solution.py:94
  36.3 0.3 fusion.68
  36.6 0.5 reshape.96
  37.4 1.3 constant_dynamic-update-slice_fusion.4
  38.7 0.2 convolution_convert_fusion.4
  38.9 0.3 convolution_add_fusion.4
  39.2 0.4 reshape.97
  39.6 0.3 fusion.71
  39.9 0.3 fusion.70
  40.3 0.3 fusion.68
  40.6 0.5 reshape.96
  41.4 1.3 constant_dynamic-update-slice_fusion.4
  42.9 0.3 convolution_add_fusion.4
  43.2 0.4 reshape.97
  43.6 0.3 fusion.71
  43.9 0.3 fusion.70
  44.3 0.3 fusion.68
  44.7 0.5 reshape.96
  45.4 1.3 constant_dynamic-update-slice_fusion.4
  46.9 0.3 convolution_add_fusion.4
  47.2 0.4 reshape.97
  47.6 0.3 fusion.71
  47.9 0.3 fusion.70
  48.3 0.3 fusion.68
  48.7 0.5 reshape.96
  49.4 1.3 constant_dynamic-update-slice_fusion.4
  50.9 0.3 convolution_add_fusion.4
  51.2 0.4 reshape.97
  51.6 0.3 fusion.71
  51.9 0.3 fusion.70
  52.3 0.8 reshape.79
  53.4 7.2 %all_to_all.19 = f32[16,4,256]{2,0,1:T(8,128)} all-to-all(f32[16,4,256]{2,0,1:T(8,128)S(1)} %copy.83), channel_id=1, replica_groups=mesh['groups'=2,'rows'=4,'cols'=4] {'cols'}, dimensions={1} | all-to-all | bytes 131072 | tf_op jit(solution)/shard_map/all_to_all | solution.py:102
  60.6 0.7 reduce-scatter.8.cloned.1.call-update
  61.3 12.6 %reduce-scatter.4.cloned.1.call-done = f32[16,256]{1,0:T(8,128)} async-done(((f32[16,1024]{1,0:T(8,128)}), f32[16,256]{1,0:T(8,128)}) %reduce-scatter.4.cloned.1.call-update) | async-done | bytes 16400 | tf_op jit(solution)/shard_map/reduce_scatter | solution.py:99
  73.9 0.8 reshape.80
  74.7 0.2 convolution_bitcast_fusion.3
  75.1 20.4 %reduce-scatter.6.cloned.1.call-done = f32[16,256]{1,0:T(8,128)} async-done(((f32[64,256]{1,0:T(8,128)}), f32[16,256]{1,0:T(8,128)}) %reduce-scatter.6.cloned.1.call-update) | async-done | bytes 16400 | tf_op jit(solution)/shard_map/reduce_scatter | solution.py:105
  95.5 0.8 reshape.81
  96.3 0.3 fusion.27
  96.7 0.7 copy.87
  97.4 0.2 convolution_bitcast_fusion.2
  97.6 58.4 %all-reduce = (f32[64,32]{0,1:T(8,128)}, f32[64,32]{0,1:T(8,128)}) all-reduce(f32[64,32]{0,1:T(8,128)S(1)} %convolution_bitcast_fusion.3, f32[64,32]{0,1:T(8,128)S(1)} %convolution_bitcast_fusion.2), channel_id=1, replica_groups=mesh['groups'=2,'rows'=4,'cols'=4] {'rows','cols'}, use_global_device_ids=true, to_apply=%region_9.10 | all-reduce | flops 4096 | bytes 32768 | tf_op jit(solution)/shard_map/psum | solution.py:115
  (58 shorter events, 3.5 us)
Async XLA Ops:
  7.2 2.1 %copy-start = (bf16[64,32]{0,1:T(8,128)(2,1)S(1)}, bf16[64,32]{0,1:T(8,128)(2,1)}, u32[]{:S(2)}) copy-start(bf16[64,32]{0,1:T(8,128)(2,1)} %param.14) | copy-start | bytes 12292
  7.2 1.1 copy-start.3
  7.2 66.7 %reduce-scatter.4.cloned.1.call-start = ((), (), s32[]{:S(2)}) async-start(), calls=%async_computation.4 | async-start | bytes 81920 | tf_op jit(solution)/shard_map/reduce_scatter | solution.py:99
  8.5 0.7 copy-start.6
  8.5 0.7 copy-start.7
  9.5 6.4 %copy-start.4 = (bf16[64,32]{0,1:T(8,128)(2,1)S(1)}, bf16[64,32]{0,1:T(8,128)(2,1)}, u32[]{:S(2)}) copy-start(bf16[64,32]{0,1:T(8,128)(2,1)} %param.13) | copy-start | bytes 12292
  21.5 14.2 %copy-start.1 = (bf16[1024,128]{1,0:T(8,128)(2,1)S(1)}, bf16[1024,128]{1,0:T(8,128)(2,1)}, u32[]{:S(2)}) copy-start(bf16[1024,128]{1,0:T(8,128)(2,1)} %param.15) | copy-start | bytes 786436
  35.7 0.7 copy-start.5
  52.3 8.2 %copy-start.2 = (f32[1024,128]{1,0:T(8,128)}, f32[1024,128]{1,0:T(8,128)S(1)}, u32[]{:S(2)}) copy-start(f32[1024,128]{1,0:T(8,128)S(1)} %get-tuple-element.63) | copy-start | bytes 1572868
  53.1 42.4 %reduce-scatter.6.cloned.1.call-start = ((), (), s32[]{:S(2)}) async-start(), calls=%async_computation.5 | async-start | bytes 81920 | tf_op jit(solution)/shard_map/reduce_scatter | solution.py:105
  60.6 95.5 %reduce-scatter.8.cloned.1.call-start = ((), (), s32[]{:S(2)}) async-start(), calls=%async_computation.6 | async-start | bytes 557056 | tf_op jit(solution)/shard_map/reduce_scatter | solution.py:108
Sparse Core Ops, SparseCore 0:
  53.3 20.6 reduce-scatter.3
  76.2 19.3 reduce-scatter.5
  99.6 54.2 reduce-scatter.7
where the time goes:
time: 163 us
  blocking collectives  91.1 us (56%)
  waiting for transfers between devices  33.7 us (21%)
  local copies, waits for them, and re-layouts  14.4 us (9%)
  between operations  14 us (9%)
  matrix products  7.47 us (5%)
    psum x1, blocking collectives, local(): lax.psum((left_term, right_term), ('rows', 'cols'))  58.4 us
    reduce_scatter x1, waiting for transfers between devices, local(): lax.psum_scatter(moved, 'rows', scatter_dimension=0, tiled=True)  20.4 us
    all_gather x1, blocking collectives, local(): right_all = lax.all_gather(right_wide, 'rows', axis=0, tiled=True)  13.8 us
    reduce_scatter x1, waiting for transfers between devices, local(): lax.psum_scatter(left_part, 'cols', scatter_dimension=1, tiled=True)  12.6 us
    all_to_all x1, blocking collectives, local(): lax.all_to_all(right_part.reshape(block, seqs * chans), 'cols', split_axi...  7.16 us
    all_gather x1, blocking collectives, local(): lax.all_gather(right_flat, 'cols', axis=1, tiled=True)  6.37 us
    dynamic_update_slice x12, local copies, waits for them, and re-layouts, local(): lax.scan(advance, beginning_position, (first_tile_list, cot_blocks))  5.69 us
    all_gather x1, blocking collectives, local(): lax.all_gather(left_flat, 'cols', axis=1, tiled=True)  5.39 us
  transfers between devices with their start and end apart: 3, of which 2 were waited for; matrix products, arithmetic and copies ran while one was open for 2% of the time, Pallas kernels for 0%

commit v1 on v0

--- a/solution.py
+++ b/solution.py
@@ -17,7 +17,7 @@
     )
 
 
-def local(
+def local_general(
     alignment_features,
     affine_factor,
     affine_offset,
@@ -136,7 +136,128 @@
     )
 
 
+def local_square(
+    alignment_features,
+    affine_factor,
+    affine_offset,
+    first_projector,
+    second_projector,
+    final_projector,
+    additive_term,
+    adjoint_update,
+):
+    rows, cols = lax.axis_size("rows"), lax.axis_size("cols")
+    zscored_alignment, reciprocal_spread, unit_alignment = layernorm_parts(
+        alignment_features, affine_factor, affine_offset
+    )
+    tokens, quarter, width = unit_alignment.shape
+    chans = first_projector.shape[1]
+    pair_ch = final_projector.shape[1]
+    flip = [(r * cols + q, q * cols + r) for r in range(rows) for q in range(cols)]
+    unit_rows = lax.all_gather(unit_alignment, "cols", axis=1, tiled=True)
+    left_rows = jnp.dot(
+        unit_rows, first_projector, preferred_element_type=jnp.float32
+    ).astype(jnp.bfloat16)
+    right_rows = jnp.dot(
+        unit_rows, second_projector, preferred_element_type=jnp.float32
+    ).astype(jnp.bfloat16)
+    seqs = left_rows.shape[1]
+    multiplier = 1.0 / seqs
+    right_cols = lax.ppermute(
+        right_rows.reshape(tokens, seqs * chans), ("rows", "cols"), flip
+    ).reshape(tokens, seqs, chans)
+    cot_flat = adjoint_update.reshape(tokens * tokens, pair_ch)
+    outer_grad = (
+        jnp.dot(cot_flat, final_projector.T, preferred_element_type=jnp.float32)
+        .astype(jnp.bfloat16)
+        .reshape(tokens, tokens, chans, chans)
+    )
+    right_part = (
+        jnp.einsum("ijcd,isc->jsd", outer_grad, left_rows, preferred_element_type=jnp.float32)
+        * multiplier
+    ).astype(jnp.bfloat16)
+    right_term = lax.ppermute(
+        right_part.reshape(tokens, seqs * chans), ("rows", "cols"), flip
+    ).reshape(tokens, seqs, chans)
+    outer = (
+        jnp.einsum("isc,jsd->ijcd", left_rows, right_cols, preferred_element_type=jnp.float32)
+        * multiplier
+    ).astype(jnp.bfloat16)
+    flat = outer.reshape(tokens * tokens, chans * chans)
+    residue_update = (
+        (jnp.dot(flat, final_projector, preferred_element_type=jnp.float32) + additive_term)
+        .astype(jnp.bfloat16)
+        .reshape(tokens, tokens, pair_ch)
+    )
+    out_term = jnp.einsum("fk,fe->ke", flat, cot_flat, preferred_element_type=jnp.float32)
+    left_term = (
+        jnp.einsum("ijcd,jsd->isc", outer_grad, right_cols, preferred_element_type=jnp.float32)
+        * multiplier
+    ).astype(jnp.bfloat16)
+    both = jnp.concatenate([left_term, right_term], axis=2)
+    slopes = jnp.einsum(
+        "tsk,tsc->kc", unit_rows, both, preferred_element_type=jnp.float32
+    ).astype(jnp.bfloat16)
+    share = out_term.shape[0] // (rows * cols)
+    out_blocks = (
+        out_term.astype(jnp.bfloat16)
+        .reshape(rows, cols, share * pair_ch)
+        .transpose(1, 0, 2)
+        .reshape(cols, rows * share, pair_ch)
+    )
+    both_blocks = (
+        both.reshape(tokens, cols, quarter * 2 * chans)
+        .transpose(1, 0, 2)
+        .reshape(cols, -1, pair_ch)
+    )
+    slope_rows = slopes.reshape(-1, pair_ch)
+    message = jnp.concatenate(
+        [
+            out_blocks,
+            both_blocks,
+            jnp.broadcast_to(slope_rows, (cols,) + slope_rows.shape),
+        ],
+        axis=1,
+    )
+    got = lax.all_to_all(message, "cols", 0, 0, tiled=True)
+    summed = jnp.sum(got.astype(jnp.float32), axis=0)
+    first_cut, second_cut = rows * share, rows * share + both_blocks.shape[1]
+    back = summed[first_cut:second_cut].reshape(tokens, quarter, 2 * chans)
+    message = jnp.concatenate(
+        [
+            summed[:first_cut].reshape(rows, share, pair_ch),
+            jnp.broadcast_to(summed[second_cut:], (rows,) + slope_rows.shape),
+        ],
+        axis=1,
+    ).astype(jnp.bfloat16)
+    got = jnp.sum(
+        lax.all_to_all(message, "rows", 0, 0, tiled=True).astype(jnp.float32), axis=0
+    )
+    final_projector_slope = got[:share]
+    slopes = got[share:].reshape(width, 2 * chans)
+    high = lax.Precision.HIGHEST
+    both_projectors = jnp.concatenate([first_projector, second_projector], axis=1)
+    unit_adjoint = jnp.einsum(
+        "tsc,kc->tsk", back, both_projectors.astype(jnp.float32), precision=high
+    )
+    scaled_alignment = unit_adjoint * affine_factor
+    alignment_slope = reciprocal_spread * (
+        scaled_alignment
+        - jnp.mean(scaled_alignment, axis=-1, keepdims=True)
+        - zscored_alignment * jnp.mean(scaled_alignment * zscored_alignment, axis=-1, keepdims=True)
+    )
+    return (
+        residue_update,
+        alignment_slope,
+        final_projector_slope,
+        slopes[:, :chans],
+        slopes[:, chans:],
+    )
+
+
 def solution(mesh):
+    rows, cols = mesh.shape["rows"], mesh.shape["cols"]
+    local = local_square if rows == cols else local_general
     in_specs = (
         P(("groups", "rows"), "cols", None),
         P(),

time: 163 us -> 61.4 us (0.38)
  blocking collectives: 91.1 us -> 6.55 us
  waiting for transfers between devices: 33.7 us -> 11 us
  starting transfers between devices: 0.12 us -> 18.6 us
  between operations: 14 us -> 1.01 us
  other arithmetic: 1.35 us -> 5.27 us
  local copies, waits for them, and re-layouts: 14.4 us -> 11 us
    psum x1 -> x0, blocking collectives: 58.4 us -> none  [local(): lax.psum((left_term, right_term), ('rows', 'cols'))]
    reduce_scatter x3 -> x0, waiting for transfers between devices: 33 us -> none  [the longest x1 20.4 us: local(): lax.psum_scatter(moved, 'rows', scatter_dimension=0, tiled=True)]
    all_gather x3 -> x1, blocking collectives: 25.6 us -> 6.55 us  [local_square(): unit_rows = lax.all_gather(unit_alignment, 'cols', axis=1, tiled=True)]
    all_to_all x0 -> x2, starting transfers between devices: none -> 17.3 us  [the longest x1 13.9 us: local_square(): got = lax.all_to_all(message, 'cols', 0, 0, tiled=True)]
    all_to_all x0 -> x2, waiting for transfers between devices: none -> 11 us  [the longest x1 6.35 us: local_square(): got = lax.all_to_all(message, 'cols', 0, 0, tiled=True)]
    all_to_all x1 -> x0, blocking collectives: 7.16 us -> none  [local(): lax.all_to_all(right_part.reshape(block, seqs * chans), 'cols', split_axi...]
    dynamic_update_slice x12 -> x0, local copies, waits for them, and re-layouts: 5.69 us -> none  [local(): lax.scan(advance, beginning_position, (first_tile_list, cot_blocks))]
    convert_element_type x2 -> x1, local copies, waits for them, and re-layouts: 0.03 us -> 3.04 us  [local_square(): outer = (jnp.einsum('isc,jsd->ijcd', left_rows, right_cols, preferred_ele...]
  transfers between devices with their start and end apart: 3 -> 4, of which waited for: 2 -> 2; matrix products, arithmetic and copies ran while one was open for 2% -> 11% of each run, Pallas kernels for 0% -> 0%
where the time goes in v1:
time: 61.4 us; the launch traced here: 60.8 us
  starting transfers between devices  18.6 us (30%)
  local copies, waits for them, and re-layouts  11 us (18%)
  waiting for transfers between devices  11 us (18%)
  matrix products  7.47 us (12%)
  blocking collectives  6.55 us (11%)
  other arithmetic  5.27 us (9%)
  between operations  1.01 us (2%)
    all_to_all x1, starting transfers between devices, local_square(): got = lax.all_to_all(message, 'cols', 0, 0, tiled=True)  13.9 us
    all_gather x1, blocking collectives, local_square(): unit_rows = lax.all_gather(unit_alignment, 'cols', axis=1, tiled=True)  6.55 us
    all_to_all x1, waiting for transfers between devices, local_square(): got = lax.all_to_all(message, 'cols', 0, 0, tiled=True)  6.35 us
    all_to_all x1, waiting for transfers between devices, local_square(): lax.all_to_all(message, 'rows', 0, 0, tiled=True).astype(jnp.float32)  4.62 us
    all_to_all x1, starting transfers between devices, local_square(): lax.all_to_all(message, 'rows', 0, 0, tiled=True).astype(jnp.float32)  3.3 us
    convert_element_type x1, local copies, waits for them, and re-layouts, local_square(): outer = (jnp.einsum('isc,jsd->ijcd', left_rows, right_cols, preferred_ele...  3.04 us
    reshape x1, local copies, waits for them, and re-layouts, local_square(): flat = outer.reshape(tokens * tokens, chans * chans)  2.23 us
    dot_general x1, matrix products, local_square(): jnp.einsum('isc,jsd->ijcd', left_rows, right_cols, preferred_element_type...  2.08 us
  transfers between devices with their start and end apart: 4, of which 2 were waited for; matrix products, arithmetic and copies ran while one was open for 11% of the time, Pallas kernels for 0%

profile of v1, /device:TPU:0, one launch (start us, length us, event | category | flops | bytes accessed | tf_op | source)
XLA Modules:
  0.0 60.8 jit_solution(8519164496767124898)
XLA Ops:
  0.6 0.0 copy-start
  0.6 1.0 %reduce_sum.54 = f32[16,8]{1,0:T(8,128)S(1)} reduce(f32[16,8,64]{2,1,0:T(8,128)} %param.8, f32[]{:T(128)} %constant.4.clone.1), dimensions={2}, to_apply=%region_0.0 | reduce | flops 8064 | bytes 33284 | tf_op jit(solution)/shard_map/reduce_sum | solution.py:8
  1.6 1.0 %multiply_reduce_fusion.1 = f32[16,8]{1,0:T(8,128)S(1)} fusion(f32[16,8,64]{2,1,0:T(8,128)} %param.8, f32[16,8]{1,0:T(8,128)S(1)} %broadcast_multiply_fusion.2), kind=kLoop, calls=%fused_computation.33 | loop fusion | flops 24448 | bytes 33792 | tf_op jit(solution)/shard_map/reduce_sum | solution.py:10
  2.7 0.0 copy-start.3
  2.7 1.0 %add_convert_fusion = bf16[16,8,64]{2,1,0:T(8,128)(2,1)S(1)} fusion(f32[16,8,64]{2,1,0:T(8,128)} %param.8, f32[64]{0:T(128)} %param.10, f32[64]{0:T(128)} %param.9, f32[16,8]{1,0:T(8,128)S(1)} %add_rsqrt_fusion, f32[16,8]{1,0:T(8,128)S(1)} %broadcast_multiply_fusion.2), kind=kLoop, calls=%fused_computation.32 | loop fusion | flops 40960 | bytes 50688 | tf_op jit(solution)/shard_map/convert_element_type | solution.py:16
  3.6 6.5 %all_gather.3 = bf16[16,32,64]{2,1,0:T(8,128)(2,1)S(1)} all-gather(bf16[16,8,64]{2,1,0:T(8,128)(2,1)S(1)} %add_convert_fusion), channel_id=1, replica_groups=mesh['groups'=2,'rows'=4,'cols'=4] {'cols'}, dimensions={1}, use_global_device_ids=true | all-gather | bytes 81920 | tf_op jit(solution)/shard_map/all_gather | solution.py:157
  10.2 0.9 %convolution_convert_fusion.3 = bf16[16,32,32]{2,1,0:T(8,128)(2,1)S(1)} fusion(bf16[16,32,64]{2,1,0:T(8,128)(2,1)S(1)} %all_gather.3, bf16[64,32]{0,1:T(8,128)(2,1)} %param.12), kind=kOutput, calls=%fused_computation.11 | convolution fusion | flops 2113536 | bytes 102400 | tf_op jit(solution)/shard_map/dot_general | solution.py:161
  11.1 0.2 reshape.82
  11.2 0.7 %collective-permute-start = (bf16[16,1024]{1,0:T(8,128)(2,1)S(1)}, bf16[16,1024]{1,0:T(8,128)(2,1)S(1)}, u32[]{:S(2)}, u32[]{:S(2)}) collective-permute-start(bf16[16,1024]{1,0:T(8,128)(2,1)S(1)} %reshape.82), channel_id=1, source_target_pairs={{0,0},{1,4},{2,8},{3,12},{4,1},{5,5},{6,9},{7,13},{8,2},{9,6},{10,... | collective-permute-start | bytes 98312 | tf_op jit(solution)/shard_map/ppermute | solution.py:166
  11.9 1.1 %convolution_convert_fusion = bf16[256,1024]{1,0:T(8,128)(2,1)S(1)} fusion(bf16[256,128]{1,0:T(8,128)(2,1)} %bitcast.81, bf16[1024,128]{1,0:T(8,128)(2,1)S(1)} %copy-done), kind=kOutput, calls=%fused_computation.2 | convolution fusion | flops 67371008 | bytes 851968 | tf_op jit(solution)/shard_map/dot_general | solution.py:171
  13.1 1.6 %reshape.89 = bf16[16,16,32,32]{3,2,1,0:T(8,128)(2,1)S(1)} reshape(bf16[256,1024]{1,0:T(8,128)(2,1)S(1)} %convolution_convert_fusion) | data formatting | bytes 1048576 | tf_op jit(solution)/shard_map/reshape | solution.py:173
  14.7 0.2 convolution_convert_fusion.2
  14.8 0.6 fusion.5
  15.4 0.2 reshape.90
  15.6 0.7 %collective-permute-start.1 = (bf16[16,1024]{1,0:T(8,128)(2,1)S(1)}, bf16[16,1024]{1,0:T(8,128)(2,1)S(1)}, u32[]{:S(2)}, u32[]{:S(2)}) collective-permute-start(bf16[16,1024]{1,0:T(8,128)(2,1)S(1)} %reshape.90), channel_id=1, source_target_pairs={{0,0},{1,4},{2,8},{3,12},{4,1},{5,5},{6,9},{7,13},{8,2},{9,6},{10,... | collective-permute-start | bytes 98312 | tf_op jit(solution)/shard_map/ppermute | solution.py:179
  16.3 0.1 reshape.102
  16.4 0.8 %fusion.6 = bf16[16,32,32]{2,1,0:T(8,128)(2,1)S(1)} fusion(bf16[16,32,32,1]{2,1,0,3:T(8,128)(2,1)S(1)} %reshape.102, bf16[16,16,32,32]{3,2,1,0:T(8,128)(2,1)S(1)} %reshape.89), kind=kOutput, calls=%fused_computation.13 | convolution fusion | flops 16809984 | bytes 589824 | tf_op jit(solution)/shard_map/ijcd,jsd->isc/dot_general | solution.py:194
  17.3 0.1 reshape.91
  17.4 0.1 pad_maximum_fusion.1
  17.5 0.2 fusion.8
  17.7 0.1 reshape.92
  17.9 0.1 reshape.94
  18.0 0.1 reshape.93
  18.0 0.1 reshape.83
  18.2 2.1 %fusion = bf16[16,16,32,32]{2,3,0,1:T(8,128)(2,1)} fusion(bf16[16,32,32]{2,1,0:T(8,128)(2,1)S(1)} %reshape.83, bf16[16,32,32]{2,1,0:T(8,128)(2,1)S(1)} %convolution_convert_fusion.2), kind=kOutput, calls=%fused_computation.1 | convolution fusion | flops 17301504 | bytes 589824 | tf_op jit(solution)/shard_map/isc,jsd->ijcd/dot_general | solution.py:183
  20.3 3.0 %copy.19 = bf16[16,16,32,32]{3,2,1,0:T(8,128)(2,1)S(1)} copy(bf16[16,16,32,32]{2,3,0,1:T(8,128)(2,1)} %fusion) | data formatting | bytes 1048576 | tf_op jit(solution)/shard_map/convert_element_type | solution.py:185
  23.3 2.2 %reshape.84 = bf16[256,1024]{1,0:T(8,128)(2,1)S(1)} reshape(bf16[16,16,32,32]{3,2,1,0:T(8,128)(2,1)S(1)} %copy.19) | data formatting | bytes 1048576 | tf_op jit(solution)/shard_map/reshape | solution.py:186
  25.6 0.3 convolution_convert_fusion.1
  26.0 0.1 reshape.87
  26.1 0.2 copy.38
  26.3 0.3 reshape.88
  26.6 0.8 %pad_maximum_fusion = bf16[4,352,128]{2,1,0:T(8,128)(2,1)} fusion(bf16[4,32,128]{2,1,0:T(8,128)(2,1)S(1)} %broadcast_in_dim.4, bf16[4,64,128]{2,1,0:T(8,128)(2,1)S(1)} %reshape.93, bf16[4,256,128]{2,1,0:T(8,128)(2,1)S(1)} %reshape.88), kind=kLoop, calls=%fused_computation.20 | loop fusion | flops 1081344 | bytes 720896 | tf_op jit(solution)/shard_map/concatenate | solution.py:214
  27.3 13.9 %all-to-all-start = ((bf16[4,352,128]{2,1,0:T(8,128)(2,1)}), bf16[4,352,128]{2,1,0:T(8,128)(2,1)S(1)}, u32[]{:S(2)}, u32[]{:S(2)}) async-start(bf16[4,352,128]{2,1,0:T(8,128)(2,1)} %pad_maximum_fusion), calls=%async_computation | async-start | bytes 720896 | tf_op jit(solution)/shard_map/all_to_all | solution.py:222
  41.3 0.1 copy.23
  41.4 0.1 copy.24
  41.5 0.9 %fusion.7 = bf16[256,128]{1,0:T(8,128)(2,1)} fusion(bf16[256,1024]{1,0:T(8,128)(2,1)S(1)} %reshape.84, bf16[1024,128]{1,0:T(8,128)(2,1)S(1)} %copy-done, f32[128]{0:T(128)S(1)} %copy-done.6), kind=kOutput, calls=%fused_computation.15 | convolution fusion | flops 67174400 | bytes 852480 | tf_op jit(solution)/shard_map/dot_general | solution.py:188
  42.4 6.3 %all-to-all-done = bf16[4,352,128]{2,1,0:T(8,128)(2,1)S(1)} async-done(((bf16[4,352,128]{2,1,0:T(8,128)(2,1)}), bf16[4,352,128]{2,1,0:T(8,128)(2,1)S(1)}, u32[]{:S(2)}, u32[]{:S(2)}) %all-to-all-start) | async-done | bytes 360480 | tf_op jit(solution)/shard_map/all_to_all | solution.py:222
  48.9 0.6 %pad_maximum_fusion.2 = bf16[4,96,128]{2,1,0:T(8,128)(2,1)} fusion(bf16[4,32,128]{2,1,0:T(8,128)(2,1)S(1)} %broadcast_in_dim.5, bf16[4,64,128]{2,1,0:T(8,128)(2,1)S(1)} %bitcast.79), kind=kLoop, calls=%fused_computation.28 | loop fusion | flops 196608 | bytes 196608 | tf_op jit(solution)/shard_map/concatenate | solution.py:226
  49.5 3.3 %all-to-all-start.1 = ((bf16[4,96,128]{2,1,0:T(8,128)(2,1)}), bf16[4,96,128]{2,1,0:T(8,128)(2,1)S(1)}, u32[]{:S(2)}, u32[]{:S(2)}) async-start(bf16[4,96,128]{2,1,0:T(8,128)(2,1)} %pad_maximum_fusion.2), calls=%async_computation.1 | async-start | bytes 196608 | tf_op jit(solution)/shard_map/all_to_all | solution.py:234
  52.8 0.1 reshape.95
  52.9 0.3 fusion.17
  53.3 0.8 %subtract_multiply_fusion = f32[16,8,64]{2,1,0:T(8,128)} fusion(f32[16,8,64]{2,1,0:T(8,128)S(1)} %get-tuple-element.14, f32[16,8,64]{2,1,0:T(8,128)S(1)} %copy-done.1, f32[16,8]{1,0:T(8,128)S(1)} %get-tuple-element.15, f32[16,8]{1,0:T(8,128)S(1)} %get-tuple-element.16, f32[16,8]{1,0:T(8,128)S(1)} %add_rsqrt_fusion, f32[16,8]{1,0:T(8,128)S(1)} %broadcast_multiply_fusion.2), kind=kLoop, calls=%fused_computation.30 | loop fusion | flops 49152 | bytes 100352 | tf_op jit(solution)/shard_map/mul | solution.py:244
  54.0 4.6 %all-to-all-done.1 = bf16[4,96,128]{2,1,0:T(8,128)(2,1)S(1)} async-done(((bf16[4,96,128]{2,1,0:T(8,128)(2,1)}), bf16[4,96,128]{2,1,0:T(8,128)(2,1)S(1)}, u32[]{:S(2)}, u32[]{:S(2)}) %all-to-all-start.1) | async-done | bytes 98336 | tf_op jit(solution)/shard_map/all_to_all | solution.py:234
  58.7 0.6 %slice.32 = f32[64,128]{1,0:T(8,128)} slice(f32[96,128]{1,0:T(8,128)S(1)} %convert_reduce_fusion.1), slice={[0:64], [0:128]} | slice | bytes 65536 | tf_op jit(solution)/shard_map/slice | solution.py:236
  59.3 0.1 reshape.97
  59.4 0.1 fusion.18
  59.4 0.7 %copy.27 = f32[64,32]{0,1:T(8,128)} copy(f32[64,32]{1,0:T(8,128)S(1)} %get-tuple-element.13) | data formatting | bytes 16384
  60.1 0.7 %copy.28 = f32[64,32]{0,1:T(8,128)} copy(f32[64,32]{1,0:T(8,128)S(1)} %get-tuple-element.12) | data formatting | bytes 16384
  (26 shorter events, 0.2 us)
Async XLA Ops:
  0.6 11.3 %copy-start = (bf16[1024,128]{1,0:T(8,128)(2,1)S(1)}, bf16[1024,128]{1,0:T(8,128)(2,1)}, u32[]{:S(2)}) copy-start(bf16[1024,128]{1,0:T(8,128)(2,1)} %param.13) | copy-start | bytes 786436
  2.7 12.0 %copy-start.3 = (bf16[64,32]{0,1:T(8,128)(2,1)S(1)}, bf16[64,32]{0,1:T(8,128)(2,1)}, u32[]{:S(2)}) copy-start(bf16[64,32]{0,1:T(8,128)(2,1)} %param.11) | copy-start | bytes 12292
  11.2 5.0 %collective-permute-start = (bf16[16,1024]{1,0:T(8,128)(2,1)S(1)}, bf16[16,1024]{1,0:T(8,128)(2,1)S(1)}, u32[]{:S(2)}, u32[]{:S(2)}) collective-permute-start(bf16[16,1024]{1,0:T(8,128)(2,1)S(1)} %reshape.82), channel_id=1, source_target_pairs={{0,0},{1,4},{2,8},{3,12},{4,1},{5,5},{6,9},{7,13},{8,2},{9,6},{10,... | collective-permute-start | bytes 98312 | tf_op jit(solution)/shard_map/ppermute | solution.py:166
  15.6 1.7 %collective-permute-start.1 = (bf16[16,1024]{1,0:T(8,128)(2,1)S(1)}, bf16[16,1024]{1,0:T(8,128)(2,1)S(1)}, u32[]{:S(2)}, u32[]{:S(2)}) collective-permute-start(bf16[16,1024]{1,0:T(8,128)(2,1)S(1)} %reshape.90), channel_id=1, source_target_pairs={{0,0},{1,4},{2,8},{3,12},{4,1},{5,5},{6,9},{7,13},{8,2},{9,6},{10,... | collective-permute-start | bytes 98312 | tf_op jit(solution)/shard_map/ppermute | solution.py:179
  23.3 2.3 %copy-start.2 = (bf16[16,16,128]{2,1,0:T(8,128)(2,1)S(1)}, bf16[16,16,128]{2,1,0:T(8,128)(2,1)}, u32[]{:S(2)}) copy-start(bf16[16,16,128]{2,1,0:T(8,128)(2,1)} %param.15) | copy-start | bytes 196612
  25.6 15.8 %copy-start.4 = (bf16[64,32]{0,1:T(8,128)(2,1)S(1)}, bf16[64,32]{0,1:T(8,128)(2,1)}, u32[]{:S(2)}) copy-start(bf16[64,32]{0,1:T(8,128)(2,1)} %param.12) | copy-start | bytes 12292
  25.6 15.9 %copy-start.6 = (f32[128]{0:T(128)S(1)}, f32[128]{0:T(128)}, u32[]{:S(2)}) copy-start(f32[128]{0:T(128)} %param.14) | copy-start | bytes 1540
  26.3 26.6 %copy-start.1 = (f32[16,8,64]{2,1,0:T(8,128)S(1)}, f32[16,8,64]{2,1,0:T(8,128)}, u32[]{:S(2)}) copy-start(f32[16,8,64]{2,1,0:T(8,128)} %param.8) | copy-start | bytes 98308
  26.3 26.6 %copy-start.5 = (f32[64]{0:T(128)S(1)}, f32[64]{0:T(128)}, u32[]{:S(2)}) copy-start(f32[64]{0:T(128)} %param.9) | copy-start | bytes 772
  27.3 21.4 %all-to-all-start = ((bf16[4,352,128]{2,1,0:T(8,128)(2,1)}), bf16[4,352,128]{2,1,0:T(8,128)(2,1)S(1)}, u32[]{:S(2)}, u32[]{:S(2)}) async-start(bf16[4,352,128]{2,1,0:T(8,128)(2,1)} %pad_maximum_fusion), calls=%async_computation | async-start | bytes 720896 | tf_op jit(solution)/shard_map/all_to_all | solution.py:222
  49.5 9.1 %all-to-all-start.1 = ((bf16[4,96,128]{2,1,0:T(8,128)(2,1)}), bf16[4,96,128]{2,1,0:T(8,128)(2,1)S(1)}, u32[]{:S(2)}, u32[]{:S(2)}) async-start(bf16[4,96,128]{2,1,0:T(8,128)(2,1)} %pad_maximum_fusion.2), calls=%async_computation.1 | async-start | bytes 196608 | tf_op jit(solution)/shard_map/all_to_all | solution.py:234

commit v2 on v0

--- a/solution.py
+++ b/solution.py
@@ -1,6 +1,10 @@
+import functools
+
 import jax
 import jax.numpy as jnp
 from jax import lax
+from jax.experimental import pallas as pl
+from jax.experimental.pallas import tpu as pltpu
 from jax.sharding import PartitionSpec as P
 
 
@@ -17,7 +21,7 @@
     )
 
 
-def local(
+def local_general(
     alignment_features,
     affine_factor,
     affine_offset,
@@ -136,6 +140,410 @@
     )
 
 
+F32, BF16 = jnp.float32, jnp.bfloat16
+LANES, SUBLANES = 128, 8
+
+
+def dot(a, b, at=1, bt=0):
+    return lax.dot_general(a, b, (((at,), (bt,)), ((), ())), preferred_element_type=F32)
+
+
+def lane_group(shape, chans):
+    return lax.broadcasted_iota(jnp.int32, shape, len(shape) - 1) // chans
+
+
+def pick(parts, group):
+    out = parts[-1]
+    for b in range(len(parts) - 2, -1, -1):
+        out = jnp.where(group == b, parts[b], out)
+    return out
+
+
+def normalise(x):
+    centered = x - jnp.mean(x, axis=-1, keepdims=True)
+    spread = lax.rsqrt(jnp.mean(centered * centered, axis=-1, keepdims=True) + 1e-05)
+    return centered * spread, spread
+
+
+def call(kernel, out_shape, scratch=(), flops=0, **kw):
+    return pl.pallas_call(
+        kernel,
+        out_shape=out_shape,
+        scratch_shapes=list(scratch),
+        cost_estimate=pl.CostEstimate(flops=flops, bytes_accessed=0, transcendentals=0),
+        **kw,
+    )
+
+
+def norm_kernel(x_ref, gain_ref, offset_ref, out_ref):
+    tokens, quarter, width = x_ref.shape
+    xhat, _ = normalise(x_ref[...].reshape(tokens * quarter, width))
+    unit = xhat * gain_ref[...] + offset_ref[...]
+    half = tokens * quarter // 2
+    out_ref[...] = jnp.concatenate([unit[:half], unit[half:]], axis=1).astype(BF16)
+
+
+def grad_kernel(
+    cot_ref, final_ref, by_col_ref, by_row_ref, cot_cols_ref, cot_f, final_f, *, chans
+):
+    tokens, block, _ = cot_ref.shape
+    steps = by_col_ref.shape[0] // tokens
+    cot = cot_ref[...]
+    final = final_ref[...]
+    cot_f[...] = cot.astype(F32)
+    final_f[...] = final.astype(F32)
+    for j in range(block):
+        cot_cols_ref[j * tokens : (j + 1) * tokens, :] = cot_f[:, j, :].astype(BF16)
+    cot_cols = cot_cols_ref[...]
+    cot_rows = cot.reshape(tokens * block, cot.shape[2])
+    per = LANES // chans
+    for a in range(steps):
+        lanes_cd = final[a * LANES : (a + 1) * LANES]
+        got = dot(cot_cols, lanes_cd, 1, 1).astype(BF16)
+        for j in range(block):
+            by_col_ref[a * tokens : (a + 1) * tokens, j * LANES : (j + 1) * LANES] = got[
+                j * tokens : (j + 1) * tokens
+            ]
+        lanes_dc = jnp.concatenate(
+            [final_f[pl.ds(a * per + b, chans, stride=chans), :] for b in range(per)], axis=0
+        ).astype(BF16)
+        got = dot(cot_rows, lanes_dc, 1, 1).astype(BF16)
+        for i in range(tokens):
+            by_row_ref[a * block : (a + 1) * block, i * LANES : (i + 1) * LANES] = got[
+                i * block : (i + 1) * block
+            ]
+
+
+def fold(spread_ref, seqs, chans, tokens):
+    per = LANES // chans
+    group = lane_group((seqs, LANES), chans)
+    out = []
+    for p in range(tokens // per):
+        total = None
+        for shift in range(per):
+            parts = []
+            for b in range(per):
+                t = p * per + (b + shift) % per
+                parts.append(spread_ref[b * seqs : (b + 1) * seqs, t * LANES : (t + 1) * LANES])
+            part = pick(parts, group)
+            if shift:
+                part = pltpu.roll(part, shift * chans, 1)
+            total = part if total is None else total + part
+        out.append(total)
+    return out
+
+
+def padded_projectors(first, second, b, per):
+    zero = jnp.zeros_like(first)
+    return jnp.concatenate(
+        [x if i == b else zero for x in (first, second) for i in range(per)], axis=0
+    )
+
+
+def project_kernel(
+    n0, n1, n2, n3, first_ref, second_ref, by_col_ref, send_ref, left_ref, unit_ref, unit_f, proj_f, wide_f, spread_f,
+):
+    blocks = (n0, n1, n2, n3)
+    seqs, width = unit_f.shape[1], unit_f.shape[2]
+    tokens = unit_f.shape[0]
+    quarter = seqs // len(blocks)
+    chans = first_ref.shape[0]
+    per, steps = LANES // chans, chans // (LANES // chans)
+    mine = lax.axis_index("cols")
+    half = tokens // 2
+    for k, ref in enumerate(blocks):
+        at = pl.multiple_of((mine ^ k) * quarter, quarter)
+        got = ref[...].astype(F32)
+        for h in range(2):
+            unit_f[h * half : (h + 1) * half, pl.ds(at, quarter), :] = got[
+                :, h * width : (h + 1) * width
+            ].reshape(half, quarter, width)
+    unit = unit_f[...].astype(BF16)
+    first, second = first_ref[...], second_ref[...]
+    total = None
+    by_group = unit.reshape(tokens // per, per, seqs, width)
+    for b in range(per):
+        part = by_group[:, b].reshape(tokens // per * seqs, width)
+        unit_ref[b] = part
+        got = dot(part, padded_projectors(first, second, b, per), 1, 1)
+        total = got if total is None else total + got
+    rows = tokens // per * seqs
+    send_ref[0:rows, :] = total[:, LANES:].astype(BF16)
+    proj_f[0] = first.astype(F32)
+    proj_f[1] = second.astype(F32)
+    permuted = jnp.concatenate(
+        [proj_f[x, pl.ds(b, steps, stride=per), :] for x in range(2) for b in range(per)], axis=0
+    ).astype(BF16)
+    tall = dot(permuted, unit.reshape(tokens * seqs, width), 1, 1).astype(BF16).astype(F32)
+    group = lane_group((steps, LANES), chans)
+    for x in range(2):
+        for p in range(tokens // per):
+            tiles = [
+                tall[
+                    (x * per + b) * steps : (x * per + b + 1) * steps, p * LANES : (p + 1) * LANES
+                ]
+                for b in range(per)
+            ]
+            for own in range(per):
+                parts = [
+                    pltpu.roll(tile, (b - own) % per * chans, 1) if b != own else tile
+                    for b, tile in enumerate(tiles)
+                ]
+                wide_f[x, :, p * per + own, :] = pick(parts, group)
+    left = wide_f[0].reshape(steps * tokens, LANES)
+    left_ref[...] = left.astype(BF16)
+    send_ref[2 * rows : 2 * rows + steps * tokens, :] = (
+        wide_f[1].reshape(steps * tokens, LANES).astype(BF16)
+    )
+    spread_f[...] = dot(left.T.astype(BF16), by_col_ref[...])
+    for p, tile in enumerate(fold(spread_f, seqs, chans, tokens)):
+        send_ref[rows + p * seqs : rows + (p + 1) * seqs, :] = (tile * (1.0 / seqs)).astype(BF16)
+
+
+def pair_kernel(
+    right_ref, left_ref, unit_ref, by_row_ref, final_ref, cot_cols_ref, bias_ref,
+    update_ref, own_ref, m1, m2, m3,
+    outer_ref, update_f, slope_f, spread_f, both_f,
+    *, chans, rows_axis, cols_axis,
+):
+    per, steps = LANES // chans, chans // (LANES // chans)
+    tokens = update_ref.shape[0]
+    groups = tokens // per
+    seqs = both_f.shape[2]
+    rows = groups * seqs
+    quarter = seqs // cols_axis
+    share = slope_f.shape[0] // (rows_axis * cols_axis)
+    mine = lax.axis_index("cols")
+    group = lane_group((seqs, LANES), chans)
+    left = left_ref[...]
+    for p in range(groups):
+        tile = right_ref[p * seqs : (p + 1) * seqs, :].astype(F32)
+        rolled = [pltpu.roll(tile, s * chans, 1) if s else tile for s in range(per)]
+        for own in range(per):
+            j = p * per + own
+            blocks = jnp.concatenate(
+                [jnp.where(group == b, rolled[(b - own) % per], 0.0) for b in range(per)], axis=0
+            ).astype(BF16)
+            got = (dot(left, blocks) * (1.0 / seqs)).astype(BF16)
+            for a in range(steps):
+                outer_ref[j * tokens : (j + 1) * tokens, a * LANES : (a + 1) * LANES] = got[
+                    a * tokens : (a + 1) * tokens
+                ]
+    outer = outer_ref[...]
+    slope_f[...] = dot(outer, cot_cols_ref[...], 0, 0)
+    update = dot(outer, final_ref[...]) + bias_ref[...]
+    for j in range(tokens):
+        update_f[:, j, :] = update[j * tokens : (j + 1) * tokens]
+    update_ref[...] = update_f[...].astype(BF16)
+    wide = right_ref[2 * rows : 2 * rows + steps * tokens, :].astype(F32)
+    spread_f[...] = dot(wide.T.astype(BF16), by_row_ref[...])
+    for p, tile in enumerate(fold(spread_f, seqs, chans, tokens)):
+        both_f[p, 0] = tile * (1.0 / seqs)
+        both_f[p, 1] = right_ref[rows + p * seqs : rows + (p + 1) * seqs, :].astype(F32)
+    both = jnp.concatenate(
+        [both_f[:, x].reshape(rows, LANES).astype(BF16) for x in range(2)], axis=1
+    )
+    width = unit_ref.shape[2]
+    slopes = pick(
+        [dot(unit_ref[b], both, 0, 0) for b in range(per)],
+        lane_group((width, 2 * LANES), chans) % per,
+    )
+    sides = [slopes[:, x * LANES : (x + 1) * LANES] for x in range(2)]
+    sides = [s + pltpu.roll(s, LANES // 2, 1) for s in sides]
+    slopes = jnp.where(lane_group((width, LANES), LANES // 2) == 0, sides[0], sides[1])
+    for k, ref in enumerate((own_ref, m1, m2, m3)):
+        peer = mine ^ k
+        kind = ref.dtype
+        for r in range(rows_axis):
+            at = pl.multiple_of((r * cols_axis + peer) * share, share)
+            ref[r * share : (r + 1) * share, :] = slope_f[pl.ds(at, share), :].astype(kind)
+        base = rows_axis * share
+        at = pl.multiple_of(peer * quarter, quarter)
+        span = 2 * quarter
+        for p in range(groups):
+            ref[base + p * span : base + (p + 1) * span, :] = (
+                both_f[p, :, pl.ds(at, quarter), :].reshape(span, LANES).astype(kind)
+            )
+        base += groups * span
+        ref[base : base + width, :] = slopes.astype(kind)
+
+
+def between_kernel(own_ref, r1, r2, r3, back_ref, next_ref, m1, m2, m3, total_f, *, rows_axis, share):
+    total_f[...] = (
+        own_ref[...] + r1[...].astype(F32) + r2[...].astype(F32) + r3[...].astype(F32)
+    )
+    mine = lax.axis_index("rows")
+    first = rows_axis * share
+    last = first + back_ref.shape[0]
+    back_ref[...] = total_f[first:last, :]
+    slopes = total_f[last:, :]
+    for k, ref in enumerate((next_ref, m1, m2, m3)):
+        at = pl.multiple_of((mine ^ k) * share, share)
+        ref[0:share, :] = total_f[pl.ds(at, share), :].astype(ref.dtype)
+        ref[share:, :] = slopes.astype(ref.dtype)
+
+
+def back_kernel(back_ref, x_ref, gain_ref, first_ref, second_ref, out_ref, unit_f):
+    tokens, quarter, width = x_ref.shape
+    chans = first_ref.shape[0]
+    per = LANES // chans
+    groups = tokens // per
+    back = back_ref[...].reshape(groups, 2, quarter, LANES)
+    wide = jnp.concatenate([back[:, x].reshape(groups * quarter, LANES) for x in range(2)], axis=1)
+    high = wide.astype(BF16)
+    low = (wide - high.astype(F32)).astype(BF16)
+    first, second = first_ref[...], second_ref[...]
+    for b in range(per):
+        weights = padded_projectors(first, second, b, per)
+        got = dot(high, weights) + dot(low, weights)
+        for p in range(groups):
+            unit_f[p * per + b] = got[p * quarter : (p + 1) * quarter]
+    xhat, spread = normalise(x_ref[...].reshape(tokens * quarter, width))
+    g = unit_f[...].reshape(tokens * quarter, width) * gain_ref[...]
+    out = spread * (
+        g
+        - jnp.mean(g, axis=-1, keepdims=True)
+        - xhat * jnp.mean(g * xhat, axis=-1, keepdims=True)
+    )
+    out_ref[...] = out.reshape(tokens, quarter, width)
+
+
+def last_kernel(own_ref, r1, r2, r3, final_ref, first_ref, second_ref):
+    total = own_ref[...] + r1[...].astype(F32) + r2[...].astype(F32) + r3[...].astype(F32)
+    share = final_ref.shape[0]
+    final_ref[...] = total[:share]
+    slopes = total[share:].T
+    chans = first_ref.shape[0]
+    for x, ref in enumerate((first_ref, second_ref)):
+        side = slopes[x * LANES // 2 : (x + 1) * LANES // 2]
+        out = side[:chans]
+        for b in range(1, LANES // 2 // chans):
+            out = out + side[b * chans : (b + 1) * chans]
+        ref[...] = out
+
+
+def exchange(messages, axis):
+    size = lax.axis_size(axis)
+    return [
+        lax.ppermute(m, axis, [(p, p ^ k) for p in range(size)])
+        for k, m in enumerate(messages, 1)
+    ]
+
+
+def local_square(
+    alignment_features,
+    affine_factor,
+    affine_offset,
+    first_projector,
+    second_projector,
+    final_projector,
+    additive_term,
+    adjoint_update,
+):
+    rows, cols = lax.axis_size("rows"), lax.axis_size("cols")
+    tokens, quarter, width = alignment_features.shape
+    chans = first_projector.shape[1]
+    total, pair_ch = final_projector.shape
+    seqs = quarter * cols
+    per, steps = LANES // chans, chans // (LANES // chans)
+    share = total // (rows * cols)
+    flip = [(r * cols + q, q * cols + r) for r in range(rows) for q in range(cols)]
+    shape = jax.ShapeDtypeStruct
+    gain = affine_factor.reshape(1, width)
+    offset = affine_offset.reshape(1, width)
+    first, second = first_projector.T, second_projector.T
+    wide = tokens * LANES
+    tall = steps * tokens
+    packed = tokens // per * seqs
+    unit = call(norm_kernel, shape((tokens * quarter // 2, 2 * width), BF16))(
+        alignment_features, gain, offset
+    )
+    units = [unit] + exchange([unit] * (cols - 1), "cols")
+    by_col, by_row, cot_cols = call(
+        functools.partial(grad_kernel, chans=chans),
+        (
+            shape((tall, wide), BF16),
+            shape((tall, wide), BF16),
+            shape((tokens * tokens, pair_ch), BF16),
+        ),
+        [pltpu.VMEM(adjoint_update.shape, F32), pltpu.VMEM((total, pair_ch), F32)],
+        flops=8 * tokens * tokens * total * pair_ch,
+    )(adjoint_update, final_projector)
+    send, left, unit_rows = call(
+        project_kernel,
+        (
+            shape((2 * packed + tall, LANES), BF16),
+            shape((tall, LANES), BF16),
+            shape((per, packed, width), BF16),
+        ),
+        [
+            pltpu.VMEM((tokens, seqs, width), F32),
+            pltpu.VMEM((2, chans, width), F32),
+            pltpu.VMEM((2, steps, tokens, LANES), F32),
+            pltpu.VMEM((LANES, wide), F32),
+        ],
+    )(*units, first, second, by_col)
+    right = lax.ppermute(send, ("rows", "cols"), flip)
+    message = rows * share + 2 * quarter * tokens // per + width
+    update, own, *messages = call(
+        functools.partial(pair_kernel, chans=chans, rows_axis=rows, cols_axis=cols),
+        (
+            shape((tokens, tokens, pair_ch), BF16),
+            shape((message, LANES), F32),
+            *[shape((message, LANES), BF16)] * (cols - 1),
+        ),
+        [
+            pltpu.VMEM((tokens * tokens, total), BF16),
+            pltpu.VMEM((tokens, tokens, pair_ch), F32),
+            pltpu.VMEM((total, pair_ch), F32),
+            pltpu.VMEM((LANES, wide), F32),
+            pltpu.VMEM((tokens // per, 2, seqs, LANES), F32),
+        ],
+    )(right, left, unit_rows, by_row, final_projector, cot_cols, additive_term.reshape(1, pair_ch))
+    got = exchange(messages, "cols")
+    back, own, *messages = call(
+        functools.partial(between_kernel, rows_axis=rows, share=share),
+        (
+            shape((2 * quarter * tokens // per, LANES), F32),
+            shape((share + width, LANES), F32),
+            *[shape((share + width, LANES), BF16)] * (rows - 1),
+        ),
+        [pltpu.VMEM((message, LANES), F32)],
+    )(own, *got)
+    got = exchange(messages, "rows")
+    alignment_slope = call(
+        back_kernel,
+        shape((tokens, quarter, width), F32),
+        [pltpu.VMEM((tokens, quarter, width), F32)],
+        flops=10**8,
+    )(back, alignment_features, gain, first, second)
+    final_slope, first_slope, second_slope = call(
+        last_kernel,
+        (shape((share, pair_ch), F32), shape((chans, width), F32), shape((chans, width), F32)),
+    )(own, *got)
+    return update, alignment_slope, final_slope, first_slope.T, second_slope.T
+
+
+def fits(mesh, alignment_features, first_projector, final_projector):
+    rows, cols = mesh.shape["rows"], mesh.shape["cols"]
+    tokens = alignment_features.shape[0] // (mesh.shape["groups"] * rows)
+    quarter = alignment_features.shape[1] // cols
+    width, chans = first_projector.shape
+    per = LANES // chans
+    return (
+        rows == cols == 4
+        and chans * per == LANES
+        and chans % per == 0
+        and chans // per == SUBLANES
+        and 2 * width == LANES
+        and final_projector.shape[1] == LANES
+        and quarter == SUBLANES
+        and tokens % (2 * SUBLANES) == 0
+        and quarter * cols == chans
+        and chans // per * tokens == LANES
+    )
+
+
 def solution(mesh):
     in_specs = (
         P(("groups", "rows"), "cols", None),
@@ -154,4 +562,15 @@
         P("groups", None),
         P("groups", None),
     )
-    return jax.shard_map(local, mesh=mesh, in_specs=in_specs, out_specs=out_specs, check_vma=False)
+
+    def whole(*args):
+        square = fits(mesh, args[0], args[3], args[5])
+        return jax.shard_map(
+            local_square if square else local_general,
+            mesh=mesh,
+            in_specs=in_specs,
+            out_specs=out_specs,
+            check_vma=False,
+        )(*args)
+
+    return whole

time: 163 us -> 47.2 us (0.29)
  blocking collectives: 91.1 us -> 0 us
  waiting for transfers between devices: 33.7 us -> 8.26 us
  starting transfers between devices: 0.12 us -> 20 us
  Pallas kernels: 0 us -> 15.4 us
  between operations: 14 us -> 0.67 us
  local copies, waits for them, and re-layouts: 14.4 us -> 2.49 us
  matrix products: 7.47 us -> 0 us
    psum x1 -> x0, blocking collectives: 58.4 us -> none  [local(): lax.psum((left_term, right_term), ('rows', 'cols'))]
    reduce_scatter x3 -> x0, waiting for transfers between devices: 33 us -> none  [the longest x1 20.4 us: local(): lax.psum_scatter(moved, 'rows', scatter_dimension=0, tiled=True)]
    all_gather x3 -> x0, blocking collectives: 25.6 us -> none  [the longest x1 13.8 us: local(): right_all = lax.all_gather(right_wide, 'rows', axis=0, tiled=True)]
    ppermute x0 -> x10, starting transfers between devices: none -> 20 us  [the longest x9 18.4 us: exchange(): lax.ppermute(m, axis, [(p, p ^ k) for p in range(size)])]
    pallas_call x0 -> x7, Pallas kernels: none -> 15.4 us  [the longest x1 3.25 us: local_square(): call(functools.partial(pair_kernel, chans=chans, rows_axis=rows, cols_axi...]
    ppermute x0 -> x10, waiting for transfers between devices: none -> 8.26 us  [the longest x9 8.26 us: exchange(): lax.ppermute(m, axis, [(p, p ^ k) for p in range(size)])]
    dot_general x30 -> x0, matrix products: 7.47 us -> none  [the longest x4 1.28 us: advance(): jnp.einsum('isc,jsd->ijcd', left_slab, right_cols, preferred_element_type...]
    all_to_all x1 -> x0, blocking collectives: 7.16 us -> none  [local(): lax.all_to_all(right_part.reshape(block, seqs * chans), 'cols', split_axi...]
  transfers between devices with their start and end apart: 3 -> 10, of which waited for: 2 -> 4; matrix products, arithmetic and copies ran while one was open for 2% -> 0% of each run, Pallas kernels for 0% -> 10%
where the time goes in v2:
time: 47.2 us; the launch traced here: 46.8 us
  starting transfers between devices  20 us (42%)
  Pallas kernels  15.4 us (33%)
  waiting for transfers between devices  8.26 us (18%)
  local copies, waits for them, and re-layouts  2.49 us (5%)
  between operations  0.67 us (1%)
    ppermute x9, starting transfers between devices, exchange(): lax.ppermute(m, axis, [(p, p ^ k) for p in range(size)])  18.4 us
    ppermute x9, waiting for transfers between devices, exchange(): lax.ppermute(m, axis, [(p, p ^ k) for p in range(size)])  8.26 us
    pallas_call x1, Pallas kernels, local_square(): call(functools.partial(pair_kernel, chans=chans, rows_axis=rows, cols_axi...  3.25 us
    pallas_call x1, Pallas kernels, local_square(): call(project_kernel, (shape((2 * packed + tall, LANES), BF16), shape((tal...  2.66 us
    pallas_call x1, Pallas kernels, local_square(): call(functools.partial(grad_kernel, chans=chans), (shape((tall, wide), BF...  2.66 us
    unnamed x20, local copies, waits for them, and re-layouts  2.49 us
    pallas_call x1, Pallas kernels, local_square(): call(back_kernel, shape((tokens, quarter, width), F32), [pltpu.VMEM((toke...  1.81 us
    pallas_call x1, Pallas kernels, local_square(): call(functools.partial(between_kernel, rows_axis=rows, share=share), (sha...  1.79 us
  transfers between devices with their start and end apart: 10, of which 4 were waited for; matrix products, arithmetic and copies ran while one was open for 0% of the time, Pallas kernels for 10%

profile of v2, /device:TPU:0, one launch (start us, length us, event | category | flops | bytes accessed | tf_op | source)
XLA Modules:
  0.0 46.8 jit_solution(4984113545067736259)
XLA Ops:
  0.6 1.7 %shard_map.119.n0 = bf16[64,128]{1,0:T(8,128)(2,1)} custom-call(f32[16,8,64]{2,1,0:T(8,128)} %x_ref.3, f32[1,64]{1,0:T(1,128)} %bitcast.13, f32[1,64]{1,0:T(1,128)} %bitcast.12), custom_call_target="tpu_custom_call" | custom-call | tf_op jit(solution)/shard_map/pallas_call | solution.py:458
  2.3 2.4 %collective-permute-start.2 = (bf16[64,128]{1,0:T(8,128)(2,1)}, bf16[64,128]{1,0:T(8,128)(2,1)S(1)}, u32[]{:S(2)}, u32[]{:S(2)}) collective-permute-start(bf16[64,128]{1,0:T(8,128)(2,1)} %shard_map.119.n0), channel_id=1, source_target_pairs={{0,3},{1,2},{2,1},{3,0},{4,7},{5,6},{6,5},{7,4},{8,11},{9,10},{10,... | collective-permute-start | bytes 49160 | tf_op jit(solution)/shard_map/ppermute | solution.py:428
  4.7 0.6 %collective-permute-start.1 = (bf16[64,128]{1,0:T(8,128)(2,1)}, bf16[64,128]{1,0:T(8,128)(2,1)S(1)}, u32[]{:S(2)}, u32[]{:S(2)}) collective-permute-start(bf16[64,128]{1,0:T(8,128)(2,1)} %shard_map.119.n0), channel_id=1, source_target_pairs={{0,2},{1,3},{2,0},{3,1},{4,6},{5,7},{6,4},{7,5},{8,10},{9,11},{10,... | collective-permute-start | bytes 49160 | tf_op jit(solution)/shard_map/ppermute | solution.py:428
  5.3 0.1 collective-permute-start
  5.4 2.7 %shard_map.120 = (bf16[128,2048]{1,0:T(8,128)(2,1)}, bf16[128,2048]{1,0:T(8,128)(2,1)}, bf16[256,128]{1,0:T(8,128)(2,1)}) custom-call(bf16[16,16,128]{2,1,0:T(8,128)(2,1)} %cot_ref.1, bf16[1024,128]{1,0:T(8,128)(2,1)} %final_ref.3), custom_call_target="tpu_custom_call" | custom-call | flops 268435456 | tf_op jit(solution)/shard_map/pallas_call | solution.py:462
  8.1 0.0 collective-permute-done.2.n3
  8.1 0.0 copy-start.7
  8.1 0.6 %collective-permute-done.1.n2 = bf16[64,128]{1,0:T(8,128)(2,1)S(1)} collective-permute-done((bf16[64,128]{1,0:T(8,128)(2,1)}, bf16[64,128]{1,0:T(8,128)(2,1)S(1)}, u32[]{:S(2)}, u32[]{:S(2)}) %collective-permute-start.1) | collective-permute-done | bytes 16416 | tf_op jit(solution)/shard_map/ppermute | solution.py:428
  8.7 0.0 copy-start.8
  8.7 0.0 collective-permute-done.n1
  8.7 0.0 copy-start.9
  8.7 0.0 copy-done.7
  8.7 0.6 %copy-done.8 = bf16[64,128]{1,0:T(8,128)(2,1)} copy-done((bf16[64,128]{1,0:T(8,128)(2,1)}, bf16[64,128]{1,0:T(8,128)(2,1)S(1)}, u32[]{:S(2)}) %copy-start.8) | copy-done | bytes 16408
  9.3 0.0 copy-done.9
  9.3 2.7 %shard_map.121 = (bf16[384,128]{1,0:T(8,128)(2,1)}, bf16[128,128]{1,0:T(8,128)(2,1)}, bf16[4,128,64]{2,1,0:T(8,128)(2,1)}) custom-call(bf16[64,128]{1,0:T(8,128)(2,1)} %shard_map.119.n0, bf16[64,128]{1,0:T(8,128)(2,1)} %copy-done.9, bf16[64,128]{1,0:T(8,128)(2,1)} %copy-done.8, bf16[64,128]{1,0:T(8,128)(2,1)} %copy-done.7, bf16[32,64]{1,0:T(8,128)(2,1)} %bitcast.7, ...), custom_call_target="tpu_custom_call" | custom-call | tf_op jit(solution)/shard_map/pallas_call | solution.py:472
  12.0 1.5 %collective-permute-start.3 = (bf16[384,128]{1,0:T(8,128)(2,1)}, bf16[384,128]{1,0:T(8,128)(2,1)S(1)}, u32[]{:S(2)}, u32[]{:S(2)}) collective-permute-start(bf16[384,128]{1,0:T(8,128)(2,1)} %get-tuple-element.25), channel_id=1, source_target_pairs={{0,0},{1,4},{2,8},{3,12},{4,1},{5,5},{6,9},{7,13},{8,2},{9,6},{10,... | collective-permute-start | bytes 294920 | tf_op jit(solution)/shard_map/ppermute | solution.py:486
  13.5 0.0 collective-permute-done.3.right_ref
  13.5 0.0 copy-start.3
  13.5 0.6 %copy-done.3 = bf16[384,128]{1,0:T(8,128)(2,1)} copy-done((bf16[384,128]{1,0:T(8,128)(2,1)}, bf16[384,128]{1,0:T(8,128)(2,1)S(1)}, u32[]{:S(2)}) %copy-start.3) | copy-done | bytes 98328
  14.2 3.2 %shard_map.122 = (bf16[16,16,128]{2,1,0:T(8,128)(2,1)}, f32[384,128]{1,0:T(8,128)}, bf16[384,128]{1,0:T(8,128)(2,1)}, bf16[384,128]{1,0:T(8,128)(2,1)}, bf16[384,128]{1,0:T(8,128)(2,1)}) custom-call(bf16[384,128]{1,0:T(8,128)(2,1)} %copy-done.3, bf16[128,128]{1,0:T(8,128)(2,1)} %get-tuple-element.26.left_ref, ...), custom_call_target="tpu_custom_call" | custom-call | tf_op jit(solution)/shard_map/pallas_call | solution.py:488
  17.4 4.6 %collective-permute-start.4 = (bf16[384,128]{1,0:T(8,128)(2,1)}, bf16[384,128]{1,0:T(8,128)(2,1)S(1)}, u32[]{:S(2)}, u32[]{:S(2)}) collective-permute-start(bf16[384,128]{1,0:T(8,128)(2,1)} %get-tuple-element.32), channel_id=1, source_target_pairs={{0,1},{1,0},{2,3},{3,2},{4,5},{5,4},{6,7},{7,6},{8,9},{9,8},{10,11... | collective-permute-start | bytes 294920 | tf_op jit(solution)/shard_map/ppermute | solution.py:428
  22.0 6.3 %collective-permute-start.5 = (bf16[384,128]{1,0:T(8,128)(2,1)}, bf16[384,128]{1,0:T(8,128)(2,1)S(1)}, u32[]{:S(2)}, u32[]{:S(2)}) collective-permute-start(bf16[384,128]{1,0:T(8,128)(2,1)} %get-tuple-element.33), channel_id=1, source_target_pairs={{0,2},{1,3},{2,0},{3,1},{4,6},{5,7},{6,4},{7,5},{8,10},{9,11},{10,... | collective-permute-start | bytes 294920 | tf_op jit(solution)/shard_map/ppermute | solution.py:428
  28.2 0.1 collective-permute-start.6
  28.4 0.0 collective-permute-done.4.r1
  28.4 0.0 copy-start
  28.4 3.7 %collective-permute-done.5.r2 = bf16[384,128]{1,0:T(8,128)(2,1)S(1)} collective-permute-done((bf16[384,128]{1,0:T(8,128)(2,1)}, bf16[384,128]{1,0:T(8,128)(2,1)S(1)}, u32[]{:S(2)}, u32[]{:S(2)}) %collective-permute-start.5) | collective-permute-done | bytes 98336 | tf_op jit(solution)/shard_map/ppermute | solution.py:428
  32.1 0.0 copy-start.1
  32.1 1.7 %collective-permute-done.6.r3 = bf16[384,128]{1,0:T(8,128)(2,1)S(1)} collective-permute-done((bf16[384,128]{1,0:T(8,128)(2,1)}, bf16[384,128]{1,0:T(8,128)(2,1)S(1)}, u32[]{:S(2)}, u32[]{:S(2)}) %collective-permute-start.6) | collective-permute-done | bytes 98336 | tf_op jit(solution)/shard_map/ppermute | solution.py:428
  33.8 0.0 copy-start.2
  33.8 0.0 copy-done
  33.8 0.0 copy-done.1
  33.8 0.6 %copy-done.2 = bf16[384,128]{1,0:T(8,128)(2,1)} copy-done((bf16[384,128]{1,0:T(8,128)(2,1)}, bf16[384,128]{1,0:T(8,128)(2,1)S(1)}, u32[]{:S(2)}) %copy-start.2) | copy-done | bytes 98328
  34.5 1.8 %shard_map.123 = (f32[64,128]{1,0:T(8,128)}, f32[128,128]{1,0:T(8,128)}, bf16[128,128]{1,0:T(8,128)(2,1)}, bf16[128,128]{1,0:T(8,128)(2,1)}, bf16[128,128]{1,0:T(8,128)(2,1)}) custom-call(f32[384,128]{1,0:T(8,128)} %get-tuple-element.31.own_ref, bf16[384,128]{1,0:T(8,128)(2,1)} %copy-done, bf16[384,128]{1,0:T(8,128)(2,1)} %copy-done.1, ...), custom_call_target="tpu_custom_call" | custom-call | tf_op jit(solution)/shard_map/pallas_call | solution.py:504
  36.3 0.1 collective-permute-start.7
  36.3 2.4 %collective-permute-start.8 = (bf16[128,128]{1,0:T(8,128)(2,1)}, bf16[128,128]{1,0:T(8,128)(2,1)S(1)}, u32[]{:S(2)}, u32[]{:S(2)}) collective-permute-start(bf16[128,128]{1,0:T(8,128)(2,1)} %get-tuple-element.38), channel_id=1, source_target_pairs={{0,8},{4,12},{8,0},{12,4},{1,9},{5,13},{9,1},{13,5},{2,10},{6,14},... | collective-permute-start | bytes 98312 | tf_op jit(solution)/shard_map/ppermute | solution.py:428
  38.7 1.9 %collective-permute-start.9 = (bf16[128,128]{1,0:T(8,128)(2,1)}, bf16[128,128]{1,0:T(8,128)(2,1)S(1)}, u32[]{:S(2)}, u32[]{:S(2)}) collective-permute-start(bf16[128,128]{1,0:T(8,128)(2,1)} %get-tuple-element.39), channel_id=1, source_target_pairs={{0,12},{4,8},{8,4},{12,0},{1,13},{5,9},{9,5},{13,1},{2,14},{6,10},... | collective-permute-start | bytes 98312 | tf_op jit(solution)/shard_map/ppermute | solution.py:428
  40.6 1.8 %shard_map.124 = f32[16,8,64]{2,1,0:T(8,128)} custom-call(f32[64,128]{1,0:T(8,128)} %get-tuple-element.35.back_ref, f32[16,8,64]{2,1,0:T(8,128)} %x_ref.3, f32[1,64]{1,0:T(1,128)} %bitcast.14, bf16[32,64]{1,0:T(8,128)(2,1)} %bitcast.8, bf16[32,64]{1,0:T(8,128)(2,1)} %bitcast.10), custom_call_target="tpu_custom_call" | custom-call | flops 100000000 | tf_op jit(solution)/shard_map/pallas_call | solution.py:514
  42.5 0.0 collective-permute-done.7.r1
  42.5 0.0 copy-start.4
  42.5 0.0 collective-permute-done.8.r2
  42.5 0.0 copy-start.5
  42.5 2.2 %collective-permute-done.9.r3 = bf16[128,128]{1,0:T(8,128)(2,1)S(1)} collective-permute-done((bf16[128,128]{1,0:T(8,128)(2,1)}, bf16[128,128]{1,0:T(8,128)(2,1)S(1)}, u32[]{:S(2)}, u32[]{:S(2)}) %collective-permute-start.9) | collective-permute-done | bytes 32800 | tf_op jit(solution)/shard_map/ppermute | solution.py:428
  44.6 0.0 copy-start.6
  44.6 0.0 copy-done.4
  44.6 0.0 copy-done.5
  44.6 0.6 %copy-done.6 = bf16[128,128]{1,0:T(8,128)(2,1)} copy-done((bf16[128,128]{1,0:T(8,128)(2,1)}, bf16[128,128]{1,0:T(8,128)(2,1)S(1)}, u32[]{:S(2)}) %copy-start.6) | copy-done | bytes 32792
  45.2 1.6 %shard_map.125 = (f32[64,128]{1,0:T(8,128)}, f32[32,64]{1,0:T(8,128)}, f32[32,64]{1,0:T(8,128)}) custom-call(f32[128,128]{1,0:T(8,128)} %get-tuple-element.36.own_ref, bf16[128,128]{1,0:T(8,128)(2,1)} %copy-done.4, bf16[128,128]{1,0:T(8,128)(2,1)} %copy-done.5, bf16[128,128]{1,0:T(8,128)(2,1)} %copy-done.6), custom_call_target="tpu_custom_call" | custom-call | tf_op jit(solution)/shard_map/pallas_call | solution.py:520
Async XLA Ops:
  2.3 5.7 %collective-permute-start.2 = (bf16[64,128]{1,0:T(8,128)(2,1)}, bf16[64,128]{1,0:T(8,128)(2,1)S(1)}, u32[]{:S(2)}, u32[]{:S(2)}) collective-permute-start(bf16[64,128]{1,0:T(8,128)(2,1)} %shard_map.119.n0), channel_id=1, source_target_pairs={{0,3},{1,2},{2,1},{3,0},{4,7},{5,6},{6,5},{7,4},{8,11},{9,10},{10,... | collective-permute-start | bytes 49160 | tf_op jit(solution)/shard_map/ppermute | solution.py:428
  4.7 3.9 %collective-permute-start.1 = (bf16[64,128]{1,0:T(8,128)(2,1)}, bf16[64,128]{1,0:T(8,128)(2,1)S(1)}, u32[]{:S(2)}, u32[]{:S(2)}) collective-permute-start(bf16[64,128]{1,0:T(8,128)(2,1)} %shard_map.119.n0), channel_id=1, source_target_pairs={{0,2},{1,3},{2,0},{3,1},{4,6},{5,7},{6,4},{7,5},{8,10},{9,11},{10,... | collective-permute-start | bytes 49160 | tf_op jit(solution)/shard_map/ppermute | solution.py:428
  5.3 3.4 %collective-permute-start = (bf16[64,128]{1,0:T(8,128)(2,1)}, bf16[64,128]{1,0:T(8,128)(2,1)S(1)}, u32[]{:S(2)}, u32[]{:S(2)}) collective-permute-start(bf16[64,128]{1,0:T(8,128)(2,1)} %shard_map.119.n0), channel_id=1, source_target_pairs={{0,1},{1,0},{2,3},{3,2},{4,5},{5,4},{6,7},{7,6},{8,9},{9,8},{10,11... | collective-permute-start | bytes 49160 | tf_op jit(solution)/shard_map/ppermute | solution.py:428
  8.1 0.6 %copy-start.7 = (bf16[64,128]{1,0:T(8,128)(2,1)}, bf16[64,128]{1,0:T(8,128)(2,1)S(1)}, u32[]{:S(2)}) copy-start(bf16[64,128]{1,0:T(8,128)(2,1)S(1)} %collective-permute-done.2.n3) | copy-start | bytes 49156
  8.7 0.6 %copy-start.8 = (bf16[64,128]{1,0:T(8,128)(2,1)}, bf16[64,128]{1,0:T(8,128)(2,1)S(1)}, u32[]{:S(2)}) copy-start(bf16[64,128]{1,0:T(8,128)(2,1)S(1)} %collective-permute-done.1.n2) | copy-start | bytes 49156
  8.7 0.6 %copy-start.9 = (bf16[64,128]{1,0:T(8,128)(2,1)}, bf16[64,128]{1,0:T(8,128)(2,1)S(1)}, u32[]{:S(2)}) copy-start(bf16[64,128]{1,0:T(8,128)(2,1)S(1)} %collective-permute-done.n1) | copy-start | bytes 49156
  12.0 1.5 %collective-permute-start.3 = (bf16[384,128]{1,0:T(8,128)(2,1)}, bf16[384,128]{1,0:T(8,128)(2,1)S(1)}, u32[]{:S(2)}, u32[]{:S(2)}) collective-permute-start(bf16[384,128]{1,0:T(8,128)(2,1)} %get-tuple-element.25), channel_id=1, source_target_pairs={{0,0},{1,4},{2,8},{3,12},{4,1},{5,5},{6,9},{7,13},{8,2},{9,6},{10,... | collective-permute-start | bytes 294920 | tf_op jit(solution)/shard_map/ppermute | solution.py:486
  13.5 0.6 %copy-start.3 = (bf16[384,128]{1,0:T(8,128)(2,1)}, bf16[384,128]{1,0:T(8,128)(2,1)S(1)}, u32[]{:S(2)}) copy-start(bf16[384,128]{1,0:T(8,128)(2,1)S(1)} %collective-permute-done.3.right_ref) | copy-start | bytes 294916
  17.4 10.9 %collective-permute-start.4 = (bf16[384,128]{1,0:T(8,128)(2,1)}, bf16[384,128]{1,0:T(8,128)(2,1)S(1)}, u32[]{:S(2)}, u32[]{:S(2)}) collective-permute-start(bf16[384,128]{1,0:T(8,128)(2,1)} %get-tuple-element.32), channel_id=1, source_target_pairs={{0,1},{1,0},{2,3},{3,2},{4,5},{5,4},{6,7},{7,6},{8,9},{9,8},{10,11... | collective-permute-start | bytes 294920 | tf_op jit(solution)/shard_map/ppermute | solution.py:428
  22.0 10.1 %collective-permute-start.5 = (bf16[384,128]{1,0:T(8,128)(2,1)}, bf16[384,128]{1,0:T(8,128)(2,1)S(1)}, u32[]{:S(2)}, u32[]{:S(2)}) collective-permute-start(bf16[384,128]{1,0:T(8,128)(2,1)} %get-tuple-element.33), channel_id=1, source_target_pairs={{0,2},{1,3},{2,0},{3,1},{4,6},{5,7},{6,4},{7,5},{8,10},{9,11},{10,... | collective-permute-start | bytes 294920 | tf_op jit(solution)/shard_map/ppermute | solution.py:428
  28.2 5.6 %collective-permute-start.6 = (bf16[384,128]{1,0:T(8,128)(2,1)}, bf16[384,128]{1,0:T(8,128)(2,1)S(1)}, u32[]{:S(2)}, u32[]{:S(2)}) collective-permute-start(bf16[384,128]{1,0:T(8,128)(2,1)} %get-tuple-element.34), channel_id=1, source_target_pairs={{0,3},{1,2},{2,1},{3,0},{4,7},{5,6},{6,5},{7,4},{8,11},{9,10},{10,... | collective-permute-start | bytes 294920 | tf_op jit(solution)/shard_map/ppermute | solution.py:428
  28.4 5.5 %copy-start = (bf16[384,128]{1,0:T(8,128)(2,1)}, bf16[384,128]{1,0:T(8,128)(2,1)S(1)}, u32[]{:S(2)}) copy-start(bf16[384,128]{1,0:T(8,128)(2,1)S(1)} %collective-permute-done.4.r1) | copy-start | bytes 294916
  32.1 1.7 %copy-start.1 = (bf16[384,128]{1,0:T(8,128)(2,1)}, bf16[384,128]{1,0:T(8,128)(2,1)S(1)}, u32[]{:S(2)}) copy-start(bf16[384,128]{1,0:T(8,128)(2,1)S(1)} %collective-permute-done.5.r2) | copy-start | bytes 294916
  33.8 0.6 %copy-start.2 = (bf16[384,128]{1,0:T(8,128)(2,1)}, bf16[384,128]{1,0:T(8,128)(2,1)S(1)}, u32[]{:S(2)}) copy-start(bf16[384,128]{1,0:T(8,128)(2,1)S(1)} %collective-permute-done.6.r3) | copy-start | bytes 294916
  36.3 6.2 %collective-permute-start.7 = (bf16[128,128]{1,0:T(8,128)(2,1)}, bf16[128,128]{1,0:T(8,128)(2,1)S(1)}, u32[]{:S(2)}, u32[]{:S(2)}) collective-permute-start(bf16[128,128]{1,0:T(8,128)(2,1)} %get-tuple-element.37), channel_id=1, source_target_pairs={{0,4},{4,0},{8,12},{12,8},{1,5},{5,1},{9,13},{13,9},{2,6},{6,2},{1... | collective-permute-start | bytes 98312 | tf_op jit(solution)/shard_map/ppermute | solution.py:428
  36.3 6.1 %collective-permute-start.8 = (bf16[128,128]{1,0:T(8,128)(2,1)}, bf16[128,128]{1,0:T(8,128)(2,1)S(1)}, u32[]{:S(2)}, u32[]{:S(2)}) collective-permute-start(bf16[128,128]{1,0:T(8,128)(2,1)} %get-tuple-element.38), channel_id=1, source_target_pairs={{0,8},{4,12},{8,0},{12,4},{1,9},{5,13},{9,1},{13,5},{2,10},{6,14},... | collective-permute-start | bytes 98312 | tf_op jit(solution)/shard_map/ppermute | solution.py:428
  38.7 5.9 %collective-permute-start.9 = (bf16[128,128]{1,0:T(8,128)(2,1)}, bf16[128,128]{1,0:T(8,128)(2,1)S(1)}, u32[]{:S(2)}, u32[]{:S(2)}) collective-permute-start(bf16[128,128]{1,0:T(8,128)(2,1)} %get-tuple-element.39), channel_id=1, source_target_pairs={{0,12},{4,8},{8,4},{12,0},{1,13},{5,9},{9,5},{13,1},{2,14},{6,10},... | collective-permute-start | bytes 98312 | tf_op jit(solution)/shard_map/ppermute | solution.py:428
  42.5 2.2 %copy-start.4 = (bf16[128,128]{1,0:T(8,128)(2,1)}, bf16[128,128]{1,0:T(8,128)(2,1)S(1)}, u32[]{:S(2)}) copy-start(bf16[128,128]{1,0:T(8,128)(2,1)S(1)} %collective-permute-done.7.r1) | copy-start | bytes 98308
  42.5 2.2 %copy-start.5 = (bf16[128,128]{1,0:T(8,128)(2,1)}, bf16[128,128]{1,0:T(8,128)(2,1)S(1)}, u32[]{:S(2)}) copy-start(bf16[128,128]{1,0:T(8,128)(2,1)S(1)} %collective-permute-done.8.r2) | copy-start | bytes 98308
  44.6 0.6 %copy-start.6 = (bf16[128,128]{1,0:T(8,128)(2,1)}, bf16[128,128]{1,0:T(8,128)(2,1)S(1)}, u32[]{:S(2)}) copy-start(bf16[128,128]{1,0:T(8,128)(2,1)S(1)} %collective-permute-done.9.r3) | copy-start | bytes 98308

commit v3 on v2

--- a/solution.py
+++ b/solution.py
@@ -165,14 +165,21 @@
     return centered * spread, spread
 
 
-def call(kernel, out_shape, scratch=(), flops=0, **kw):
-    return pl.pallas_call(
-        kernel,
-        out_shape=out_shape,
-        scratch_shapes=list(scratch),
-        cost_estimate=pl.CostEstimate(flops=flops, bytes_accessed=0, transcendentals=0),
-        **kw,
-    )
+def call(kernel, out_shape, scratch=(), flops=0):
+    on_chip = pl.BlockSpec(memory_space=pltpu.VMEM)
+
+    def run(*args):
+        return pl.pallas_call(
+            kernel,
+            out_shape=out_shape,
+            in_specs=[on_chip] * len(args),
+            out_specs=jax.tree.map(lambda _: on_chip, out_shape),
+            scratch_shapes=list(scratch),
+            cost_estimate=pl.CostEstimate(flops=flops, bytes_accessed=0, transcendentals=0),
+            compiler_params=pltpu.CompilerParams(vmem_limit_bytes=16 * 2**20),
+        )(*args)
+
+    return run
 
 
 def norm_kernel(x_ref, gain_ref, offset_ref, out_ref):

time: 47.2 us -> 38.9 us (0.82)
  Pallas kernels: 15.4 us -> 5.24 us
  waiting for transfers between devices: 8.26 us -> 10.3 us
  starting transfers between devices: 20 us -> 19.3 us
  local copies, waits for them, and re-layouts: 2.49 us -> 3.11 us
    pallas_call x7, Pallas kernels: 15.4 us -> 5.24 us  [run(): pl.pallas_call(kernel, out_shape=out_shape, in_specs=[on_chip] * len(args...]
    ppermute x9, waiting for transfers between devices: 8.26 us -> 10.3 us  [exchange(): lax.ppermute(m, axis, [(p, p ^ k) for p in range(size)])]
    ppermute x1, starting transfers between devices: 1.54 us -> 0.67 us  [local_square(): right = lax.ppermute(send, ('rows', 'cols'), flip)]
    unnamed x20 -> x18, local copies, waits for them, and re-layouts: 2.49 us -> 3.11 us
  transfers between devices with their start and end apart: 10 -> 10, of which waited for: 4 -> 5; matrix products, arithmetic and copies ran while one was open for 0% -> 0% of each run, Pallas kernels for 10% -> 4%
where the time goes in v3:
time: 38.9 us; the launch traced here: 38.7 us
  starting transfers between devices  19.3 us (50%)
  waiting for transfers between devices  10.3 us (26%)
  Pallas kernels  5.24 us (13%)
  local copies, waits for them, and re-layouts  3.11 us (8%)
  between operations  0.72 us (2%)
    ppermute x9, starting transfers between devices, exchange(): lax.ppermute(m, axis, [(p, p ^ k) for p in range(size)])  18.7 us
    ppermute x9, waiting for transfers between devices, exchange(): lax.ppermute(m, axis, [(p, p ^ k) for p in range(size)])  10.3 us
    pallas_call x7, Pallas kernels, run(): pl.pallas_call(kernel, out_shape=out_shape, in_specs=[on_chip] * len(args...  5.24 us
    unnamed x18, local copies, waits for them, and re-layouts  3.11 us
  transfers between devices with their start and end apart: 10, of which 5 were waited for; matrix products, arithmetic and copies ran while one was open for 0% of the time, Pallas kernels for 4%

profile of v3, /device:TPU:0, one launch (start us, length us, event | category | flops | bytes accessed | tf_op | source)
XLA Modules:
  0.0 38.7 jit_solution(13239493615763985114)
XLA Ops:
  0.6 0.0 copy-start.6
  0.6 0.0 copy-start.7
  0.7 0.6 %copy-done.6 = f32[64]{0:T(128)S(1)} copy-done((f32[64]{0:T(128)S(1)}, f32[64]{0:T(128)}, u32[]{:S(2)}) %copy-start.6) | copy-done | bytes 280
  1.3 0.0 copy-done.7
  1.3 0.0 copy-start.1
  1.3 0.8 %copy-done.1 = f32[16,8,64]{2,1,0:T(8,128)S(1)} copy-done((f32[16,8,64]{2,1,0:T(8,128)S(1)}, f32[16,8,64]{2,1,0:T(8,128)}, u32[]{:S(2)}) %copy-start.1) | copy-done | bytes 32792
  2.1 0.0 copy-start.8
  2.1 0.2 shard_map.119.n0
  2.4 2.5 %collective-permute-start.2 = (bf16[64,128]{1,0:T(8,128)(2,1)S(1)}, bf16[64,128]{1,0:T(8,128)(2,1)S(1)}, u32[]{:S(2)}, u32[]{:S(2)}) collective-permute-start(bf16[64,128]{1,0:T(8,128)(2,1)S(1)} %shard_map.119.n0), channel_id=1, source_target_pairs={{0,3},{1,2},{2,1},{3,0},{4,7},{5,6},{6,5},{7,4},{8,11},{9,10},{10,... | collective-permute-start | bytes 49160 | tf_op jit(solution)/shard_map/ppermute | solution.py:435
  4.8 0.6 %collective-permute-start.1 = (bf16[64,128]{1,0:T(8,128)(2,1)S(1)}, bf16[64,128]{1,0:T(8,128)(2,1)S(1)}, u32[]{:S(2)}, u32[]{:S(2)}) collective-permute-start(bf16[64,128]{1,0:T(8,128)(2,1)S(1)} %shard_map.119.n0), channel_id=1, source_target_pairs={{0,2},{1,3},{2,0},{3,1},{4,6},{5,7},{6,4},{7,5},{8,10},{9,11},{10,... | collective-permute-start | bytes 49160 | tf_op jit(solution)/shard_map/ppermute | solution.py:435
  5.5 0.0 collective-permute-start
  5.5 0.0 copy-done.8
  5.5 0.0 copy-start
  5.5 0.9 %copy-done = bf16[1024,128]{1,0:T(8,128)(2,1)S(1)} copy-done((bf16[1024,128]{1,0:T(8,128)(2,1)S(1)}, bf16[1024,128]{1,0:T(8,128)(2,1)}, u32[]{:S(2)}) %copy-start) | copy-done | bytes 262168
  6.5 0.0 copy-start.3
  6.5 0.0 copy-start.4
  6.5 0.7 %shard_map.120 = (bf16[128,2048]{1,0:T(8,128)(2,1)S(1)}, bf16[128,2048]{1,0:T(8,128)(2,1)S(1)}, bf16[256,128]{1,0:T(8,128)(2,1)S(1)}) custom-call(bf16[16,16,128]{2,1,0:T(8,128)(2,1)S(1)} %copy-done.8, bf16[1024,128]{1,0:T(8,128)(2,1)S(1)} %copy-done), custom_call_target="tpu_custom_call" | custom-call | flops 268435456 | tf_op jit(solution)/shard_map/pallas_call | solution.py:172
  7.2 0.0 collective-permute-done.2.n3
  7.2 1.4 %collective-permute-done.1.n2 = bf16[64,128]{1,0:T(8,128)(2,1)S(1)} collective-permute-done((bf16[64,128]{1,0:T(8,128)(2,1)S(1)}, bf16[64,128]{1,0:T(8,128)(2,1)S(1)}, u32[]{:S(2)}, u32[]{:S(2)}) %collective-permute-start.1) | collective-permute-done | bytes 16416 | tf_op jit(solution)/shard_map/ppermute | solution.py:435
  8.6 0.0 collective-permute-done.n1
  8.6 0.0 copy-done.3
  8.6 0.0 copy-done.4
  8.6 0.9 %shard_map.121 = (bf16[384,128]{1,0:T(8,128)(2,1)S(1)}, bf16[128,128]{1,0:T(8,128)(2,1)S(1)}, bf16[4,128,64]{2,1,0:T(8,128)(2,1)S(1)}) custom-call(bf16[64,128]{1,0:T(8,128)(2,1)S(1)} %shard_map.119.n0, bf16[64,128]{1,0:T(8,128)(2,1)S(1)} %collective-permute-done.n1, bf16[64,128]{1,0:T(8,128)(2,1)S(1)} %collective-permute-done.1.n2, ...), custom_call_target="tpu_custom_call" | custom-call | tf_op jit(solution)/shard_map/pallas_call | solution.py:172
  9.5 0.7 %collective-permute-start.3 = (bf16[384,128]{1,0:T(8,128)(2,1)S(1)}, bf16[384,128]{1,0:T(8,128)(2,1)S(1)}, u32[]{:S(2)}, u32[]{:S(2)}) collective-permute-start(bf16[384,128]{1,0:T(8,128)(2,1)S(1)} %get-tuple-element.25), channel_id=1, source_target_pairs={{0,0},{1,4},{2,8},{3,12},{4,1},{5,5},{6,9},{7,13},{8,2},{9,6},{10,... | collective-permute-start | bytes 294920 | tf_op jit(solution)/shard_map/ppermute | solution.py:493
  10.1 0.0 collective-permute-done.3.right_ref
  10.2 0.0 copy-start.5
  10.2 0.6 %copy-done.5 = f32[128]{0:T(128)S(1)} copy-done((f32[128]{0:T(128)S(1)}, f32[128]{0:T(128)}, u32[]{:S(2)}) %copy-start.5) | copy-done | bytes 536
  10.8 1.7 %shard_map.122 = (bf16[16,16,128]{2,1,0:T(8,128)(2,1)}, f32[384,128]{1,0:T(8,128)S(1)}, bf16[384,128]{1,0:T(8,128)(2,1)S(1)}, bf16[384,128]{1,0:T(8,128)(2,1)S(1)}, bf16[384,128]{1,0:T(8,128)(2,1)S(1)}) custom-call(bf16[384,128]{1,0:T(8,128)(2,1)S(1)} %collective-permute-done.3.right_ref, bf16[128,128]{1,0:T(8,128)(2,1)S(1)} %get-tuple-element.26.left_ref, ...), custom_call_target="tpu_custom_call" | custom-call | tf_op jit(solution)/shard_map/pallas_call | solution.py:172
  12.5 5.2 %collective-permute-start.4 = (bf16[384,128]{1,0:T(8,128)(2,1)S(1)}, bf16[384,128]{1,0:T(8,128)(2,1)S(1)}, u32[]{:S(2)}, u32[]{:S(2)}) collective-permute-start(bf16[384,128]{1,0:T(8,128)(2,1)S(1)} %get-tuple-element.32), channel_id=1, source_target_pairs={{0,1},{1,0},{2,3},{3,2},{4,5},{5,4},{6,7},{7,6},{8,9},{9,8},{10,11... | collective-permute-start | bytes 294920 | tf_op jit(solution)/shard_map/ppermute | solution.py:435
  17.7 5.8 %collective-permute-start.5 = (bf16[384,128]{1,0:T(8,128)(2,1)S(1)}, bf16[384,128]{1,0:T(8,128)(2,1)S(1)}, u32[]{:S(2)}, u32[]{:S(2)}) collective-permute-start(bf16[384,128]{1,0:T(8,128)(2,1)S(1)} %get-tuple-element.33), channel_id=1, source_target_pairs={{0,2},{1,3},{2,0},{3,1},{4,6},{5,7},{6,4},{7,5},{8,10},{9,11},{10,... | collective-permute-start | bytes 294920 | tf_op jit(solution)/shard_map/ppermute | solution.py:435
  23.5 0.1 collective-permute-start.6
  23.6 0.0 collective-permute-done.4.r1
  23.6 3.5 %collective-permute-done.5.r2 = bf16[384,128]{1,0:T(8,128)(2,1)S(1)} collective-permute-done((bf16[384,128]{1,0:T(8,128)(2,1)S(1)}, bf16[384,128]{1,0:T(8,128)(2,1)S(1)}, u32[]{:S(2)}, u32[]{:S(2)}) %collective-permute-start.5) | collective-permute-done | bytes 98336 | tf_op jit(solution)/shard_map/ppermute | solution.py:435
  27.1 1.7 %collective-permute-done.6.r3 = bf16[384,128]{1,0:T(8,128)(2,1)S(1)} collective-permute-done((bf16[384,128]{1,0:T(8,128)(2,1)S(1)}, bf16[384,128]{1,0:T(8,128)(2,1)S(1)}, u32[]{:S(2)}, u32[]{:S(2)}) %collective-permute-start.6) | collective-permute-done | bytes 98336 | tf_op jit(solution)/shard_map/ppermute | solution.py:435
  28.9 0.0 copy-start.2
  28.9 0.1 shard_map.123
  28.9 0.2 collective-permute-start.7
  29.1 3.2 %collective-permute-start.8 = (bf16[128,128]{1,0:T(8,128)(2,1)S(1)}, bf16[128,128]{1,0:T(8,128)(2,1)S(1)}, u32[]{:S(2)}, u32[]{:S(2)}) collective-permute-start(bf16[128,128]{1,0:T(8,128)(2,1)S(1)} %get-tuple-element.38), channel_id=1, source_target_pairs={{0,8},{4,12},{8,0},{12,4},{1,9},{5,13},{9,1},{13,5},{2,10},{6,14},... | collective-permute-start | bytes 98312 | tf_op jit(solution)/shard_map/ppermute | solution.py:435
  32.3 1.1 %collective-permute-start.9 = (bf16[128,128]{1,0:T(8,128)(2,1)S(1)}, bf16[128,128]{1,0:T(8,128)(2,1)S(1)}, u32[]{:S(2)}, u32[]{:S(2)}) collective-permute-start(bf16[128,128]{1,0:T(8,128)(2,1)S(1)} %get-tuple-element.39), channel_id=1, source_target_pairs={{0,12},{4,8},{8,4},{12,0},{1,13},{5,9},{9,5},{13,1},{2,14},{6,10},... | collective-permute-start | bytes 98312 | tf_op jit(solution)/shard_map/ppermute | solution.py:435
  33.4 0.0 copy-done.2
  33.4 1.0 %shard_map.124 = f32[16,8,64]{2,1,0:T(8,128)} custom-call(f32[64,128]{1,0:T(8,128)S(1)} %get-tuple-element.35.back_ref, f32[16,8,64]{2,1,0:T(8,128)S(1)} %copy-done.2, f32[1,64]{1,0:T(1,128)S(1)} %bitcast.14, bf16[32,64]{1,0:T(8,128)(2,1)S(1)} %bitcast.8, bf16[32,64]{1,0:T(8,128)(2,1)S(1)} %bitcast.10), custom_call_target="tpu_custom_call" | custom-call | flops 100000000 | tf_op jit(solution)/shard_map/pallas_call | solution.py:172
  34.3 0.0 collective-permute-done.7.r1
  34.3 0.2 collective-permute-done.8.r2
  34.5 3.5 %collective-permute-done.9.r3 = bf16[128,128]{1,0:T(8,128)(2,1)S(1)} collective-permute-done((bf16[128,128]{1,0:T(8,128)(2,1)S(1)}, bf16[128,128]{1,0:T(8,128)(2,1)S(1)}, u32[]{:S(2)}, u32[]{:S(2)}) %collective-permute-start.9) | collective-permute-done | bytes 32800 | tf_op jit(solution)/shard_map/ppermute | solution.py:435
  38.0 0.7 %shard_map.125 = (f32[64,128]{1,0:T(8,128)}, f32[32,64]{1,0:T(8,128)}, f32[32,64]{1,0:T(8,128)}) custom-call(f32[128,128]{1,0:T(8,128)S(1)} %get-tuple-element.36.own_ref, bf16[128,128]{1,0:T(8,128)(2,1)S(1)} %collective-permute-done.7.r1, bf16[128,128]{1,0:T(8,128)(2,1)S(1)} %collective-permute-done.8.r2, bf16[128,128]{1,0:T(8,128)(2,1)S(1)} %collective-permute-done.9.r3), custom_call_target="tpu_custom_call" | custom-call | tf_op jit(solution)/shard_map/pallas_call | solution.py:172
Async XLA Ops:
  0.6 0.7 %copy-start.6 = (f32[64]{0:T(128)S(1)}, f32[64]{0:T(128)}, u32[]{:S(2)}) copy-start(f32[64]{0:T(128)} %param.10) | copy-start | bytes 772
  0.6 0.7 %copy-start.7 = (f32[64]{0:T(128)S(1)}, f32[64]{0:T(128)}, u32[]{:S(2)}) copy-start(f32[64]{0:T(128)} %param.9) | copy-start | bytes 772
  1.3 0.8 %copy-start.1 = (f32[16,8,64]{2,1,0:T(8,128)S(1)}, f32[16,8,64]{2,1,0:T(8,128)}, u32[]{:S(2)}) copy-start(f32[16,8,64]{2,1,0:T(8,128)} %x_ref.3) | copy-start | bytes 98308
  2.1 3.4 %copy-start.8 = (bf16[16,16,128]{2,1,0:T(8,128)(2,1)S(1)}, bf16[16,16,128]{2,1,0:T(8,128)(2,1)}, u32[]{:S(2)}) copy-start(bf16[16,16,128]{2,1,0:T(8,128)(2,1)} %cot_ref.1) | copy-start | bytes 196612
  2.4 4.8 %collective-permute-start.2 = (bf16[64,128]{1,0:T(8,128)(2,1)S(1)}, bf16[64,128]{1,0:T(8,128)(2,1)S(1)}, u32[]{:S(2)}, u32[]{:S(2)}) collective-permute-start(bf16[64,128]{1,0:T(8,128)(2,1)S(1)} %shard_map.119.n0), channel_id=1, source_target_pairs={{0,3},{1,2},{2,1},{3,0},{4,7},{5,6},{6,5},{7,4},{8,11},{9,10},{10,... | collective-permute-start | bytes 49160 | tf_op jit(solution)/shard_map/ppermute | solution.py:435
  4.8 3.7 %collective-permute-start.1 = (bf16[64,128]{1,0:T(8,128)(2,1)S(1)}, bf16[64,128]{1,0:T(8,128)(2,1)S(1)}, u32[]{:S(2)}, u32[]{:S(2)}) collective-permute-start(bf16[64,128]{1,0:T(8,128)(2,1)S(1)} %shard_map.119.n0), channel_id=1, source_target_pairs={{0,2},{1,3},{2,0},{3,1},{4,6},{5,7},{6,4},{7,5},{8,10},{9,11},{10,... | collective-permute-start | bytes 49160 | tf_op jit(solution)/shard_map/ppermute | solution.py:435
  5.5 3.1 %collective-permute-start = (bf16[64,128]{1,0:T(8,128)(2,1)S(1)}, bf16[64,128]{1,0:T(8,128)(2,1)S(1)}, u32[]{:S(2)}, u32[]{:S(2)}) collective-permute-start(bf16[64,128]{1,0:T(8,128)(2,1)S(1)} %shard_map.119.n0), channel_id=1, source_target_pairs={{0,1},{1,0},{2,3},{3,2},{4,5},{5,4},{6,7},{7,6},{8,9},{9,8},{10,11... | collective-permute-start | bytes 49160 | tf_op jit(solution)/shard_map/ppermute | solution.py:435
  5.5 1.0 %copy-start = (bf16[1024,128]{1,0:T(8,128)(2,1)S(1)}, bf16[1024,128]{1,0:T(8,128)(2,1)}, u32[]{:S(2)}) copy-start(bf16[1024,128]{1,0:T(8,128)(2,1)} %final_ref.3) | copy-start | bytes 786436
  6.5 2.1 %copy-start.3 = (bf16[64,32]{0,1:T(8,128)(2,1)S(1)}, bf16[64,32]{0,1:T(8,128)(2,1)}, u32[]{:S(2)}) copy-start(bf16[64,32]{0,1:T(8,128)(2,1)} %param.11) | copy-start | bytes 12292
  6.5 2.1 %copy-start.4 = (bf16[64,32]{0,1:T(8,128)(2,1)S(1)}, bf16[64,32]{0,1:T(8,128)(2,1)}, u32[]{:S(2)}) copy-start(bf16[64,32]{0,1:T(8,128)(2,1)} %param.12) | copy-start | bytes 12292
  9.5 0.7 %collective-permute-start.3 = (bf16[384,128]{1,0:T(8,128)(2,1)S(1)}, bf16[384,128]{1,0:T(8,128)(2,1)S(1)}, u32[]{:S(2)}, u32[]{:S(2)}) collective-permute-start(bf16[384,128]{1,0:T(8,128)(2,1)S(1)} %get-tuple-element.25), channel_id=1, source_target_pairs={{0,0},{1,4},{2,8},{3,12},{4,1},{5,5},{6,9},{7,13},{8,2},{9,6},{10,... | collective-permute-start | bytes 294920 | tf_op jit(solution)/shard_map/ppermute | solution.py:493
  10.2 0.7 %copy-start.5 = (f32[128]{0:T(128)S(1)}, f32[128]{0:T(128)}, u32[]{:S(2)}) copy-start(f32[128]{0:T(128)} %param.14) | copy-start | bytes 1540
  12.5 11.1 %collective-permute-start.4 = (bf16[384,128]{1,0:T(8,128)(2,1)S(1)}, bf16[384,128]{1,0:T(8,128)(2,1)S(1)}, u32[]{:S(2)}, u32[]{:S(2)}) collective-permute-start(bf16[384,128]{1,0:T(8,128)(2,1)S(1)} %get-tuple-element.32), channel_id=1, source_target_pairs={{0,1},{1,0},{2,3},{3,2},{4,5},{5,4},{6,7},{7,6},{8,9},{9,8},{10,11... | collective-permute-start | bytes 294920 | tf_op jit(solution)/shard_map/ppermute | solution.py:435
  17.7 9.4 %collective-permute-start.5 = (bf16[384,128]{1,0:T(8,128)(2,1)S(1)}, bf16[384,128]{1,0:T(8,128)(2,1)S(1)}, u32[]{:S(2)}, u32[]{:S(2)}) collective-permute-start(bf16[384,128]{1,0:T(8,128)(2,1)S(1)} %get-tuple-element.33), channel_id=1, source_target_pairs={{0,2},{1,3},{2,0},{3,1},{4,6},{5,7},{6,4},{7,5},{8,10},{9,11},{10,... | collective-permute-start | bytes 294920 | tf_op jit(solution)/shard_map/ppermute | solution.py:435
  23.5 5.4 %collective-permute-start.6 = (bf16[384,128]{1,0:T(8,128)(2,1)S(1)}, bf16[384,128]{1,0:T(8,128)(2,1)S(1)}, u32[]{:S(2)}, u32[]{:S(2)}) collective-permute-start(bf16[384,128]{1,0:T(8,128)(2,1)S(1)} %get-tuple-element.34), channel_id=1, source_target_pairs={{0,3},{1,2},{2,1},{3,0},{4,7},{5,6},{6,5},{7,4},{8,11},{9,10},{10,... | collective-permute-start | bytes 294920 | tf_op jit(solution)/shard_map/ppermute | solution.py:435
  28.9 4.5 %copy-start.2 = (f32[16,8,64]{2,1,0:T(8,128)S(1)}, f32[16,8,64]{2,1,0:T(8,128)}, u32[]{:S(2)}) copy-start(f32[16,8,64]{2,1,0:T(8,128)} %x_ref.3) | copy-start | bytes 98308
  28.9 5.4 %collective-permute-start.7 = (bf16[128,128]{1,0:T(8,128)(2,1)S(1)}, bf16[128,128]{1,0:T(8,128)(2,1)S(1)}, u32[]{:S(2)}, u32[]{:S(2)}) collective-permute-start(bf16[128,128]{1,0:T(8,128)(2,1)S(1)} %get-tuple-element.37), channel_id=1, source_target_pairs={{0,4},{4,0},{8,12},{12,8},{1,5},{5,1},{9,13},{13,9},{2,6},{6,2},{1... | collective-permute-start | bytes 98312 | tf_op jit(solution)/shard_map/ppermute | solution.py:435
  29.1 5.4 %collective-permute-start.8 = (bf16[128,128]{1,0:T(8,128)(2,1)S(1)}, bf16[128,128]{1,0:T(8,128)(2,1)S(1)}, u32[]{:S(2)}, u32[]{:S(2)}) collective-permute-start(bf16[128,128]{1,0:T(8,128)(2,1)S(1)} %get-tuple-element.38), channel_id=1, source_target_pairs={{0,8},{4,12},{8,0},{12,4},{1,9},{5,13},{9,1},{13,5},{2,10},{6,14},... | collective-permute-start | bytes 98312 | tf_op jit(solution)/shard_map/ppermute | solution.py:435
  32.3 5.7 %collective-permute-start.9 = (bf16[128,128]{1,0:T(8,128)(2,1)S(1)}, bf16[128,128]{1,0:T(8,128)(2,1)S(1)}, u32[]{:S(2)}, u32[]{:S(2)}) collective-permute-start(bf16[128,128]{1,0:T(8,128)(2,1)S(1)} %get-tuple-element.39), channel_id=1, source_target_pairs={{0,12},{4,8},{8,4},{12,0},{1,13},{5,9},{9,5},{13,1},{2,14},{6,10},... | collective-permute-start | bytes 98312 | tf_op jit(solution)/shard_map/ppermute | solution.py:435

commit v4 on v3

v4 whole, which is shorter than its diff:
```python
import functools

import jax
import jax.numpy as jnp
from jax import lax
from jax.experimental import pallas as pl
from jax.experimental.pallas import tpu as pltpu
from jax.sharding import PartitionSpec as P


def layernorm_parts(alignment_features, affine_factor, affine_offset):
    centered_alignment = alignment_features - jnp.mean(alignment_features, axis=-1, keepdims=True)
    reciprocal_spread = lax.rsqrt(
        jnp.mean(centered_alignment * centered_alignment, axis=-1, keepdims=True) + 1e-05
    )
    zscored_alignment = centered_alignment * reciprocal_spread
    return (
        zscored_alignment,
        reciprocal_spread,
        (zscored_alignment * affine_factor + affine_offset).astype(jnp.bfloat16),
    )


def local_general(
    alignment_features,
    affine_factor,
    affine_offset,
    first_projector,
    second_projector,
    final_projector,
    additive_term,
    adjoint_update,
):
    zscored_alignment, reciprocal_spread, unit_alignment = layernorm_parts(
        alignment_features, affine_factor, affine_offset
    )
    first_factor_here = jnp.dot(
        unit_alignment, first_projector, preferred_element_type=jnp.float32
    ).astype(jnp.bfloat16)
    second_factor_here = jnp.dot(
        unit_alignment, second_projector, preferred_element_type=jnp.float32
    ).astype(jnp.bfloat16)
    tokens, quarter, chans = first_factor_here.shape
    left_flat = first_factor_here.reshape(tokens, quarter * chans)
    right_flat = second_factor_here.reshape(tokens, quarter * chans)
    left_wide, right_wide = (
        lax.all_gather(left_flat, "cols", axis=1, tiled=True),
        lax.all_gather(right_flat, "cols", axis=1, tiled=True),
    )
    left_rows = left_wide.reshape(tokens, -1, chans)
    right_all = lax.all_gather(right_wide, "rows", axis=0, tiled=True)
    block = right_all.shape[0] // lax.axis_size("cols")
    right_cols = lax.dynamic_slice_in_dim(
        right_all, lax.axis_index("cols") * block, block, 0
    ).reshape(block, -1, chans)
    seqs = left_rows.shape[1]
    multiplier = 1.0 / seqs
    pair_ch = adjoint_update.shape[2]
    step_rows = 4
    rounds = tokens // step_rows
    first_tile_list = left_rows.reshape(rounds, step_rows, seqs, chans)
    cot_blocks = adjoint_update.reshape(rounds, step_rows, block, pair_ch)

    def advance(carry, inputs):
        right_acc, out_acc = carry
        left_slab, cot_slab = inputs
        outer = (
            jnp.einsum("isc,jsd->ijcd", left_slab, right_cols, preferred_element_type=jnp.float32)
            * multiplier
        ).astype(jnp.bfloat16)
        flat = outer.reshape(step_rows * block, chans * chans)
        cot_flat = cot_slab.reshape(step_rows * block, pair_ch)
        update = (
            jnp.dot(flat, final_projector, preferred_element_type=jnp.float32) + additive_term
        ).astype(jnp.bfloat16)
        outer_grad = jnp.dot(
            cot_flat, final_projector.T, preferred_element_type=jnp.float32
        ).astype(jnp.bfloat16)
        outer_grad = outer_grad.reshape(step_rows, block, chans, chans)
        left_piece = (
            jnp.einsum("ijcd,jsd->isc", outer_grad, right_cols, preferred_element_type=jnp.float32)
            * multiplier
        )
        right_acc = (
            right_acc
            + jnp.einsum("ijcd,isc->jsd", outer_grad, left_slab, preferred_element_type=jnp.float32)
            * multiplier
        )
        out_acc = out_acc + jnp.einsum(
            "fk,fe->ke", flat, cot_flat, preferred_element_type=jnp.float32
        )
        return ((right_acc, out_acc), (update.reshape(step_rows, block, pair_ch), left_piece))

    beginning_position = (
        jnp.zeros((block, seqs, chans), jnp.float32),
        jnp.zeros((chans * chans, pair_ch), jnp.float32),
    )
    (right_part, out_term), (updates, left_pieces) = lax.scan(
        advance, beginning_position, (first_tile_list, cot_blocks)
    )
    residue_update = updates.reshape(tokens, block, pair_ch)
    left_part = left_pieces.reshape(tokens, seqs * chans)
    first_adjoint = lax.psum_scatter(left_part, "cols", scatter_dimension=1, tiled=True).reshape(
        tokens, quarter, chans
    )
    moved = lax.all_to_all(
        right_part.reshape(block, seqs * chans), "cols", split_axis=1, concat_axis=0, tiled=True
    )
    right_back = lax.psum_scatter(moved, "rows", scatter_dimension=0, tiled=True).reshape(
        tokens, quarter, chans
    )
    final_projector_slope = lax.psum_scatter(
        out_term, ("rows", "cols"), scatter_dimension=0, tiled=True
    )
    unit_broadcast = unit_alignment.astype(jnp.float32)
    high = lax.Precision.HIGHEST
    left_term = jnp.einsum("tsk,tsc->kc", unit_broadcast, first_adjoint, precision=high)
    right_term = jnp.einsum("tsk,tsc->kc", unit_broadcast, right_back, precision=high)
    first_projector_slope, second_projector_slope = lax.psum(
        (left_term, right_term), ("rows", "cols")
    )
    unit_adjoint = jnp.einsum(
        "tsc,kc->tsk", first_adjoint, first_projector.astype(jnp.float32), precision=high
    )
    unit_adjoint = unit_adjoint + jnp.einsum(
        "tsc,kc->tsk", right_back, second_projector.astype(jnp.float32), precision=high
    )
    scaled_alignment = unit_adjoint * affine_factor
    alignment_slope = reciprocal_spread * (
        scaled_alignment
        - jnp.mean(scaled_alignment, axis=-1, keepdims=True)
        - zscored_alignment * jnp.mean(scaled_alignment * zscored_alignment, axis=-1, keepdims=True)
    )
    return (
        residue_update,
        alignment_slope,
        final_projector_slope,
        first_projector_slope,
        second_projector_slope,
    )


F32, BF16 = jnp.float32, jnp.bfloat16
LANES, SUBLANES = 128, 8


def dot(a, b, at=1, bt=0):
    return lax.dot_general(a, b, (((at,), (bt,)), ((), ())), preferred_element_type=F32)


def lane_group(shape, size):
    return lax.broadcasted_iota(jnp.int32, shape, len(shape) - 1) // size


def pick(parts, group):
    out = parts[-1]
    for b in range(len(parts) - 2, -1, -1):
        out = jnp.where(group == b, parts[b], out)
    return out


def normalise(x):
    centered = x - jnp.mean(x, axis=-1, keepdims=True)
    spread = lax.rsqrt(jnp.mean(centered * centered, axis=-1, keepdims=True) + 1e-05)
    return centered * spread, spread


def call(kernel, out_shape, scratch=(), flops=0, space=pltpu.VMEM):
    place = pl.BlockSpec(memory_space=space)
    on_chip = pl.BlockSpec(memory_space=pltpu.VMEM)

    def run(*args):
        return pl.pallas_call(
            kernel,
            out_shape=out_shape,
            in_specs=[place] * len(args),
            out_specs=jax.tree.map(lambda _: on_chip, out_shape),
            scratch_shapes=list(scratch),
            cost_estimate=pl.CostEstimate(flops=flops, bytes_accessed=0, transcendentals=0),
            compiler_params=pltpu.CompilerParams(vmem_limit_bytes=16 * 2**20),
        )(*args)

    return run


def norm_kernel(*refs):
    x_ref, offset_ref, sems = refs[-3:]
    count = sems.shape[0]
    sources, (out_ref, xhat_ref, spread_ref) = refs[:count], refs[count : count + 3]
    kept = (x_ref, offset_ref) + refs[count + 3 : -3]
    copies = [
        pltpu.make_async_copy(source, ref, sems.at[n])
        for n, (source, ref) in enumerate(zip(sources, kept))
    ]
    for copy in copies:
        copy.start()
    for copy in copies[:3]:
        copy.wait()
    tokens, quarter, width = x_ref.shape
    xhat, spread = normalise(x_ref[...].reshape(tokens * quarter, width))
    xhat_ref[...] = xhat
    spread_ref[...] = jnp.broadcast_to(spread, xhat.shape)
    unit = xhat * kept[2][...] + offset_ref[...]
    half = tokens * quarter // 2
    out_ref[...] = jnp.concatenate([unit[:half], unit[half:]], axis=1).astype(BF16)
    for copy in copies[3:]:
        copy.wait()


def grad_kernel(
    cot_ref, final_ref, first_ref, second_ref,
    by_col_ref, by_row_ref, cot_cols_ref, weight_ref, order_ref,
    cot_f, final_f,
    *, chans,
):
    tokens, block, _ = cot_ref.shape
    steps = by_col_ref.shape[0] // tokens
    per = LANES // chans
    cot = cot_ref[...]
    final = final_ref[...]
    cot_f[...] = cot.astype(F32)
    final_f[...] = final.astype(F32)
    for j in range(block):
        cot_cols_ref[j * tokens : (j + 1) * tokens, :] = cot_f[:, j, :].astype(BF16)
    cot_cols = cot_cols_ref[...]
    cot_rows = cot.reshape(tokens * block, cot.shape[2])
    for a in range(steps):
        got = dot(cot_cols, final[a * LANES : (a + 1) * LANES], 1, 1).astype(BF16)
        for j in range(block):
            by_col_ref[a * tokens : (a + 1) * tokens, j * LANES : (j + 1) * LANES] = got[
                j * tokens : (j + 1) * tokens
            ]
        lanes_dc = jnp.concatenate(
            [final_f[pl.ds(a * per + b, chans, stride=chans), :] for b in range(per)], axis=0
        ).astype(BF16)
        got = dot(cot_rows, lanes_dc, 1, 1).astype(BF16)
        for i in range(tokens):
            by_row_ref[a * block : (a + 1) * block, i * LANES : (i + 1) * LANES] = got[
                i * block : (i + 1) * block
            ]
    for x, ref in enumerate((first_ref, second_ref)):
        projector = ref[...]
        zero = jnp.zeros_like(projector)
        halves = [
            jnp.concatenate([projector, zero], axis=1),
            jnp.concatenate([zero, projector], axis=1),
        ]
        empty = jnp.concatenate([zero, zero], axis=1)
        for b in range(per):
            for h in range(2):
                for other in range(per):
                    at = (((x * 2) + h) * per + other) * chans
                    weight_ref[b, at : at + chans, :] = halves[h] if other == b else empty
    size = tokens * chans
    for b in range(per):
        row = lax.broadcasted_iota(jnp.int32, (size, LANES), 0)
        lane = lax.broadcasted_iota(jnp.int32, (size, LANES), 1)
        wanted = lane % tokens * chans + lane // tokens * per + b
        order_ref[:, b * LANES : (b + 1) * LANES] = jnp.where(row == wanted, 1.0, 0.0).astype(BF16)


def joint_kernel(n0, n1, n2, n3, out_ref, unit_f):
    blocks = (n0, n1, n2, n3)
    mine = lax.axis_index("cols")
    half, seqs, lanes = unit_f.shape
    quarter = seqs // len(blocks)
    for k, ref in enumerate(blocks):
        at = pl.multiple_of((mine ^ k) * quarter, quarter)
        unit_f[:, pl.ds(at, quarter), :] = ref[...].astype(F32).reshape(half, quarter, lanes)
    out_ref[...] = unit_f[...].reshape(half * seqs, lanes).astype(BF16)


def project(unit, weight_ref, x, seqs, per):
    half = unit.shape[0] // seqs
    by_group = unit.reshape(half // per, per, seqs, unit.shape[1])
    size = weight_ref.shape[1] // 2
    total = None
    for b in range(per):
        part = by_group[:, b].reshape(half // per * seqs, unit.shape[1])
        got = dot(part, weight_ref[b, x * size : (x + 1) * size, :], 1, 1)
        total = got if total is None else total + got
    total = total.astype(BF16)
    count = half // per
    return [
        total[p % count * seqs : (p % count + 1) * seqs, p // count * LANES : (p // count + 1) * LANES]
        for p in range(2 * count)
    ]


def reorder(tiles, order_ref):
    wide = dot(jnp.concatenate(tiles, axis=1), order_ref[...])
    count = wide.shape[1] // LANES
    return jnp.concatenate([wide[:, b * LANES : (b + 1) * LANES] for b in range(count)], axis=0)


def fold(spread_ref, seqs, chans, tokens):
    per = LANES // chans
    group = lane_group((seqs, LANES), chans)
    out = []
    for p in range(tokens // per):
        total = None
        for shift in range(per):
            parts = []
            for b in range(per):
                t = p * per + (b + shift) % per
                parts.append(spread_ref[b * seqs : (b + 1) * seqs, t * LANES : (t + 1) * LANES])
            part = pick(parts, group)
            if shift:
                part = pltpu.roll(part, shift * chans, 1)
            total = part if total is None else total + part
        out.append(total)
    return out


def slope(unit_turned, tiles, per, chans):
    seqs = tiles[0].shape[0]
    count = len(tiles) // 2
    group = lane_group((seqs, LANES), chans)
    rows = []
    for p in range(count):
        for b in range(per):
            rows.append(
                jnp.concatenate(
                    [jnp.where(group == b, tiles[h * count + p], 0.0) for h in range(2)], axis=1
                )
            )
    got = dot(unit_turned, jnp.concatenate(rows, axis=0).astype(BF16))
    width = unit_turned.shape[0] // 2
    return got[:width, :LANES] + got[width:, LANES:]


def left_kernel(
    unit_ref, weight_ref, order_ref, by_col_ref, left_ref, turned_ref, part_ref, spread_f, *, chans, seqs
):
    per = LANES // chans
    tokens = unit_ref.shape[0] // seqs * 2
    unit = unit_ref[...]
    turned_ref[...] = unit.astype(F32).T.astype(BF16)
    turned = reorder(project(unit, weight_ref, 0, seqs, per), order_ref)
    left_ref[...] = turned.T.astype(BF16)
    spread_f[...] = dot(turned.astype(BF16), by_col_ref[...])
    for p, tile in enumerate(fold(spread_f, seqs, chans, tokens)):
        part_ref[p] = tile * (1.0 / seqs)


def pair_kernel(
    unit_ref, left_ref, turned_ref, part_ref, weight_ref, order_ref, by_row_ref, cot_cols_ref,
    outer_ref, own_ref, m1, m2, m3,
    block_ref, slope_f, spread_f, both_f,
    *, chans, seqs, sizes,
):
    per, steps = LANES // chans, chans // (LANES // chans)
    rows, cols = sizes
    tokens = unit_ref.shape[0] // seqs * 2
    groups = tokens // per
    quarter = seqs // cols
    share = slope_f.shape[0] // (rows * cols)
    mine = lax.axis_index("cols")
    group = lane_group((seqs, LANES), chans)
    unit = unit_ref[...]
    right = project(unit, weight_ref, 1, seqs, per)
    for p, tile in enumerate(right):
        tile = tile.astype(F32)
        rolled = [pltpu.roll(tile, s * chans, 1) if s else tile for s in range(per)]
        for own in range(per):
            j = p * per + own
            for b in range(per):
                block_ref[b * seqs : (b + 1) * seqs, j * LANES : (j + 1) * LANES] = jnp.where(
                    group == b, rolled[(b - own) % per], 0.0
                ).astype(BF16)
    left = left_ref[...]
    for p in range(groups):
        span = per * LANES
        got = dot(left, block_ref[:, p * span : (p + 1) * span])
        got = (got * (1.0 / seqs)).astype(BF16)
        for own in range(per):
            j = p * per + own
            for a in range(steps):
                outer_ref[j * tokens : (j + 1) * tokens, a * LANES : (a + 1) * LANES] = got[
                    a * tokens : (a + 1) * tokens, own * LANES : (own + 1) * LANES
                ]
    spread_f[...] = dot(reorder(right, order_ref).astype(BF16), by_row_ref[...])
    slope_f[...] = dot(outer_ref[...], cot_cols_ref[...], 0, 0)
    lefts = [tile * (1.0 / seqs) for tile in fold(spread_f, seqs, chans, tokens)]
    rights = [part_ref[p] for p in range(groups)]
    for p in range(groups):
        both_f[p, 0] = lefts[p]
        both_f[p, 1] = rights[p]
    sides = [
        slope(turned_ref[...], lefts, per, chans),
        slope(unit.astype(F32).T.astype(BF16), rights, per, chans),
    ]
    width = sides[0].shape[0]
    sides = [s + pltpu.roll(s, LANES // 2, 1) for s in sides]
    slopes = jnp.where(lane_group((width, LANES), LANES // 2) == 0, sides[0], sides[1])
    for k, ref in enumerate((own_ref, m1, m2, m3)):
        peer = mine ^ k
        kind = ref.dtype
        for r in range(rows):
            at = pl.multiple_of((r * cols + peer) * share, share)
            ref[r * share : (r + 1) * share, :] = slope_f[pl.ds(at, share), :].astype(kind)
        base = rows * share
        at = pl.multiple_of(peer * quarter, quarter)
        span = groups * quarter
        for x in range(2):
            ref[base + x * span : base + (x + 1) * span, :] = (
                both_f[:, x, pl.ds(at, quarter), :].reshape(span, LANES).astype(kind)
            )
        base += 2 * span
        ref[base : base + width, :] = slopes.astype(kind)


def update_kernel(outer_ref, final_ref, bias_ref, update_ref, update_f):
    tokens = update_ref.shape[0]
    update = dot(outer_ref[...], final_ref[...]) + bias_ref[...]
    for j in range(update_ref.shape[1]):
        update_f[:, j, :] = update[j * tokens : (j + 1) * tokens]
    update_ref[...] = update_f[...].astype(BF16)


def between_kernel(
    own_ref, r1, r2, r3, left_ref, next_ref, m1, m2, m3, total_f, right_f, *, rows, share
):
    refs = (own_ref, r1, r2, r3)
    span = left_ref.shape[0]
    first = rows * share
    last = first + 2 * span
    mine, column = lax.axis_index("rows"), lax.axis_index("cols")
    for k, ref in enumerate(refs):
        right_f[column ^ k] = ref[first + span : last, :].astype(F32)
    for start, stop in ((0, first + span), (last, total_f.shape[0])):
        total = own_ref[start:stop, :]
        for ref in refs[1:]:
            total = total + ref[start:stop, :].astype(F32)
        total_f[start:stop, :] = total
    left_ref[...] = total_f[first : first + span, :]
    slopes = total_f[last:, :]
    for k, ref in enumerate((next_ref, m1, m2, m3)):
        peer = mine ^ k
        at = pl.multiple_of(peer * share, share)
        ref[0:share, :] = total_f[pl.ds(at, share), :].astype(ref.dtype)
        ref[share : share + span, :] = right_f[peer].astype(ref.dtype)
        ref[share + span :, :] = slopes.astype(ref.dtype)


def to_unit(back, projector_ref, unit_ref, quarter):
    back = back[...]
    projector = projector_ref[...]
    chans = projector.shape[0]
    high = back.astype(BF16)
    low = (back - high.astype(F32)).astype(BF16)
    zero = jnp.zeros_like(projector)
    per = LANES // chans
    for b in range(per):
        weights = jnp.concatenate([projector if i == b else zero for i in range(per)], axis=0)
        got = dot(high, weights) + dot(low, weights)
        for p in range(back.shape[0] // quarter):
            unit_ref[p * per + b] = got[p * quarter : (p + 1) * quarter]


def last_kernel(
    own_ref, r1, r2, r3, unit_ref, xhat_ref, spread_ref, gain_ref, second_ref,
    final_ref, first_slope_ref, second_slope_ref, out_ref, unit_f,
):
    total = own_ref[...] + r1[...].astype(F32) + r2[...].astype(F32) + r3[...].astype(F32)
    share = final_ref.shape[0]
    final_ref[...] = total[:share]
    tokens, quarter, width = out_ref.shape
    span = tokens * quarter * second_ref.shape[0] // LANES
    to_unit(total[share : share + span], second_ref, unit_f, quarter)
    g = (unit_ref[...] + unit_f[...]).reshape(tokens * quarter, width) * gain_ref[...]
    xhat = xhat_ref[...]
    out = spread_ref[...] * (
        g
        - jnp.mean(g, axis=-1, keepdims=True)
        - xhat * jnp.mean(g * xhat, axis=-1, keepdims=True)
    )
    out_ref[...] = out.reshape(tokens, quarter, width)
    slopes = total[share + span :].T
    chans = second_ref.shape[0]
    for x, ref in enumerate((first_slope_ref, second_slope_ref)):
        side = slopes[x * LANES // 2 : (x + 1) * LANES // 2]
        out = side[:chans]
        for b in range(1, LANES // 2 // chans):
            out = out + side[b * chans : (b + 1) * chans]
        ref[...] = out


def exchange(messages, axis):
    size = lax.axis_size(axis)
    return [
        lax.ppermute(m, axis, [(p, p ^ k) for p in range(size)])
        for k, m in enumerate(messages, 1)
    ]


def local_square(
    alignment_features,
    affine_factor,
    affine_offset,
    first_projector,
    second_projector,
    final_projector,
    additive_term,
    adjoint_update,
):
    rows, cols = lax.axis_size("rows"), lax.axis_size("cols")
    tokens, quarter, width = alignment_features.shape
    chans = first_projector.shape[1]
    total, pair_ch = final_projector.shape
    seqs = quarter * cols
    per, steps = LANES // chans, chans // (LANES // chans)
    share = total // (rows * cols)
    flip = [(r * cols + q, q * cols + r) for r in range(rows) for q in range(cols)]
    shape = jax.ShapeDtypeStruct
    wide, tall = tokens * LANES, steps * tokens
    groups = tokens // per
    half = tokens // 2
    aligned = shape((tokens, quarter, width), F32)
    flat = shape((tokens * quarter, width), F32)
    inputs = [
        alignment_features,
        affine_offset.reshape(1, width),
        affine_factor.reshape(1, width),
        adjoint_update,
        final_projector,
        first_projector.T,
        second_projector.T,
        additive_term.reshape(1, pair_ch),
    ]
    unit, xhat, spread, gain, cot, final, first, second, bias = call(
        norm_kernel,
        [shape((half * quarter, 2 * width), BF16), flat, flat]
        + [shape(i.shape, i.dtype) for i in inputs[2:]],
        [pltpu.VMEM(i.shape, i.dtype) for i in inputs[:2]]
        + [pltpu.SemaphoreType.DMA((len(inputs),))],
        space=pltpu.HBM,
    )(*[pltpu.with_memory_space_constraint(i, pltpu.HBM) for i in inputs])
    units = [unit] + exchange([unit] * (cols - 1), "cols")
    by_col, by_row, cot_cols, weight, order = call(
        functools.partial(grad_kernel, chans=chans),
        (
            shape((tall, wide), BF16),
            shape((tall, wide), BF16),
            shape((tokens * tokens, pair_ch), BF16),
            shape((per, 4 * LANES, 2 * width), BF16),
            shape((tokens * chans, per * LANES), BF16),
        ),
        [pltpu.VMEM(adjoint_update.shape, F32), pltpu.VMEM((total, pair_ch), F32)],
        flops=8 * tokens * tokens * total * pair_ch,
    )(cot, final, first, second)
    unit_rows = call(
        joint_kernel,
        shape((half * seqs, 2 * width), BF16),
        [pltpu.VMEM((half, seqs, 2 * width), F32)],
    )(*units)
    unit_cols = lax.ppermute(unit_rows, ("rows", "cols"), flip)
    left, turned, part = call(
        functools.partial(left_kernel, chans=chans, seqs=seqs),
        (
            shape((tall, LANES), BF16),
            shape((2 * width, half * seqs), BF16),
            shape((groups, seqs, LANES), F32),
        ),
        [pltpu.VMEM((LANES, wide), F32)],
        flops=10**8,
    )(unit_rows, weight, order, by_col)
    span = groups * quarter
    message = rows * share + 2 * span + width
    outer, own, *messages = call(
        functools.partial(pair_kernel, chans=chans, seqs=seqs, sizes=(rows, cols)),
        (
            shape((tokens * tokens, total), BF16),
            shape((message, LANES), F32),
            *[shape((message, LANES), BF16)] * (cols - 1),
        ),
        [
            pltpu.VMEM((LANES, wide), BF16),
            pltpu.VMEM((total, pair_ch), F32),
            pltpu.VMEM((LANES, wide), F32),
            pltpu.VMEM((groups, 2, seqs, LANES), F32),
        ],
    )(unit_cols, left, turned, part, weight, order, by_row, cot_cols)
    got = exchange(messages, "cols")
    update = call(
        update_kernel,
        shape((tokens, tokens, pair_ch), BF16),
        [pltpu.VMEM((tokens, tokens, pair_ch), F32)],
        flops=10**8,
    )(outer, final, bias)
    message = share + span + width
    back, own, *messages = call(
        functools.partial(between_kernel, rows=rows, share=share),
        (
            shape((span, LANES), F32),
            shape((message, LANES), F32),
            *[shape((message, LANES), BF16)] * (rows - 1),
        ),
        [
            pltpu.VMEM((rows * share + 2 * span + width, LANES), F32),
            pltpu.VMEM((cols, span, LANES), F32),
        ],
    )(own, *got)
    got = exchange(messages, "rows")
    from_left = call(functools.partial(to_unit, quarter=quarter), aligned, flops=10**8)(back, first)
    final_slope, first_slope, second_slope, alignment_slope = call(
        last_kernel,
        (
            shape((share, pair_ch), F32),
            shape((chans, width), F32),
            shape((chans, width), F32),
            aligned,
        ),
        [pltpu.VMEM((tokens, quarter, width), F32)],
    )(own, *got, from_left, xhat, spread, gain, second)
    return update, alignment_slope, final_slope, first_slope.T, second_slope.T


def fits(mesh, alignment_features, first_projector, final_projector):
    rows, cols = mesh.shape["rows"], mesh.shape["cols"]
    tokens = alignment_features.shape[0] // (mesh.shape["groups"] * rows)
    quarter = alignment_features.shape[1] // cols
    width, chans = first_projector.shape
    per = LANES // chans
    return (
        rows == cols == 4
        and chans * per == LANES
        and chans % per == 0
        and chans // per == SUBLANES
        and 2 * width == LANES
        and final_projector.shape[1] == LANES
        and quarter == SUBLANES
        and tokens % (2 * SUBLANES) == 0
        and quarter * cols == chans
        and chans // per * tokens == LANES
    )


def solution(mesh):
    in_specs = (
        P(("groups", "rows"), "cols", None),
        P(),
        P(),
        P(),
        P(),
        P(),
        P(),
        P(("groups", "rows"), "cols", None),
    )
    out_specs = (
        P(("groups", "rows"), "cols", None),
        P(("groups", "rows"), "cols", None),
        P(("groups", "rows", "cols"), None),
        P("groups", None),
        P("groups", None),
    )

    def whole(*args):
        square = fits(mesh, args[0], args[3], args[5])
        return jax.shard_map(
            local_square if square else local_general,
            mesh=mesh,
            in_specs=in_specs,
            out_specs=out_specs,
            check_vma=False,
        )(*args)

    return whole
```

time: 38.9 us -> 36 us (0.925)
  local copies, waits for them, and re-layouts: 3.11 us -> 0 us
  starting transfers between devices: 19.3 us -> 16.3 us
  waiting for transfers between devices: 10.3 us -> 12.5 us
  Pallas kernels: 5.24 us -> 6.37 us
    unnamed x18 -> x0, local copies, waits for them, and re-layouts: 3.11 us -> none
    ppermute x9, starting transfers between devices: 18.7 us -> 15.6 us  [exchange(): lax.ppermute(m, axis, [(p, p ^ k) for p in range(size)])]
    ppermute x9, waiting for transfers between devices: 10.3 us -> 12.5 us  [exchange(): lax.ppermute(m, axis, [(p, p ^ k) for p in range(size)])]
    pallas_call x7 -> x9, Pallas kernels: 5.24 us -> 6.37 us  [run(): pl.pallas_call(kernel, out_shape=out_shape, in_specs=[place] * len(args),...]
  transfers between devices with their start and end apart: 10 -> 10, of which waited for: 5 -> 6; matrix products, arithmetic and copies ran while one was open for 0% -> 0% of each run, Pallas kernels for 4% -> 8%
where the time goes in v4:
time: 36 us; the launch traced here: 35.9 us
  starting transfers between devices  16.3 us (45%)
  waiting for transfers between devices  12.5 us (35%)
  Pallas kernels  6.37 us (18%)
  between operations  0.7 us (2%)
    ppermute x9, starting transfers between devices, exchange(): lax.ppermute(m, axis, [(p, p ^ k) for p in range(size)])  15.6 us
    ppermute x9, waiting for transfers between devices, exchange(): lax.ppermute(m, axis, [(p, p ^ k) for p in range(size)])  12.5 us
    pallas_call x9, Pallas kernels, run(): pl.pallas_call(kernel, out_shape=out_shape, in_specs=[place] * len(args),...  6.37 us
  transfers between devices with their start and end apart: 10, of which 6 were waited for; matrix products, arithmetic and copies ran while one was open for 0% of the time, Pallas kernels for 8%

profile of v4, /device:TPU:0, one launch (start us, length us, event | category | flops | bytes accessed | tf_op | source)
XLA Modules:
  0.0 35.9 jit_solution(7065935238570357906)
XLA Ops:
  0.6 1.2 %shard_map.119 = (bf16[64,128]{1,0:T(8,128)(2,1)S(1)}, f32[128,64]{1,0:T(8,128)S(1)}, f32[128,64]{1,0:T(8,128)S(1)}, f32[1,64]{1,0:T(1,128)S(1)}, bf16[16,16,128...) custom-call(f32[16,8,64]{2,1,0:T(8,128)} %refs_0_.1, ...), custom_call_target="tpu_custom_call" | custom-call | tf_op jit(solution)/shard_map/pallas_call | solution.py:173
  1.8 2.5 %collective-permute-start.2 = (bf16[64,128]{1,0:T(8,128)(2,1)S(1)}, bf16[64,128]{1,0:T(8,128)(2,1)S(1)}, u32[]{:S(2)}, u32[]{:S(2)}) collective-permute-start(bf16[64,128]{1,0:T(8,128)(2,1)S(1)} %get-tuple-element.36.n0), channel_id=1, source_target_pairs={{0,3},{1,2},{2,1},{3,0},{4,7},{5,6},{6,5},{7,4},{8,11},{9,10},{10,... | collective-permute-start | bytes 49160 | tf_op jit(solution)/shard_map/ppermute | solution.py:492
  4.3 0.6 %collective-permute-start.1 = (bf16[64,128]{1,0:T(8,128)(2,1)S(1)}, bf16[64,128]{1,0:T(8,128)(2,1)S(1)}, u32[]{:S(2)}, u32[]{:S(2)}) collective-permute-start(bf16[64,128]{1,0:T(8,128)(2,1)S(1)} %get-tuple-element.36.n0), channel_id=1, source_target_pairs={{0,2},{1,3},{2,0},{3,1},{4,6},{5,7},{6,4},{7,5},{8,10},{9,11},{10,... | collective-permute-start | bytes 49160 | tf_op jit(solution)/shard_map/ppermute | solution.py:492
  4.9 0.0 collective-permute-start
  5.0 0.8 %collective-permute-done.2.n3 = bf16[64,128]{1,0:T(8,128)(2,1)S(1)} collective-permute-done((bf16[64,128]{1,0:T(8,128)(2,1)S(1)}, bf16[64,128]{1,0:T(8,128)(2,1)S(1)}, u32[]{:S(2)}, u32[]{:S(2)}) %collective-permute-start.2) | collective-permute-done | bytes 16416 | tf_op jit(solution)/shard_map/ppermute | solution.py:492
  5.7 2.3 %collective-permute-done.1.n2 = bf16[64,128]{1,0:T(8,128)(2,1)S(1)} collective-permute-done((bf16[64,128]{1,0:T(8,128)(2,1)S(1)}, bf16[64,128]{1,0:T(8,128)(2,1)S(1)}, u32[]{:S(2)}, u32[]{:S(2)}) %collective-permute-start.1) | collective-permute-done | bytes 16416 | tf_op jit(solution)/shard_map/ppermute | solution.py:492
  8.0 0.0 collective-permute-done.n1
  8.1 0.7 %collective-permute-start.3 = (bf16[256,128]{1,0:T(8,128)(2,1)S(1)}, bf16[256,128]{1,0:T(8,128)(2,1)S(1)}, u32[]{:S(2)}, u32[]{:S(2)}) collective-permute-start(bf16[256,128]{1,0:T(8,128)(2,1)S(1)} %shard_map.120.unit_ref), channel_id=1, source_target_pairs={{0,0},{1,4},{2,8},{3,12},{4,1},{5,5},{6,9},{7,13},{8,2},{9,6},{10,... | collective-permute-start | bytes 196616 | tf_op jit(solution)/shard_map/ppermute | solution.py:557
  8.7 0.9 %shard_map.121 = (bf16[128,2048]{1,0:T(8,128)(2,1)S(1)}, bf16[128,2048]{1,0:T(8,128)(2,1)S(1)}, bf16[256,128]{1,0:T(8,128)(2,1)S(1)}, bf16[4,512,128]{2,1,0:T(8,128)(2,1)S(1)}, bf16[512,512]{1,0:T(8,128)(2,1)S(1)}) custom-call(bf16[16,16,128]{2,1,0:T(8,128)(2,1)S(1)} %get-tuple-element.37.cot_ref, bf16[1024,128]{1,0:T(8,128)(2,1)S(1)} %get-tuple-element.38.final_ref, ...), custom_call_target="tpu_custom_call" | custom-call | flops 268435456 | tf_op jit(solution)/shard_map/pallas_call | solution.py:173
  9.6 0.8 %shard_map.122 = (bf16[128,128]{1,0:T(8,128)(2,1)S(1)}, bf16[128,256]{1,0:T(8,128)(2,1)S(1)}, f32[4,32,128]{2,1,0:T(8,128)S(1)}) custom-call(bf16[256,128]{1,0:T(8,128)(2,1)S(1)} %shard_map.120.unit_ref, bf16[4,512,128]{2,1,0:T(8,128)(2,1)S(1)} %get-tuple-element.41.weight_ref, bf16[512,512]{1,0:T(8,128)(2,1)S(1)} %get-tuple-element.42.order_ref, ...), custom_call_target="tpu_custom_call" | custom-call | flops 100000000 | tf_op jit(solution)/shard_map/pallas_call | solution.py:173
  10.4 0.0 collective-permute-done.3.unit_ref
  10.4 1.4 %shard_map.123 = (bf16[256,1024]{1,0:T(8,128)(2,1)S(1)}, f32[384,128]{1,0:T(8,128)S(1)}, bf16[384,128]{1,0:T(8,128)(2,1)S(1)}, bf16[384,128]{1,0:T(8,128)(2,1)S(1)}, bf16[384,128]{1,0:T(8,128)(2,1)S(1)}) custom-call(bf16[256,128]{1,0:T(8,128)(2,1)S(1)} %collective-permute-done.3.unit_ref, bf16[128,128]{1,0:T(8,128)(2,1)S(1)} %get-tuple-element.44.left_ref, ...), custom_call_target="tpu_custom_call" | custom-call | tf_op jit(solution)/shard_map/pallas_call | solution.py:173
  11.9 3.2 %collective-permute-start.4 = (bf16[384,128]{1,0:T(8,128)(2,1)S(1)}, bf16[384,128]{1,0:T(8,128)(2,1)S(1)}, u32[]{:S(2)}, u32[]{:S(2)}) collective-permute-start(bf16[384,128]{1,0:T(8,128)(2,1)S(1)} %get-tuple-element.52), channel_id=1, source_target_pairs={{0,1},{1,0},{2,3},{3,2},{4,5},{5,4},{6,7},{7,6},{8,9},{9,8},{10,11... | collective-permute-start | bytes 294920 | tf_op jit(solution)/shard_map/ppermute | solution.py:492
  15.1 4.8 %collective-permute-start.5 = (bf16[384,128]{1,0:T(8,128)(2,1)S(1)}, bf16[384,128]{1,0:T(8,128)(2,1)S(1)}, u32[]{:S(2)}, u32[]{:S(2)}) collective-permute-start(bf16[384,128]{1,0:T(8,128)(2,1)S(1)} %get-tuple-element.53), channel_id=1, source_target_pairs={{0,2},{1,3},{2,0},{3,1},{4,6},{5,7},{6,4},{7,5},{8,10},{9,11},{10,... | collective-permute-start | bytes 294920 | tf_op jit(solution)/shard_map/ppermute | solution.py:492
  19.9 0.0 collective-permute-start.6
  19.9 0.0 collective-permute-done.4.r1
  19.9 3.6 %collective-permute-done.5.r2 = bf16[384,128]{1,0:T(8,128)(2,1)S(1)} collective-permute-done((bf16[384,128]{1,0:T(8,128)(2,1)S(1)}, bf16[384,128]{1,0:T(8,128)(2,1)S(1)}, u32[]{:S(2)}, u32[]{:S(2)}) %collective-permute-start.5) | collective-permute-done | bytes 98336 | tf_op jit(solution)/shard_map/ppermute | solution.py:492
  23.5 1.6 %collective-permute-done.6.r3 = bf16[384,128]{1,0:T(8,128)(2,1)S(1)} collective-permute-done((bf16[384,128]{1,0:T(8,128)(2,1)S(1)}, bf16[384,128]{1,0:T(8,128)(2,1)S(1)}, u32[]{:S(2)}, u32[]{:S(2)}) %collective-permute-start.6) | collective-permute-done | bytes 98336 | tf_op jit(solution)/shard_map/ppermute | solution.py:492
  25.1 0.1 shard_map.125
  25.2 0.4 %collective-permute-start.7 = (bf16[160,128]{1,0:T(8,128)(2,1)S(1)}, bf16[160,128]{1,0:T(8,128)(2,1)S(1)}, u32[]{:S(2)}, u32[]{:S(2)}) collective-permute-start(bf16[160,128]{1,0:T(8,128)(2,1)S(1)} %get-tuple-element.56), channel_id=1, source_target_pairs={{0,4},{4,0},{8,12},{12,8},{1,5},{5,1},{9,13},{13,9},{2,6},{6,2},{1... | collective-permute-start | bytes 122888 | tf_op jit(solution)/shard_map/ppermute | solution.py:492
  25.6 3.6 %collective-permute-start.8 = (bf16[160,128]{1,0:T(8,128)(2,1)S(1)}, bf16[160,128]{1,0:T(8,128)(2,1)S(1)}, u32[]{:S(2)}, u32[]{:S(2)}) collective-permute-start(bf16[160,128]{1,0:T(8,128)(2,1)S(1)} %get-tuple-element.57), channel_id=1, source_target_pairs={{0,8},{4,12},{8,0},{12,4},{1,9},{5,13},{9,1},{13,5},{2,10},{6,14},... | collective-permute-start | bytes 122888 | tf_op jit(solution)/shard_map/ppermute | solution.py:492
  29.2 0.4 %collective-permute-start.9 = (bf16[160,128]{1,0:T(8,128)(2,1)S(1)}, bf16[160,128]{1,0:T(8,128)(2,1)S(1)}, u32[]{:S(2)}, u32[]{:S(2)}) collective-permute-start(bf16[160,128]{1,0:T(8,128)(2,1)S(1)} %get-tuple-element.58), channel_id=1, source_target_pairs={{0,12},{4,8},{8,4},{12,0},{1,13},{5,9},{9,5},{13,1},{2,14},{6,10},... | collective-permute-start | bytes 122888 | tf_op jit(solution)/shard_map/ppermute | solution.py:492
  29.6 1.0 %shard_map.124 = bf16[16,16,128]{2,1,0:T(8,128)(2,1)} custom-call(bf16[256,1024]{1,0:T(8,128)(2,1)S(1)} %get-tuple-element.49.outer_ref, bf16[1024,128]{1,0:T(8,128)(2,1)S(1)} %get-tuple-element.38.final_ref, f32[1,128]{1,0:T(1,128)S(1)} %get-tuple-element.50.bias_ref), custom_call_target="tpu_custom_call" | custom-call | flops 100000000 | tf_op jit(solution)/shard_map/pallas_call | solution.py:173
  30.6 0.1 shard_map.126.unit_ref
  30.7 0.0 collective-permute-done.7.r1
  30.7 1.3 %collective-permute-done.8.r2 = bf16[160,128]{1,0:T(8,128)(2,1)S(1)} collective-permute-done((bf16[160,128]{1,0:T(8,128)(2,1)S(1)}, bf16[160,128]{1,0:T(8,128)(2,1)S(1)}, u32[]{:S(2)}, u32[]{:S(2)}) %collective-permute-start.8) | collective-permute-done | bytes 40992 | tf_op jit(solution)/shard_map/ppermute | solution.py:492
  32.0 2.9 %collective-permute-done.9.r3 = bf16[160,128]{1,0:T(8,128)(2,1)S(1)} collective-permute-done((bf16[160,128]{1,0:T(8,128)(2,1)S(1)}, bf16[160,128]{1,0:T(8,128)(2,1)S(1)}, u32[]{:S(2)}, u32[]{:S(2)}) %collective-permute-start.9) | collective-permute-done | bytes 40992 | tf_op jit(solution)/shard_map/ppermute | solution.py:492
  35.0 0.9 %shard_map.127 = (f32[64,128]{1,0:T(8,128)}, f32[32,64]{1,0:T(8,128)}, f32[32,64]{1,0:T(8,128)}, f32[16,8,64]{2,1,0:T(8,128)}) custom-call(f32[160,128]{1,0:T(8,128)S(1)} %get-tuple-element.55.own_ref, bf16[160,128]{1,0:T(8,128)(2,1)S(1)} %collective-permute-done.7.r1, bf16[160,128]{1,0:T(8,128)(2,1)S(1)} %collective-permute-done.8.r2, ...), custom_call_target="tpu_custom_call" | custom-call | tf_op jit(solution)/shard_map/pallas_call | solution.py:173
  (1 shorter events, 0.0 us)
Async XLA Ops:
  1.8 3.9 %collective-permute-start.2 = (bf16[64,128]{1,0:T(8,128)(2,1)S(1)}, bf16[64,128]{1,0:T(8,128)(2,1)S(1)}, u32[]{:S(2)}, u32[]{:S(2)}) collective-permute-start(bf16[64,128]{1,0:T(8,128)(2,1)S(1)} %get-tuple-element.36.n0), channel_id=1, source_target_pairs={{0,3},{1,2},{2,1},{3,0},{4,7},{5,6},{6,5},{7,4},{8,11},{9,10},{10,... | collective-permute-start | bytes 49160 | tf_op jit(solution)/shard_map/ppermute | solution.py:492
  4.3 3.7 %collective-permute-start.1 = (bf16[64,128]{1,0:T(8,128)(2,1)S(1)}, bf16[64,128]{1,0:T(8,128)(2,1)S(1)}, u32[]{:S(2)}, u32[]{:S(2)}) collective-permute-start(bf16[64,128]{1,0:T(8,128)(2,1)S(1)} %get-tuple-element.36.n0), channel_id=1, source_target_pairs={{0,2},{1,3},{2,0},{3,1},{4,6},{5,7},{6,4},{7,5},{8,10},{9,11},{10,... | collective-permute-start | bytes 49160 | tf_op jit(solution)/shard_map/ppermute | solution.py:492
  4.9 3.1 %collective-permute-start = (bf16[64,128]{1,0:T(8,128)(2,1)S(1)}, bf16[64,128]{1,0:T(8,128)(2,1)S(1)}, u32[]{:S(2)}, u32[]{:S(2)}) collective-permute-start(bf16[64,128]{1,0:T(8,128)(2,1)S(1)} %get-tuple-element.36.n0), channel_id=1, source_target_pairs={{0,1},{1,0},{2,3},{3,2},{4,5},{5,4},{6,7},{7,6},{8,9},{9,8},{10,11... | collective-permute-start | bytes 49160 | tf_op jit(solution)/shard_map/ppermute | solution.py:492
  8.1 2.4 %collective-permute-start.3 = (bf16[256,128]{1,0:T(8,128)(2,1)S(1)}, bf16[256,128]{1,0:T(8,128)(2,1)S(1)}, u32[]{:S(2)}, u32[]{:S(2)}) collective-permute-start(bf16[256,128]{1,0:T(8,128)(2,1)S(1)} %shard_map.120.unit_ref), channel_id=1, source_target_pairs={{0,0},{1,4},{2,8},{3,12},{4,1},{5,5},{6,9},{7,13},{8,2},{9,6},{10,... | collective-permute-start | bytes 196616 | tf_op jit(solution)/shard_map/ppermute | solution.py:557
  11.9 8.0 %collective-permute-start.4 = (bf16[384,128]{1,0:T(8,128)(2,1)S(1)}, bf16[384,128]{1,0:T(8,128)(2,1)S(1)}, u32[]{:S(2)}, u32[]{:S(2)}) collective-permute-start(bf16[384,128]{1,0:T(8,128)(2,1)S(1)} %get-tuple-element.52), channel_id=1, source_target_pairs={{0,1},{1,0},{2,3},{3,2},{4,5},{5,4},{6,7},{7,6},{8,9},{9,8},{10,11... | collective-permute-start | bytes 294920 | tf_op jit(solution)/shard_map/ppermute | solution.py:492
  15.1 8.4 %collective-permute-start.5 = (bf16[384,128]{1,0:T(8,128)(2,1)S(1)}, bf16[384,128]{1,0:T(8,128)(2,1)S(1)}, u32[]{:S(2)}, u32[]{:S(2)}) collective-permute-start(bf16[384,128]{1,0:T(8,128)(2,1)S(1)} %get-tuple-element.53), channel_id=1, source_target_pairs={{0,2},{1,3},{2,0},{3,1},{4,6},{5,7},{6,4},{7,5},{8,10},{9,11},{10,... | collective-permute-start | bytes 294920 | tf_op jit(solution)/shard_map/ppermute | solution.py:492
  19.9 5.2 %collective-permute-start.6 = (bf16[384,128]{1,0:T(8,128)(2,1)S(1)}, bf16[384,128]{1,0:T(8,128)(2,1)S(1)}, u32[]{:S(2)}, u32[]{:S(2)}) collective-permute-start(bf16[384,128]{1,0:T(8,128)(2,1)S(1)} %get-tuple-element.54), channel_id=1, source_target_pairs={{0,3},{1,2},{2,1},{3,0},{4,7},{5,6},{6,5},{7,4},{8,11},{9,10},{10,... | collective-permute-start | bytes 294920 | tf_op jit(solution)/shard_map/ppermute | solution.py:492
  25.2 5.6 %collective-permute-start.7 = (bf16[160,128]{1,0:T(8,128)(2,1)S(1)}, bf16[160,128]{1,0:T(8,128)(2,1)S(1)}, u32[]{:S(2)}, u32[]{:S(2)}) collective-permute-start(bf16[160,128]{1,0:T(8,128)(2,1)S(1)} %get-tuple-element.56), channel_id=1, source_target_pairs={{0,4},{4,0},{8,12},{12,8},{1,5},{5,1},{9,13},{13,9},{2,6},{6,2},{1... | collective-permute-start | bytes 122888 | tf_op jit(solution)/shard_map/ppermute | solution.py:492
  25.6 6.5 %collective-permute-start.8 = (bf16[160,128]{1,0:T(8,128)(2,1)S(1)}, bf16[160,128]{1,0:T(8,128)(2,1)S(1)}, u32[]{:S(2)}, u32[]{:S(2)}) collective-permute-start(bf16[160,128]{1,0:T(8,128)(2,1)S(1)} %get-tuple-element.57), channel_id=1, source_target_pairs={{0,8},{4,12},{8,0},{12,4},{1,9},{5,13},{9,1},{13,5},{2,10},{6,14},... | collective-permute-start | bytes 122888 | tf_op jit(solution)/shard_map/ppermute | solution.py:492
  29.2 5.8 %collective-permute-start.9 = (bf16[160,128]{1,0:T(8,128)(2,1)S(1)}, bf16[160,128]{1,0:T(8,128)(2,1)S(1)}, u32[]{:S(2)}, u32[]{:S(2)}) collective-permute-start(bf16[160,128]{1,0:T(8,128)(2,1)S(1)} %get-tuple-element.58), channel_id=1, source_target_pairs={{0,12},{4,8},{8,4},{12,0},{1,13},{5,9},{9,5},{13,1},{2,14},{6,10},... | collective-permute-start | bytes 122888 | tf_op jit(solution)/shard_map/ppermute | solution.py:492

commit v5 on v4

--- a/solution.py
+++ b/solution.py
@@ -345,7 +345,7 @@
 
 def pair_kernel(
     unit_ref, left_ref, turned_ref, part_ref, weight_ref, order_ref, by_row_ref, cot_cols_ref,
-    outer_ref, own_ref, m1, m2, m3,
+    outer_ref, own_ref, m3, m2, m1,
     block_ref, slope_f, spread_f, both_f,
     *, chans, seqs, sizes,
 ):
@@ -419,7 +419,7 @@
 
 
 def between_kernel(
-    own_ref, r1, r2, r3, left_ref, next_ref, m1, m2, m3, total_f, right_f, *, rows, share
+    own_ref, r3, r2, r1, left_ref, next_ref, m3, m2, m1, total_f, right_f, *, rows, share
 ):
     refs = (own_ref, r1, r2, r3)
     span = left_ref.shape[0]
@@ -459,7 +459,7 @@
 
 
 def last_kernel(
-    own_ref, r1, r2, r3, unit_ref, xhat_ref, spread_ref, gain_ref, second_ref,
+    own_ref, r3, r2, r1, unit_ref, xhat_ref, spread_ref, gain_ref, second_ref,
     final_ref, first_slope_ref, second_slope_ref, out_ref, unit_f,
 ):
     total = own_ref[...] + r1[...].astype(F32) + r2[...].astype(F32) + r3[...].astype(F32)
@@ -486,12 +486,22 @@
         ref[...] = out
 
 
-def exchange(messages, axis):
+def exchange(messages, axis, order):
     size = lax.axis_size(axis)
-    return [
-        lax.ppermute(m, axis, [(p, p ^ k) for p in range(size)])
-        for k, m in enumerate(messages, 1)
-    ]
+    got = {}
+    for k in order:
+        got[k] = lax.ppermute(messages[k], axis, [(p, p ^ k) for p in range(size)])
+    return [got[k] for k in sorted(got)]
+
+
+def holders(rows, cols):
+    pairs = []
+    for r in range(rows):
+        far = sorted((z for z in range(rows) if z != r), key=lambda z: (-abs(z - r), z))
+        near = sorted((q for q in range(cols) if q != r), key=lambda q: (q // 2 != r // 2, q))
+        pairs += [(r * cols + r, r * cols + r)]
+        pairs += [(r * cols + q, z * cols + r) for q, z in zip(near, far)]
+    return sorted(pairs)
 
 
 def local_square(
@@ -511,7 +521,6 @@
     seqs = quarter * cols
     per, steps = LANES // chans, chans // (LANES // chans)
     share = total // (rows * cols)
-    flip = [(r * cols + q, q * cols + r) for r in range(rows) for q in range(cols)]
     shape = jax.ShapeDtypeStruct
     wide, tall = tokens * LANES, steps * tokens
     groups = tokens // per
@@ -536,7 +545,7 @@
         + [pltpu.SemaphoreType.DMA((len(inputs),))],
         space=pltpu.HBM,
     )(*[pltpu.with_memory_space_constraint(i, pltpu.HBM) for i in inputs])
-    units = [unit] + exchange([unit] * (cols - 1), "cols")
+    units = [unit] + exchange([unit] * cols, "cols", (1, 2, 3))
     by_col, by_row, cot_cols, weight, order = call(
         functools.partial(grad_kernel, chans=chans),
         (
@@ -554,7 +563,7 @@
         shape((half * seqs, 2 * width), BF16),
         [pltpu.VMEM((half, seqs, 2 * width), F32)],
     )(*units)
-    unit_cols = lax.ppermute(unit_rows, ("rows", "cols"), flip)
+    unit_cols = lax.ppermute(unit_rows, ("rows", "cols"), holders(rows, cols))
     left, turned, part = call(
         functools.partial(left_kernel, chans=chans, seqs=seqs),
         (
@@ -581,7 +590,7 @@
             pltpu.VMEM((groups, 2, seqs, LANES), F32),
         ],
     )(unit_cols, left, turned, part, weight, order, by_row, cot_cols)
-    got = exchange(messages, "cols")
+    got = exchange([own] + messages[::-1], "cols", (1, 2, 3))
     update = call(
         update_kernel,
         shape((tokens, tokens, pair_ch), BF16),
@@ -600,8 +609,8 @@
             pltpu.VMEM((rows * share + 2 * span + width, LANES), F32),
             pltpu.VMEM((cols, span, LANES), F32),
         ],
-    )(own, *got)
-    got = exchange(messages, "rows")
+    )(own, *got[::-1])
+    got = exchange([own] + messages[::-1], "rows", (1, 2, 3))
     from_left = call(functools.partial(to_unit, quarter=quarter), aligned, flops=10**8)(back, first)
     final_slope, first_slope, second_slope, alignment_slope = call(
         last_kernel,
@@ -612,7 +621,7 @@
             aligned,
         ),
         [pltpu.VMEM((tokens, quarter, width), F32)],
-    )(own, *got, from_left, xhat, spread, gain, second)
+    )(own, *got[::-1], from_left, xhat, spread, gain, second)
     return update, alignment_slope, final_slope, first_slope.T, second_slope.T
 
 

time: 36 us -> 32.4 us (0.90)
  waiting for transfers between devices: 12.5 us -> 10.2 us
  starting transfers between devices: 16.3 us -> 14.9 us
    ppermute x10, waiting for transfers between devices: 12.5 us -> 10.2 us  [the longest x9 10.2 us: exchange(): got[k] = lax.ppermute(messages[k], axis, [(p, p ^ k) for p in range(size)])]
    ppermute x10, starting transfers between devices: 16.3 us -> 14.9 us  [the longest x9 14.3 us: exchange(): got[k] = lax.ppermute(messages[k], axis, [(p, p ^ k) for p in range(size)])]
  transfers between devices with their start and end apart: 10 -> 10, of which waited for: 6 -> 6; matrix products, arithmetic and copies ran while one was open for 0% -> 0% of each run, Pallas kernels for 8% -> 9%
where the time goes in v5:
time: 32.4 us; the launch traced here: 32.2 us
  starting transfers between devices  14.9 us (46%)
  waiting for transfers between devices  10.2 us (31%)
  Pallas kernels  6.37 us (20%)
  between operations  0.7 us (2%)
    ppermute x9, starting transfers between devices, exchange(): got[k] = lax.ppermute(messages[k], axis, [(p, p ^ k) for p in range(size)])  14.3 us
    ppermute x9, waiting for transfers between devices, exchange(): got[k] = lax.ppermute(messages[k], axis, [(p, p ^ k) for p in range(size)])  10.2 us
    pallas_call x9, Pallas kernels, run(): pl.pallas_call(kernel, out_shape=out_shape, in_specs=[place] * len(args),...  6.37 us
    ppermute x1, starting transfers between devices, local_square(): unit_cols = lax.ppermute(unit_rows, ('rows', 'cols'), holders(rows, cols))  0.66 us
  transfers between devices with their start and end apart: 10, of which 6 were waited for; matrix products, arithmetic and copies ran while one was open for 0% of the time, Pallas kernels for 9%

profile of v5, /device:TPU:0, one launch (start us, length us, event | category | flops | bytes accessed | tf_op | source)
XLA Modules:
  0.0 32.2 jit_solution(15506641958776207602)
XLA Ops:
  0.6 1.2 %shard_map.119 = (bf16[64,128]{1,0:T(8,128)(2,1)S(1)}, f32[128,64]{1,0:T(8,128)S(1)}, f32[128,64]{1,0:T(8,128)S(1)}, f32[1,64]{1,0:T(1,128)S(1)}, bf16[16,16,128...) custom-call(f32[16,8,64]{2,1,0:T(8,128)} %refs_0_.1, ...), custom_call_target="tpu_custom_call" | custom-call | tf_op jit(solution)/shard_map/pallas_call | solution.py:173
  1.8 2.5 %collective-permute-start.2 = (bf16[64,128]{1,0:T(8,128)(2,1)S(1)}, bf16[64,128]{1,0:T(8,128)(2,1)S(1)}, u32[]{:S(2)}, u32[]{:S(2)}) collective-permute-start(bf16[64,128]{1,0:T(8,128)(2,1)S(1)} %get-tuple-element.36.n0), channel_id=1, source_target_pairs={{0,3},{1,2},{2,1},{3,0},{4,7},{5,6},{6,5},{7,4},{8,11},{9,10},{10,... | collective-permute-start | bytes 49160 | tf_op jit(solution)/shard_map/ppermute | solution.py:493
  4.3 0.6 %collective-permute-start.1 = (bf16[64,128]{1,0:T(8,128)(2,1)S(1)}, bf16[64,128]{1,0:T(8,128)(2,1)S(1)}, u32[]{:S(2)}, u32[]{:S(2)}) collective-permute-start(bf16[64,128]{1,0:T(8,128)(2,1)S(1)} %get-tuple-element.36.n0), channel_id=1, source_target_pairs={{0,2},{1,3},{2,0},{3,1},{4,6},{5,7},{6,4},{7,5},{8,10},{9,11},{10,... | collective-permute-start | bytes 49160 | tf_op jit(solution)/shard_map/ppermute | solution.py:493
  4.9 0.0 collective-permute-start
  5.0 0.8 %collective-permute-done.2.n3 = bf16[64,128]{1,0:T(8,128)(2,1)S(1)} collective-permute-done((bf16[64,128]{1,0:T(8,128)(2,1)S(1)}, bf16[64,128]{1,0:T(8,128)(2,1)S(1)}, u32[]{:S(2)}, u32[]{:S(2)}) %collective-permute-start.2) | collective-permute-done | bytes 16416 | tf_op jit(solution)/shard_map/ppermute | solution.py:493
  5.7 2.3 %collective-permute-done.1.n2 = bf16[64,128]{1,0:T(8,128)(2,1)S(1)} collective-permute-done((bf16[64,128]{1,0:T(8,128)(2,1)S(1)}, bf16[64,128]{1,0:T(8,128)(2,1)S(1)}, u32[]{:S(2)}, u32[]{:S(2)}) %collective-permute-start.1) | collective-permute-done | bytes 16416 | tf_op jit(solution)/shard_map/ppermute | solution.py:493
  8.0 0.0 collective-permute-done.n1
  8.1 0.7 %collective-permute-start.3 = (bf16[256,128]{1,0:T(8,128)(2,1)S(1)}, bf16[256,128]{1,0:T(8,128)(2,1)S(1)}, u32[]{:S(2)}, u32[]{:S(2)}) collective-permute-start(bf16[256,128]{1,0:T(8,128)(2,1)S(1)} %shard_map.120.unit_ref), channel_id=1, source_target_pairs={{0,0},{1,12},{2,8},{3,4},{4,13},{5,5},{6,1},{7,9},{8,6},{9,14},{10... | collective-permute-start | bytes 196616 | tf_op jit(solution)/shard_map/ppermute | solution.py:566
  8.7 0.9 %shard_map.121 = (bf16[128,2048]{1,0:T(8,128)(2,1)S(1)}, bf16[128,2048]{1,0:T(8,128)(2,1)S(1)}, bf16[256,128]{1,0:T(8,128)(2,1)S(1)}, bf16[4,512,128]{2,1,0:T(8,128)(2,1)S(1)}, bf16[512,512]{1,0:T(8,128)(2,1)S(1)}) custom-call(bf16[16,16,128]{2,1,0:T(8,128)(2,1)S(1)} %get-tuple-element.37.cot_ref, bf16[1024,128]{1,0:T(8,128)(2,1)S(1)} %get-tuple-element.38.final_ref, ...), custom_call_target="tpu_custom_call" | custom-call | flops 268435456 | tf_op jit(solution)/shard_map/pallas_call | solution.py:173
  9.6 0.8 %shard_map.122 = (bf16[128,128]{1,0:T(8,128)(2,1)S(1)}, bf16[128,256]{1,0:T(8,128)(2,1)S(1)}, f32[4,32,128]{2,1,0:T(8,128)S(1)}) custom-call(bf16[256,128]{1,0:T(8,128)(2,1)S(1)} %shard_map.120.unit_ref, bf16[4,512,128]{2,1,0:T(8,128)(2,1)S(1)} %get-tuple-element.41.weight_ref, bf16[512,512]{1,0:T(8,128)(2,1)S(1)} %get-tuple-element.42.order_ref, ...), custom_call_target="tpu_custom_call" | custom-call | flops 100000000 | tf_op jit(solution)/shard_map/pallas_call | solution.py:173
  10.4 0.0 collective-permute-done.3.unit_ref
  10.4 1.4 %shard_map.123 = (bf16[256,1024]{1,0:T(8,128)(2,1)S(1)}, f32[384,128]{1,0:T(8,128)S(1)}, bf16[384,128]{1,0:T(8,128)(2,1)S(1)}, bf16[384,128]{1,0:T(8,128)(2,1)S(1)}, bf16[384,128]{1,0:T(8,128)(2,1)S(1)}) custom-call(bf16[256,128]{1,0:T(8,128)(2,1)S(1)} %collective-permute-done.3.unit_ref, bf16[128,128]{1,0:T(8,128)(2,1)S(1)} %get-tuple-element.44.left_ref, ...), custom_call_target="tpu_custom_call" | custom-call | tf_op jit(solution)/shard_map/pallas_call | solution.py:173
  11.9 5.5 %collective-permute-start.4 = (bf16[384,128]{1,0:T(8,128)(2,1)S(1)}, bf16[384,128]{1,0:T(8,128)(2,1)S(1)}, u32[]{:S(2)}, u32[]{:S(2)}) collective-permute-start(bf16[384,128]{1,0:T(8,128)(2,1)S(1)} %get-tuple-element.52), channel_id=1, source_target_pairs={{0,3},{1,2},{2,1},{3,0},{4,7},{5,6},{6,5},{7,4},{8,11},{9,10},{10,... | collective-permute-start | bytes 294920 | tf_op jit(solution)/shard_map/ppermute | solution.py:493
  17.3 1.2 %collective-permute-start.5 = (bf16[384,128]{1,0:T(8,128)(2,1)S(1)}, bf16[384,128]{1,0:T(8,128)(2,1)S(1)}, u32[]{:S(2)}, u32[]{:S(2)}) collective-permute-start(bf16[384,128]{1,0:T(8,128)(2,1)S(1)} %get-tuple-element.53), channel_id=1, source_target_pairs={{0,2},{1,3},{2,0},{3,1},{4,6},{5,7},{6,4},{7,5},{8,10},{9,11},{10,... | collective-permute-start | bytes 294920 | tf_op jit(solution)/shard_map/ppermute | solution.py:493
  18.5 0.0 collective-permute-start.6
  18.5 2.0 %collective-permute-done.4.r3 = bf16[384,128]{1,0:T(8,128)(2,1)S(1)} collective-permute-done((bf16[384,128]{1,0:T(8,128)(2,1)S(1)}, bf16[384,128]{1,0:T(8,128)(2,1)S(1)}, u32[]{:S(2)}, u32[]{:S(2)}) %collective-permute-start.4) | collective-permute-done | bytes 98336 | tf_op jit(solution)/shard_map/ppermute | solution.py:493
  20.5 2.7 %collective-permute-done.5.r2 = bf16[384,128]{1,0:T(8,128)(2,1)S(1)} collective-permute-done((bf16[384,128]{1,0:T(8,128)(2,1)S(1)}, bf16[384,128]{1,0:T(8,128)(2,1)S(1)}, u32[]{:S(2)}, u32[]{:S(2)}) %collective-permute-start.5) | collective-permute-done | bytes 98336 | tf_op jit(solution)/shard_map/ppermute | solution.py:493
  23.2 0.0 collective-permute-done.6.r1
  23.2 0.1 shard_map.125
  23.3 3.1 %collective-permute-start.7 = (bf16[160,128]{1,0:T(8,128)(2,1)S(1)}, bf16[160,128]{1,0:T(8,128)(2,1)S(1)}, u32[]{:S(2)}, u32[]{:S(2)}) collective-permute-start(bf16[160,128]{1,0:T(8,128)(2,1)S(1)} %get-tuple-element.56), channel_id=1, source_target_pairs={{0,12},{4,8},{8,4},{12,0},{1,13},{5,9},{9,5},{13,1},{2,14},{6,10},... | collective-permute-start | bytes 122888 | tf_op jit(solution)/shard_map/ppermute | solution.py:493
  26.4 0.0 collective-permute-start.8
  26.4 1.3 %collective-permute-start.9 = (bf16[160,128]{1,0:T(8,128)(2,1)S(1)}, bf16[160,128]{1,0:T(8,128)(2,1)S(1)}, u32[]{:S(2)}, u32[]{:S(2)}) collective-permute-start(bf16[160,128]{1,0:T(8,128)(2,1)S(1)} %get-tuple-element.58), channel_id=1, source_target_pairs={{0,4},{4,0},{8,12},{12,8},{1,5},{5,1},{9,13},{13,9},{2,6},{6,2},{1... | collective-permute-start | bytes 122888 | tf_op jit(solution)/shard_map/ppermute | solution.py:493
  27.7 1.0 %shard_map.124 = bf16[16,16,128]{2,1,0:T(8,128)(2,1)} custom-call(bf16[256,1024]{1,0:T(8,128)(2,1)S(1)} %get-tuple-element.49.outer_ref, bf16[1024,128]{1,0:T(8,128)(2,1)S(1)} %get-tuple-element.38.final_ref, f32[1,128]{1,0:T(1,128)S(1)} %get-tuple-element.50.bias_ref), custom_call_target="tpu_custom_call" | custom-call | flops 100000000 | tf_op jit(solution)/shard_map/pallas_call | solution.py:173
  28.7 0.1 shard_map.126.unit_ref
  28.8 0.3 %collective-permute-done.7.r3 = bf16[160,128]{1,0:T(8,128)(2,1)S(1)} collective-permute-done((bf16[160,128]{1,0:T(8,128)(2,1)S(1)}, bf16[160,128]{1,0:T(8,128)(2,1)S(1)}, u32[]{:S(2)}, u32[]{:S(2)}) %collective-permute-start.7) | collective-permute-done | bytes 40992 | tf_op jit(solution)/shard_map/ppermute | solution.py:493
  29.2 2.2 %collective-permute-done.8.r2 = bf16[160,128]{1,0:T(8,128)(2,1)S(1)} collective-permute-done((bf16[160,128]{1,0:T(8,128)(2,1)S(1)}, bf16[160,128]{1,0:T(8,128)(2,1)S(1)}, u32[]{:S(2)}, u32[]{:S(2)}) %collective-permute-start.8) | collective-permute-done | bytes 40992 | tf_op jit(solution)/shard_map/ppermute | solution.py:493
  31.3 0.0 collective-permute-done.9.r1
  31.3 0.9 %shard_map.127 = (f32[64,128]{1,0:T(8,128)}, f32[32,64]{1,0:T(8,128)}, f32[32,64]{1,0:T(8,128)}, f32[16,8,64]{2,1,0:T(8,128)}) custom-call(f32[160,128]{1,0:T(8,128)S(1)} %get-tuple-element.55.own_ref, bf16[160,128]{1,0:T(8,128)(2,1)S(1)} %collective-permute-done.7.r3, bf16[160,128]{1,0:T(8,128)(2,1)S(1)} %collective-permute-done.8.r2, ...), custom_call_target="tpu_custom_call" | custom-call | tf_op jit(solution)/shard_map/pallas_call | solution.py:173
  (1 shorter events, 0.0 us)
Async XLA Ops:
  1.8 3.9 %collective-permute-start.2 = (bf16[64,128]{1,0:T(8,128)(2,1)S(1)}, bf16[64,128]{1,0:T(8,128)(2,1)S(1)}, u32[]{:S(2)}, u32[]{:S(2)}) collective-permute-start(bf16[64,128]{1,0:T(8,128)(2,1)S(1)} %get-tuple-element.36.n0), channel_id=1, source_target_pairs={{0,3},{1,2},{2,1},{3,0},{4,7},{5,6},{6,5},{7,4},{8,11},{9,10},{10,... | collective-permute-start | bytes 49160 | tf_op jit(solution)/shard_map/ppermute | solution.py:493
  4.3 3.7 %collective-permute-start.1 = (bf16[64,128]{1,0:T(8,128)(2,1)S(1)}, bf16[64,128]{1,0:T(8,128)(2,1)S(1)}, u32[]{:S(2)}, u32[]{:S(2)}) collective-permute-start(bf16[64,128]{1,0:T(8,128)(2,1)S(1)} %get-tuple-element.36.n0), channel_id=1, source_target_pairs={{0,2},{1,3},{2,0},{3,1},{4,6},{5,7},{6,4},{7,5},{8,10},{9,11},{10,... | collective-permute-start | bytes 49160 | tf_op jit(solution)/shard_map/ppermute | solution.py:493
  4.9 3.1 %collective-permute-start = (bf16[64,128]{1,0:T(8,128)(2,1)S(1)}, bf16[64,128]{1,0:T(8,128)(2,1)S(1)}, u32[]{:S(2)}, u32[]{:S(2)}) collective-permute-start(bf16[64,128]{1,0:T(8,128)(2,1)S(1)} %get-tuple-element.36.n0), channel_id=1, source_target_pairs={{0,1},{1,0},{2,3},{3,2},{4,5},{5,4},{6,7},{7,6},{8,9},{9,8},{10,11... | collective-permute-start | bytes 49160 | tf_op jit(solution)/shard_map/ppermute | solution.py:493
  8.1 2.4 %collective-permute-start.3 = (bf16[256,128]{1,0:T(8,128)(2,1)S(1)}, bf16[256,128]{1,0:T(8,128)(2,1)S(1)}, u32[]{:S(2)}, u32[]{:S(2)}) collective-permute-start(bf16[256,128]{1,0:T(8,128)(2,1)S(1)} %shard_map.120.unit_ref), channel_id=1, source_target_pairs={{0,0},{1,12},{2,8},{3,4},{4,13},{5,5},{6,1},{7,9},{8,6},{9,14},{10... | collective-permute-start | bytes 196616 | tf_op jit(solution)/shard_map/ppermute | solution.py:566
  11.9 8.7 %collective-permute-start.4 = (bf16[384,128]{1,0:T(8,128)(2,1)S(1)}, bf16[384,128]{1,0:T(8,128)(2,1)S(1)}, u32[]{:S(2)}, u32[]{:S(2)}) collective-permute-start(bf16[384,128]{1,0:T(8,128)(2,1)S(1)} %get-tuple-element.52), channel_id=1, source_target_pairs={{0,3},{1,2},{2,1},{3,0},{4,7},{5,6},{6,5},{7,4},{8,11},{9,10},{10,... | collective-permute-start | bytes 294920 | tf_op jit(solution)/shard_map/ppermute | solution.py:493
  17.3 5.9 %collective-permute-start.5 = (bf16[384,128]{1,0:T(8,128)(2,1)S(1)}, bf16[384,128]{1,0:T(8,128)(2,1)S(1)}, u32[]{:S(2)}, u32[]{:S(2)}) collective-permute-start(bf16[384,128]{1,0:T(8,128)(2,1)S(1)} %get-tuple-element.53), channel_id=1, source_target_pairs={{0,2},{1,3},{2,0},{3,1},{4,6},{5,7},{6,4},{7,5},{8,10},{9,11},{10,... | collective-permute-start | bytes 294920 | tf_op jit(solution)/shard_map/ppermute | solution.py:493
  18.5 4.7 %collective-permute-start.6 = (bf16[384,128]{1,0:T(8,128)(2,1)S(1)}, bf16[384,128]{1,0:T(8,128)(2,1)S(1)}, u32[]{:S(2)}, u32[]{:S(2)}) collective-permute-start(bf16[384,128]{1,0:T(8,128)(2,1)S(1)} %get-tuple-element.54), channel_id=1, source_target_pairs={{0,1},{1,0},{2,3},{3,2},{4,5},{5,4},{6,7},{7,6},{8,9},{9,8},{10,11... | collective-permute-start | bytes 294920 | tf_op jit(solution)/shard_map/ppermute | solution.py:493
  23.3 5.9 %collective-permute-start.7 = (bf16[160,128]{1,0:T(8,128)(2,1)S(1)}, bf16[160,128]{1,0:T(8,128)(2,1)S(1)}, u32[]{:S(2)}, u32[]{:S(2)}) collective-permute-start(bf16[160,128]{1,0:T(8,128)(2,1)S(1)} %get-tuple-element.56), channel_id=1, source_target_pairs={{0,12},{4,8},{8,4},{12,0},{1,13},{5,9},{9,5},{13,1},{2,14},{6,10},... | collective-permute-start | bytes 122888 | tf_op jit(solution)/shard_map/ppermute | solution.py:493
  26.4 4.9 %collective-permute-start.8 = (bf16[160,128]{1,0:T(8,128)(2,1)S(1)}, bf16[160,128]{1,0:T(8,128)(2,1)S(1)}, u32[]{:S(2)}, u32[]{:S(2)}) collective-permute-start(bf16[160,128]{1,0:T(8,128)(2,1)S(1)} %get-tuple-element.57), channel_id=1, source_target_pairs={{0,8},{4,12},{8,0},{12,4},{1,9},{5,13},{9,1},{13,5},{2,10},{6,14},... | collective-permute-start | bytes 122888 | tf_op jit(solution)/shard_map/ppermute | solution.py:493
  26.4 4.9 %collective-permute-start.9 = (bf16[160,128]{1,0:T(8,128)(2,1)S(1)}, bf16[160,128]{1,0:T(8,128)(2,1)S(1)}, u32[]{:S(2)}, u32[]{:S(2)}) collective-permute-start(bf16[160,128]{1,0:T(8,128)(2,1)S(1)} %get-tuple-element.58), channel_id=1, source_target_pairs={{0,4},{4,0},{8,12},{12,8},{1,5},{5,1},{9,13},{13,9},{2,6},{6,2},{1... | collective-permute-start | bytes 122888 | tf_op jit(solution)/shard_map/ppermute | solution.py:493

commit v6 on v5

--- a/solution.py
+++ b/solution.py
@@ -1,4 +1,5 @@
 import functools
+import itertools
 
 import jax
 import jax.numpy as jnp
@@ -259,15 +260,22 @@
         order_ref[:, b * LANES : (b + 1) * LANES] = jnp.where(row == wanted, 1.0, 0.0).astype(BF16)
 
 
-def joint_kernel(n0, n1, n2, n3, out_ref, unit_f):
-    blocks = (n0, n1, n2, n3)
-    mine = lax.axis_index("cols")
+def half_kernel(own_ref, other_ref, out_ref, unit_f):
+    low = lax.axis_index("cols") % 2
     half, seqs, lanes = unit_f.shape
-    quarter = seqs // len(blocks)
-    for k, ref in enumerate(blocks):
-        at = pl.multiple_of((mine ^ k) * quarter, quarter)
+    quarter = seqs // 2
+    for k, ref in enumerate((own_ref, other_ref)):
+        at = pl.multiple_of((low ^ k) * quarter, quarter)
         unit_f[:, pl.ds(at, quarter), :] = ref[...].astype(F32).reshape(half, quarter, lanes)
     out_ref[...] = unit_f[...].reshape(half * seqs, lanes).astype(BF16)
+
+
+def join(first_half, refs, unit_ref):
+    half, seqs, lanes = unit_ref.shape
+    for k, ref in enumerate(refs):
+        at = pl.multiple_of((first_half ^ k) * (seqs // 2), seqs // 2)
+        unit_ref[:, pl.ds(at, seqs // 2), :] = ref[...].reshape(half, seqs // 2, lanes)
+    return unit_ref[...].reshape(half * seqs, lanes)
 
 
 def project(unit, weight_ref, x, seqs, per):
@@ -330,11 +338,13 @@
 
 
 def left_kernel(
-    unit_ref, weight_ref, order_ref, by_col_ref, left_ref, turned_ref, part_ref, spread_f, *, chans, seqs
+    u0, u1, weight_ref, order_ref, by_col_ref, left_ref, turned_ref, part_ref, unit_ref, spread_f,
+    *, chans,
 ):
     per = LANES // chans
-    tokens = unit_ref.shape[0] // seqs * 2
-    unit = unit_ref[...]
+    half, seqs, _ = unit_ref.shape
+    tokens = 2 * half
+    unit = join(lax.axis_index("cols") // 2, (u0, u1), unit_ref)
     turned_ref[...] = unit.astype(F32).T.astype(BF16)
     turned = reorder(project(unit, weight_ref, 0, seqs, per), order_ref)
     left_ref[...] = turned.T.astype(BF16)
@@ -344,20 +354,22 @@
 
 
 def pair_kernel(
-    unit_ref, left_ref, turned_ref, part_ref, weight_ref, order_ref, by_row_ref, cot_cols_ref,
+    u0, u1, left_ref, turned_ref, part_ref, weight_ref, order_ref, by_row_ref, cot_cols_ref,
     outer_ref, own_ref, m3, m2, m1,
-    block_ref, slope_f, spread_f, both_f,
-    *, chans, seqs, sizes,
+    block_ref, slope_f, spread_f, both_f, unit_ref,
+    *, chans, sizes, first_halves,
 ):
     per, steps = LANES // chans, chans // (LANES // chans)
     rows, cols = sizes
-    tokens = unit_ref.shape[0] // seqs * 2
+    half, seqs, _ = unit_ref.shape
+    tokens = 2 * half
     groups = tokens // per
     quarter = seqs // cols
     share = slope_f.shape[0] // (rows * cols)
     mine = lax.axis_index("cols")
     group = lane_group((seqs, LANES), chans)
-    unit = unit_ref[...]
+    place = lax.axis_index("rows") * cols + mine
+    unit = join((first_halves >> place) & 1, (u0, u1), unit_ref)
     right = project(unit, weight_ref, 1, seqs, per)
     for p, tile in enumerate(right):
         tile = tile.astype(F32)
@@ -495,13 +507,26 @@
 
 
 def holders(rows, cols):
-    pairs = []
+    first, second, mask = [], [], 0
     for r in range(rows):
-        far = sorted((z for z in range(rows) if z != r), key=lambda z: (-abs(z - r), z))
-        near = sorted((q for q in range(cols) if q != r), key=lambda q: (q // 2 != r // 2, q))
-        pairs += [(r * cols + r, r * cols + r)]
-        pairs += [(r * cols + q, z * cols + r) for q, z in zip(near, far)]
-    return sorted(pairs)
+
+        def hops(to):
+            return [abs(z - r) + (q // 2 != r // 2) for q, z in enumerate(to) if z != r]
+
+        best = None
+        for a in itertools.permutations(range(rows)):
+            for b in itertools.permutations(range(rows)):
+                if any(a.index(z) // 2 == b.index(z) // 2 for z in range(rows)):
+                    continue
+                cost = (max(hops(a) + hops(b)), sum(hops(a) + hops(b)))
+                if best is None or cost < best[0]:
+                    best = cost, a, b
+        _, a, b = best
+        first += [(r * cols + q, z * cols + r) for q, z in enumerate(a)]
+        second += [(r * cols + q, z * cols + r) for q, z in enumerate(b)]
+        for q, z in enumerate(a):
+            mask |= q // 2 << (z * cols + r)
+    return first, second, mask
 
 
 def local_square(
@@ -545,7 +570,16 @@
         + [pltpu.SemaphoreType.DMA((len(inputs),))],
         space=pltpu.HBM,
     )(*[pltpu.with_memory_space_constraint(i, pltpu.HBM) for i in inputs])
-    units = [unit] + exchange([unit] * cols, "cols", (1, 2, 3))
+    pairs = [(p, p ^ 1) for p in range(cols)]
+    halves = call(
+        half_kernel,
+        shape((half * seqs // 2, 2 * width), BF16),
+        [pltpu.VMEM((half, seqs // 2, 2 * width), F32)],
+    )(unit, lax.ppermute(unit, "cols", pairs))
+    from_first, from_second, first_halves = holders(rows, cols)
+    cols_a = lax.ppermute(halves, ("rows", "cols"), from_first)
+    cols_b = lax.ppermute(halves, ("rows", "cols"), from_second)
+    across = lax.ppermute(halves, "cols", [(p, p ^ 2) for p in range(cols)])
     by_col, by_row, cot_cols, weight, order = call(
         functools.partial(grad_kernel, chans=chans),
         (
@@ -558,26 +592,22 @@
         [pltpu.VMEM(adjoint_update.shape, F32), pltpu.VMEM((total, pair_ch), F32)],
         flops=8 * tokens * tokens * total * pair_ch,
     )(cot, final, first, second)
-    unit_rows = call(
-        joint_kernel,
-        shape((half * seqs, 2 * width), BF16),
-        [pltpu.VMEM((half, seqs, 2 * width), F32)],
-    )(*units)
-    unit_cols = lax.ppermute(unit_rows, ("rows", "cols"), holders(rows, cols))
     left, turned, part = call(
-        functools.partial(left_kernel, chans=chans, seqs=seqs),
+        functools.partial(left_kernel, chans=chans),
         (
             shape((tall, LANES), BF16),
             shape((2 * width, half * seqs), BF16),
             shape((groups, seqs, LANES), F32),
         ),
-        [pltpu.VMEM((LANES, wide), F32)],
+        [pltpu.VMEM((half, seqs, 2 * width), BF16), pltpu.VMEM((LANES, wide), F32)],
         flops=10**8,
-    )(unit_rows, weight, order, by_col)
+    )(halves, across, weight, order, by_col)
     span = groups * quarter
     message = rows * share + 2 * span + width
     outer, own, *messages = call(
-        functools.partial(pair_kernel, chans=chans, seqs=seqs, sizes=(rows, cols)),
+        functools.partial(
+            pair_kernel, chans=chans, sizes=(rows, cols), first_halves=first_halves
+        ),
         (
             shape((tokens * tokens, total), BF16),
             shape((message, LANES), F32),
@@ -588,8 +618,9 @@
             pltpu.VMEM((total, pair_ch), F32),
             pltpu.VMEM((LANES, wide), F32),
             pltpu.VMEM((groups, 2, seqs, LANES), F32),
+            pltpu.VMEM((half, seqs, 2 * width), BF16),
         ],
-    )(unit_cols, left, turned, part, weight, order, by_row, cot_cols)
+    )(cols_a, cols_b, left, turned, part, weight, order, by_row, cot_cols)
     got = exchange([own] + messages[::-1], "cols", (1, 2, 3))
     update = call(
         update_kernel,
@@ -666,12 +697,13 @@
 
     def whole(*args):
         square = fits(mesh, args[0], args[3], args[5])
-        return jax.shard_map(
+        step = jax.shard_map(
             local_square if square else local_general,
             mesh=mesh,
             in_specs=in_specs,
             out_specs=out_specs,
             check_vma=False,
-        )(*args)
+        )
+        return step(*args)
 
     return whole

time: 32.4 us -> 32.1 us (level)
  waiting for transfers between devices: 10.2 us -> 7.76 us
  starting transfers between devices: 14.9 us -> 17.1 us
    ppermute x1 -> x4, starting transfers between devices: 0.66 us -> 6.68 us  [the longest x1 2.88 us: local_square(): across = lax.ppermute(halves, 'cols', [(p, p ^ 2) for p in range(cols)])]
    ppermute x9 -> x6, starting transfers between devices: 14.3 us -> 10.4 us  [exchange(): got[k] = lax.ppermute(messages[k], axis, [(p, p ^ k) for p in range(size)])]
    ppermute x9 -> x6, waiting for transfers between devices: 10.2 us -> 6.91 us  [exchange(): got[k] = lax.ppermute(messages[k], axis, [(p, p ^ k) for p in range(size)])]
    ppermute x1 -> x4, waiting for transfers between devices: 0.01 us -> 0.85 us  [the longest x1 0.84 us: local_square(): lax.ppermute(unit, 'cols', pairs)]
  transfers between devices with their start and end apart: 10 -> 10, of which waited for: 6 -> 5; matrix products, arithmetic and copies ran while one was open for 0% -> 0% of each run, Pallas kernels for 9% -> 9%
where the time goes in v6:
time: 32.1 us; the launch traced here: 31.9 us
  starting transfers between devices  17.1 us (53%)
  waiting for transfers between devices  7.76 us (24%)
  Pallas kernels  6.37 us (20%)
  between operations  0.71 us (2%)
    ppermute x6, starting transfers between devices, exchange(): got[k] = lax.ppermute(messages[k], axis, [(p, p ^ k) for p in range(size)])  10.4 us
    ppermute x6, waiting for transfers between devices, exchange(): got[k] = lax.ppermute(messages[k], axis, [(p, p ^ k) for p in range(size)])  6.91 us
    pallas_call x9, Pallas kernels, run(): pl.pallas_call(kernel, out_shape=out_shape, in_specs=[place] * len(args),...  6.37 us
    ppermute x1, starting transfers between devices, local_square(): across = lax.ppermute(halves, 'cols', [(p, p ^ 2) for p in range(cols)])  2.88 us
    ppermute x1, starting transfers between devices, local_square(): cols_b = lax.ppermute(halves, ('rows', 'cols'), from_second)  2.59 us
    ppermute x1, waiting for transfers between devices, local_square(): lax.ppermute(unit, 'cols', pairs)  0.84 us
    ppermute x1, starting transfers between devices, local_square(): cols_a = lax.ppermute(halves, ('rows', 'cols'), from_first)  0.65 us
  transfers between devices with their start and end apart: 10, of which 5 were waited for; matrix products, arithmetic and copies ran while one was open for 0% of the time, Pallas kernels for 9%

profile of v6, /device:TPU:0, one launch (start us, length us, event | category | flops | bytes accessed | tf_op | source)
XLA Modules:
  0.0 31.9 jit_solution(10586137879748968581)
XLA Ops:
  0.6 1.2 %shard_map.119 = (bf16[64,128]{1,0:T(8,128)(2,1)S(1)}, f32[128,64]{1,0:T(8,128)S(1)}, f32[128,64]{1,0:T(8,128)S(1)}, f32[1,64]{1,0:T(1,128)S(1)}, bf16[16,16,128...) custom-call(f32[16,8,64]{2,1,0:T(8,128)} %refs_0_.1, ...), custom_call_target="tpu_custom_call" | custom-call | tf_op jit(solution)/shard_map/pallas_call | solution.py:174
  1.8 0.6 %collective-permute-start = (bf16[64,128]{1,0:T(8,128)(2,1)S(1)}, bf16[64,128]{1,0:T(8,128)(2,1)S(1)}, u32[]{:S(2)}, u32[]{:S(2)}) collective-permute-start(bf16[64,128]{1,0:T(8,128)(2,1)S(1)} %get-tuple-element.36.own_ref), channel_id=1, source_target_pairs={{0,1},{1,0},{2,3},{3,2},{4,5},{5,4},{6,7},{7,6},{8,9},{9,8},{10,11... | collective-permute-start | bytes 49160 | tf_op jit(solution)/shard_map/ppermute | solution.py:578
  2.4 0.8 %collective-permute-done.other_ref = bf16[64,128]{1,0:T(8,128)(2,1)S(1)} collective-permute-done((bf16[64,128]{1,0:T(8,128)(2,1)S(1)}, bf16[64,128]{1,0:T(8,128)(2,1)S(1)}, u32[]{:S(2)}, u32[]{:S(2)}) %collective-permute-start) | collective-permute-done | bytes 16416 | tf_op jit(solution)/shard_map/ppermute | solution.py:578
  3.2 2.9 %collective-permute-start.3 = (bf16[128,128]{1,0:T(8,128)(2,1)S(1)}, bf16[128,128]{1,0:T(8,128)(2,1)S(1)}, u32[]{:S(2)}, u32[]{:S(2)}) collective-permute-start(bf16[128,128]{1,0:T(8,128)(2,1)S(1)} %shard_map.120.u0), channel_id=1, source_target_pairs={{0,2},{1,3},{2,0},{3,1},{4,6},{5,7},{6,4},{7,5},{8,10},{9,11},{10,... | collective-permute-start | bytes 98312 | tf_op jit(solution)/shard_map/ppermute | solution.py:582
  6.1 2.6 %collective-permute-start.2 = (bf16[128,128]{1,0:T(8,128)(2,1)S(1)}, bf16[128,128]{1,0:T(8,128)(2,1)S(1)}, u32[]{:S(2)}, u32[]{:S(2)}) collective-permute-start(bf16[128,128]{1,0:T(8,128)(2,1)S(1)} %shard_map.120.u0), channel_id=1, source_target_pairs={{0,8},{1,12},{2,0},{3,4},{4,9},{5,13},{6,1},{7,5},{8,10},{9,14},{1... | collective-permute-start | bytes 98312 | tf_op jit(solution)/shard_map/ppermute | solution.py:581
  8.7 0.7 %collective-permute-start.1 = (bf16[128,128]{1,0:T(8,128)(2,1)S(1)}, bf16[128,128]{1,0:T(8,128)(2,1)S(1)}, u32[]{:S(2)}, u32[]{:S(2)}) collective-permute-start(bf16[128,128]{1,0:T(8,128)(2,1)S(1)} %shard_map.120.u0), channel_id=1, source_target_pairs={{0,0},{1,4},{2,8},{3,12},{4,1},{5,5},{6,9},{7,13},{8,2},{9,6},{10,... | collective-permute-start | bytes 98312 | tf_op jit(solution)/shard_map/ppermute | solution.py:580
  9.4 0.9 %shard_map.121 = (bf16[128,2048]{1,0:T(8,128)(2,1)S(1)}, bf16[128,2048]{1,0:T(8,128)(2,1)S(1)}, bf16[256,128]{1,0:T(8,128)(2,1)S(1)}, bf16[4,512,128]{2,1,0:T(8,128)(2,1)S(1)}, bf16[512,512]{1,0:T(8,128)(2,1)S(1)}) custom-call(bf16[16,16,128]{2,1,0:T(8,128)(2,1)S(1)} %get-tuple-element.37.cot_ref, bf16[1024,128]{1,0:T(8,128)(2,1)S(1)} %get-tuple-element.38.final_ref, ...), custom_call_target="tpu_custom_call" | custom-call | flops 268435456 | tf_op jit(solution)/shard_map/pallas_call | solution.py:174
  10.3 0.0 collective-permute-done.3.u1
  10.3 0.8 %shard_map.122 = (bf16[128,128]{1,0:T(8,128)(2,1)S(1)}, bf16[128,256]{1,0:T(8,128)(2,1)S(1)}, f32[4,32,128]{2,1,0:T(8,128)S(1)}) custom-call(bf16[128,128]{1,0:T(8,128)(2,1)S(1)} %shard_map.120.u0, bf16[128,128]{1,0:T(8,128)(2,1)S(1)} %collective-permute-done.3.u1, bf16[4,512,128]{2,1,0:T(8,128)(2,1)S(1)} %get-tuple-element.41.weight_ref, ...), custom_call_target="tpu_custom_call" | custom-call | flops 100000000 | tf_op jit(solution)/shard_map/pallas_call | solution.py:174
  11.1 0.0 collective-permute-done.2.u1
  11.1 0.0 collective-permute-done.1.u0
  11.1 1.4 %shard_map.123 = (bf16[256,1024]{1,0:T(8,128)(2,1)S(1)}, f32[384,128]{1,0:T(8,128)S(1)}, bf16[384,128]{1,0:T(8,128)(2,1)S(1)}, bf16[384,128]{1,0:T(8,128)(2,1)S(1)}, bf16[384,128]{1,0:T(8,128)(2,1)S(1)}) custom-call(bf16[128,128]{1,0:T(8,128)(2,1)S(1)} %collective-permute-done.1.u0, bf16[128,128]{1,0:T(8,128)(2,1)S(1)} %collective-permute-done.2.u1, ...), custom_call_target="tpu_custom_call" | custom-call | tf_op jit(solution)/shard_map/pallas_call | solution.py:174
  12.5 5.7 %collective-permute-start.4 = (bf16[384,128]{1,0:T(8,128)(2,1)S(1)}, bf16[384,128]{1,0:T(8,128)(2,1)S(1)}, u32[]{:S(2)}, u32[]{:S(2)}) collective-permute-start(bf16[384,128]{1,0:T(8,128)(2,1)S(1)} %get-tuple-element.52), channel_id=1, source_target_pairs={{0,3},{1,2},{2,1},{3,0},{4,7},{5,6},{6,5},{7,4},{8,11},{9,10},{10,... | collective-permute-start | bytes 294920 | tf_op jit(solution)/shard_map/ppermute | solution.py:505
  18.3 0.0 collective-permute-start.5
  18.3 0.2 collective-permute-start.6
  18.5 3.0 %collective-permute-done.4.r3 = bf16[384,128]{1,0:T(8,128)(2,1)S(1)} collective-permute-done((bf16[384,128]{1,0:T(8,128)(2,1)S(1)}, bf16[384,128]{1,0:T(8,128)(2,1)S(1)}, u32[]{:S(2)}, u32[]{:S(2)}) %collective-permute-start.4) | collective-permute-done | bytes 98336 | tf_op jit(solution)/shard_map/ppermute | solution.py:505
  21.4 2.3 %collective-permute-done.5.r2 = bf16[384,128]{1,0:T(8,128)(2,1)S(1)} collective-permute-done((bf16[384,128]{1,0:T(8,128)(2,1)S(1)}, bf16[384,128]{1,0:T(8,128)(2,1)S(1)}, u32[]{:S(2)}, u32[]{:S(2)}) %collective-permute-start.5) | collective-permute-done | bytes 98336 | tf_op jit(solution)/shard_map/ppermute | solution.py:505
  23.7 0.0 collective-permute-done.6.r1
  23.7 0.1 shard_map.125
  23.8 1.6 %collective-permute-start.7 = (bf16[160,128]{1,0:T(8,128)(2,1)S(1)}, bf16[160,128]{1,0:T(8,128)(2,1)S(1)}, u32[]{:S(2)}, u32[]{:S(2)}) collective-permute-start(bf16[160,128]{1,0:T(8,128)(2,1)S(1)} %get-tuple-element.56), channel_id=1, source_target_pairs={{0,12},{4,8},{8,4},{12,0},{1,13},{5,9},{9,5},{13,1},{2,14},{6,10},... | collective-permute-start | bytes 122888 | tf_op jit(solution)/shard_map/ppermute | solution.py:505
  25.4 0.7 %collective-permute-start.8 = (bf16[160,128]{1,0:T(8,128)(2,1)S(1)}, bf16[160,128]{1,0:T(8,128)(2,1)S(1)}, u32[]{:S(2)}, u32[]{:S(2)}) collective-permute-start(bf16[160,128]{1,0:T(8,128)(2,1)S(1)} %get-tuple-element.57), channel_id=1, source_target_pairs={{0,8},{4,12},{8,0},{12,4},{1,9},{5,13},{9,1},{13,5},{2,10},{6,14},... | collective-permute-start | bytes 122888 | tf_op jit(solution)/shard_map/ppermute | solution.py:505
  26.1 2.2 %collective-permute-start.9 = (bf16[160,128]{1,0:T(8,128)(2,1)S(1)}, bf16[160,128]{1,0:T(8,128)(2,1)S(1)}, u32[]{:S(2)}, u32[]{:S(2)}) collective-permute-start(bf16[160,128]{1,0:T(8,128)(2,1)S(1)} %get-tuple-element.58), channel_id=1, source_target_pairs={{0,4},{4,0},{8,12},{12,8},{1,5},{5,1},{9,13},{13,9},{2,6},{6,2},{1... | collective-permute-start | bytes 122888 | tf_op jit(solution)/shard_map/ppermute | solution.py:505
  28.3 1.0 %shard_map.124 = bf16[16,16,128]{2,1,0:T(8,128)(2,1)} custom-call(bf16[256,1024]{1,0:T(8,128)(2,1)S(1)} %get-tuple-element.49.outer_ref, bf16[1024,128]{1,0:T(8,128)(2,1)S(1)} %get-tuple-element.38.final_ref, f32[1,128]{1,0:T(1,128)S(1)} %get-tuple-element.50.bias_ref), custom_call_target="tpu_custom_call" | custom-call | flops 100000000 | tf_op jit(solution)/shard_map/pallas_call | solution.py:174
  29.2 0.1 shard_map.126.unit_ref
  29.3 0.8 %collective-permute-done.7.r3 = bf16[160,128]{1,0:T(8,128)(2,1)S(1)} collective-permute-done((bf16[160,128]{1,0:T(8,128)(2,1)S(1)}, bf16[160,128]{1,0:T(8,128)(2,1)S(1)}, u32[]{:S(2)}, u32[]{:S(2)}) %collective-permute-start.7) | collective-permute-done | bytes 40992 | tf_op jit(solution)/shard_map/ppermute | solution.py:505
  30.1 0.8 %collective-permute-done.8.r2 = bf16[160,128]{1,0:T(8,128)(2,1)S(1)} collective-permute-done((bf16[160,128]{1,0:T(8,128)(2,1)S(1)}, bf16[160,128]{1,0:T(8,128)(2,1)S(1)}, u32[]{:S(2)}, u32[]{:S(2)}) %collective-permute-start.8) | collective-permute-done | bytes 40992 | tf_op jit(solution)/shard_map/ppermute | solution.py:505
  31.0 0.0 collective-permute-done.9.r1
  31.0 0.9 %shard_map.127 = (f32[64,128]{1,0:T(8,128)}, f32[32,64]{1,0:T(8,128)}, f32[32,64]{1,0:T(8,128)}, f32[16,8,64]{2,1,0:T(8,128)}) custom-call(f32[160,128]{1,0:T(8,128)S(1)} %get-tuple-element.55.own_ref, bf16[160,128]{1,0:T(8,128)(2,1)S(1)} %collective-permute-done.7.r3, bf16[160,128]{1,0:T(8,128)(2,1)S(1)} %collective-permute-done.8.r2, ...), custom_call_target="tpu_custom_call" | custom-call | tf_op jit(solution)/shard_map/pallas_call | solution.py:174
  (1 shorter events, 0.0 us)
Async XLA Ops:
  1.8 1.4 %collective-permute-start = (bf16[64,128]{1,0:T(8,128)(2,1)S(1)}, bf16[64,128]{1,0:T(8,128)(2,1)S(1)}, u32[]{:S(2)}, u32[]{:S(2)}) collective-permute-start(bf16[64,128]{1,0:T(8,128)(2,1)S(1)} %get-tuple-element.36.own_ref), channel_id=1, source_target_pairs={{0,1},{1,0},{2,3},{3,2},{4,5},{5,4},{6,7},{7,6},{8,9},{9,8},{10,11... | collective-permute-start | bytes 49160 | tf_op jit(solution)/shard_map/ppermute | solution.py:578
  3.2 7.0 %collective-permute-start.3 = (bf16[128,128]{1,0:T(8,128)(2,1)S(1)}, bf16[128,128]{1,0:T(8,128)(2,1)S(1)}, u32[]{:S(2)}, u32[]{:S(2)}) collective-permute-start(bf16[128,128]{1,0:T(8,128)(2,1)S(1)} %shard_map.120.u0), channel_id=1, source_target_pairs={{0,2},{1,3},{2,0},{3,1},{4,6},{5,7},{6,4},{7,5},{8,10},{9,11},{10,... | collective-permute-start | bytes 98312 | tf_op jit(solution)/shard_map/ppermute | solution.py:582
  6.1 5.0 %collective-permute-start.2 = (bf16[128,128]{1,0:T(8,128)(2,1)S(1)}, bf16[128,128]{1,0:T(8,128)(2,1)S(1)}, u32[]{:S(2)}, u32[]{:S(2)}) collective-permute-start(bf16[128,128]{1,0:T(8,128)(2,1)S(1)} %shard_map.120.u0), channel_id=1, source_target_pairs={{0,8},{1,12},{2,0},{3,4},{4,9},{5,13},{6,1},{7,5},{8,10},{9,14},{1... | collective-permute-start | bytes 98312 | tf_op jit(solution)/shard_map/ppermute | solution.py:581
  8.7 2.4 %collective-permute-start.1 = (bf16[128,128]{1,0:T(8,128)(2,1)S(1)}, bf16[128,128]{1,0:T(8,128)(2,1)S(1)}, u32[]{:S(2)}, u32[]{:S(2)}) collective-permute-start(bf16[128,128]{1,0:T(8,128)(2,1)S(1)} %shard_map.120.u0), channel_id=1, source_target_pairs={{0,0},{1,4},{2,8},{3,12},{4,1},{5,5},{6,9},{7,13},{8,2},{9,6},{10,... | collective-permute-start | bytes 98312 | tf_op jit(solution)/shard_map/ppermute | solution.py:580
  12.5 8.9 %collective-permute-start.4 = (bf16[384,128]{1,0:T(8,128)(2,1)S(1)}, bf16[384,128]{1,0:T(8,128)(2,1)S(1)}, u32[]{:S(2)}, u32[]{:S(2)}) collective-permute-start(bf16[384,128]{1,0:T(8,128)(2,1)S(1)} %get-tuple-element.52), channel_id=1, source_target_pairs={{0,3},{1,2},{2,1},{3,0},{4,7},{5,6},{6,5},{7,4},{8,11},{9,10},{10,... | collective-permute-start | bytes 294920 | tf_op jit(solution)/shard_map/ppermute | solution.py:505
  18.3 5.5 %collective-permute-start.5 = (bf16[384,128]{1,0:T(8,128)(2,1)S(1)}, bf16[384,128]{1,0:T(8,128)(2,1)S(1)}, u32[]{:S(2)}, u32[]{:S(2)}) collective-permute-start(bf16[384,128]{1,0:T(8,128)(2,1)S(1)} %get-tuple-element.53), channel_id=1, source_target_pairs={{0,2},{1,3},{2,0},{3,1},{4,6},{5,7},{6,4},{7,5},{8,10},{9,11},{10,... | collective-permute-start | bytes 294920 | tf_op jit(solution)/shard_map/ppermute | solution.py:505
  18.3 5.5 %collective-permute-start.6 = (bf16[384,128]{1,0:T(8,128)(2,1)S(1)}, bf16[384,128]{1,0:T(8,128)(2,1)S(1)}, u32[]{:S(2)}, u32[]{:S(2)}) collective-permute-start(bf16[384,128]{1,0:T(8,128)(2,1)S(1)} %get-tuple-element.54), channel_id=1, source_target_pairs={{0,1},{1,0},{2,3},{3,2},{4,5},{5,4},{6,7},{7,6},{8,9},{9,8},{10,11... | collective-permute-start | bytes 294920 | tf_op jit(solution)/shard_map/ppermute | solution.py:505
  23.8 6.3 %collective-permute-start.7 = (bf16[160,128]{1,0:T(8,128)(2,1)S(1)}, bf16[160,128]{1,0:T(8,128)(2,1)S(1)}, u32[]{:S(2)}, u32[]{:S(2)}) collective-permute-start(bf16[160,128]{1,0:T(8,128)(2,1)S(1)} %get-tuple-element.56), channel_id=1, source_target_pairs={{0,12},{4,8},{8,4},{12,0},{1,13},{5,9},{9,5},{13,1},{2,14},{6,10},... | collective-permute-start | bytes 122888 | tf_op jit(solution)/shard_map/ppermute | solution.py:505
  25.4 5.6 %collective-permute-start.8 = (bf16[160,128]{1,0:T(8,128)(2,1)S(1)}, bf16[160,128]{1,0:T(8,128)(2,1)S(1)}, u32[]{:S(2)}, u32[]{:S(2)}) collective-permute-start(bf16[160,128]{1,0:T(8,128)(2,1)S(1)} %get-tuple-element.57), channel_id=1, source_target_pairs={{0,8},{4,12},{8,0},{12,4},{1,9},{5,13},{9,1},{13,5},{2,10},{6,14},... | collective-permute-start | bytes 122888 | tf_op jit(solution)/shard_map/ppermute | solution.py:505
  26.1 4.9 %collective-permute-start.9 = (bf16[160,128]{1,0:T(8,128)(2,1)S(1)}, bf16[160,128]{1,0:T(8,128)(2,1)S(1)}, u32[]{:S(2)}, u32[]{:S(2)}) collective-permute-start(bf16[160,128]{1,0:T(8,128)(2,1)S(1)} %get-tuple-element.58), channel_id=1, source_target_pairs={{0,4},{4,0},{8,12},{12,8},{1,5},{5,1},{9,13},{13,9},{2,6},{6,2},{1... | collective-permute-start | bytes 122888 | tf_op jit(solution)/shard_map/ppermute | solution.py:505

commit v7 on v6

--- a/solution.py
+++ b/solution.py
@@ -402,9 +402,13 @@
         slope(turned_ref[...], lefts, per, chans),
         slope(unit.astype(F32).T.astype(BF16), rights, per, chans),
     ]
-    width = sides[0].shape[0]
     sides = [s + pltpu.roll(s, LANES // 2, 1) for s in sides]
-    slopes = jnp.where(lane_group((width, LANES), LANES // 2) == 0, sides[0], sides[1])
+    sides = [s + pltpu.roll(s, LANES // 4, 1) for s in sides]
+    width = sides[0].shape[0] // 2
+    slopes = pick(
+        [side[h * width : (h + 1) * width] for h in range(2) for side in sides],
+        lane_group((width, LANES), chans),
+    )
     for k, ref in enumerate((own_ref, m1, m2, m3)):
         peer = mine ^ k
         kind = ref.dtype
@@ -491,11 +495,9 @@
     slopes = total[share + span :].T
     chans = second_ref.shape[0]
     for x, ref in enumerate((first_slope_ref, second_slope_ref)):
-        side = slopes[x * LANES // 2 : (x + 1) * LANES // 2]
-        out = side[:chans]
-        for b in range(1, LANES // 2 // chans):
-            out = out + side[b * chans : (b + 1) * chans]
-        ref[...] = out
+        ref[...] = jnp.concatenate(
+            [slopes[(2 * h + x) * chans : (2 * h + x + 1) * chans] for h in range(2)], axis=1
+        )
 
 
 def exchange(messages, axis, order):
@@ -529,7 +531,11 @@
     return first, second, mask
 
 
-def local_square(
+def local_square(*args):
+    return local_square_(*args)
+
+
+def local_square_(
     alignment_features,
     affine_factor,
     affine_offset,
@@ -570,17 +576,17 @@
         + [pltpu.SemaphoreType.DMA((len(inputs),))],
         space=pltpu.HBM,
     )(*[pltpu.with_memory_space_constraint(i, pltpu.HBM) for i in inputs])
-    pairs = [(p, p ^ 1) for p in range(cols)]
+    partner = lax.ppermute(unit, "cols", [(p, p ^ 1) for p in range(cols)])
     halves = call(
         half_kernel,
         shape((half * seqs // 2, 2 * width), BF16),
         [pltpu.VMEM((half, seqs // 2, 2 * width), F32)],
-    )(unit, lax.ppermute(unit, "cols", pairs))
+    )(unit, partner)
     from_first, from_second, first_halves = holders(rows, cols)
     cols_a = lax.ppermute(halves, ("rows", "cols"), from_first)
     cols_b = lax.ppermute(halves, ("rows", "cols"), from_second)
     across = lax.ppermute(halves, "cols", [(p, p ^ 2) for p in range(cols)])
-    by_col, by_row, cot_cols, weight, order = call(
+    grad = call(
         functools.partial(grad_kernel, chans=chans),
         (
             shape((tall, wide), BF16),
@@ -591,7 +597,8 @@
         ),
         [pltpu.VMEM(adjoint_update.shape, F32), pltpu.VMEM((total, pair_ch), F32)],
         flops=8 * tokens * tokens * total * pair_ch,
-    )(cot, final, first, second)
+    )
+    by_col, by_row, cot_cols, weight, order = grad(cot, final, first, second)
     left, turned, part = call(
         functools.partial(left_kernel, chans=chans),
         (
@@ -603,7 +610,7 @@
         flops=10**8,
     )(halves, across, weight, order, by_col)
     span = groups * quarter
-    message = rows * share + 2 * span + width
+    message = rows * share + 2 * span + width // 2
     outer, own, *messages = call(
         functools.partial(
             pair_kernel, chans=chans, sizes=(rows, cols), first_halves=first_halves
@@ -628,7 +635,7 @@
         [pltpu.VMEM((tokens, tokens, pair_ch), F32)],
         flops=10**8,
     )(outer, final, bias)
-    message = share + span + width
+    message = share + span + width // 2
     back, own, *messages = call(
         functools.partial(between_kernel, rows=rows, share=share),
         (
@@ -637,7 +644,7 @@
             *[shape((message, LANES), BF16)] * (rows - 1),
         ),
         [
-            pltpu.VMEM((rows * share + 2 * span + width, LANES), F32),
+            pltpu.VMEM((rows * share + 2 * span + width // 2, LANES), F32),
             pltpu.VMEM((cols, span, LANES), F32),
         ],
     )(own, *got[::-1])

time: 32.1 us -> 31.4 us (0.978)
  waiting for transfers between devices: 7.76 us -> 7.03 us
    ppermute x6, waiting for transfers between devices: 6.91 us -> 6.18 us  [exchange(): got[k] = lax.ppermute(messages[k], axis, [(p, p ^ k) for p in range(size)])]
  transfers between devices with their start and end apart: 10 -> 10, of which waited for: 5 -> 6; matrix products, arithmetic and copies ran while one was open for 0% -> 0% of each run, Pallas kernels for 9% -> 9%
where the time goes in v7:
time: 31.4 us; the launch traced here: 31.3 us
  starting transfers between devices  17.1 us (54%)
  waiting for transfers between devices  7.03 us (22%)
  Pallas kernels  6.47 us (21%)
  between operations  0.7 us (2%)
    ppermute x6, starting transfers between devices, exchange(): got[k] = lax.ppermute(messages[k], axis, [(p, p ^ k) for p in range(size)])  10.4 us
    pallas_call x9, Pallas kernels, run(): pl.pallas_call(kernel, out_shape=out_shape, in_specs=[place] * len(args),...  6.47 us
    ppermute x6, waiting for transfers between devices, exchange(): got[k] = lax.ppermute(messages[k], axis, [(p, p ^ k) for p in range(size)])  6.18 us
    ppermute x1, starting transfers between devices, local_square_(): across = lax.ppermute(halves, 'cols', [(p, p ^ 2) for p in range(cols)])  2.88 us
    ppermute x1, starting transfers between devices, local_square_(): cols_b = lax.ppermute(halves, ('rows', 'cols'), from_second)  2.59 us
    ppermute x1, waiting for transfers between devices, local_square_(): partner = lax.ppermute(unit, 'cols', [(p, p ^ 1) for p in range(cols)])  0.84 us
    ppermute x1, starting transfers between devices, local_square_(): cols_a = lax.ppermute(halves, ('rows', 'cols'), from_first)  0.65 us
  transfers between devices with their start and end apart: 10, of which 6 were waited for; matrix products, arithmetic and copies ran while one was open for 0% of the time, Pallas kernels for 9%

profile of v7, /device:TPU:0, one launch (start us, length us, event | category | flops | bytes accessed | tf_op | source)
XLA Modules:
  0.0 31.3 jit_solution(11644791203743945038)
XLA Ops:
  0.6 1.2 %shard_map.119 = (bf16[64,128]{1,0:T(8,128)(2,1)S(1)}, f32[128,64]{1,0:T(8,128)S(1)}, f32[128,64]{1,0:T(8,128)S(1)}, f32[1,64]{1,0:T(1,128)S(1)}, bf16[16,16,128...) custom-call(f32[16,8,64]{2,1,0:T(8,128)} %refs_0_.1, ...), custom_call_target="tpu_custom_call" | custom-call | tf_op jit(solution)/shard_map/pallas_call | solution.py:174
  1.8 0.6 %collective-permute-start = (bf16[64,128]{1,0:T(8,128)(2,1)S(1)}, bf16[64,128]{1,0:T(8,128)(2,1)S(1)}, u32[]{:S(2)}, u32[]{:S(2)}) collective-permute-start(bf16[64,128]{1,0:T(8,128)(2,1)S(1)} %get-tuple-element.36.own_ref), channel_id=1, source_target_pairs={{0,1},{1,0},{2,3},{3,2},{4,5},{5,4},{6,7},{7,6},{8,9},{9,8},{10,11... | collective-permute-start | bytes 49160 | tf_op jit(solution)/shard_map/ppermute | solution.py:579
  2.4 0.8 %collective-permute-done.other_ref = bf16[64,128]{1,0:T(8,128)(2,1)S(1)} collective-permute-done((bf16[64,128]{1,0:T(8,128)(2,1)S(1)}, bf16[64,128]{1,0:T(8,128)(2,1)S(1)}, u32[]{:S(2)}, u32[]{:S(2)}) %collective-permute-start) | collective-permute-done | bytes 16416 | tf_op jit(solution)/shard_map/ppermute | solution.py:579
  3.2 2.9 %collective-permute-start.3 = (bf16[128,128]{1,0:T(8,128)(2,1)S(1)}, bf16[128,128]{1,0:T(8,128)(2,1)S(1)}, u32[]{:S(2)}, u32[]{:S(2)}) collective-permute-start(bf16[128,128]{1,0:T(8,128)(2,1)S(1)} %shard_map.120.u0), channel_id=1, source_target_pairs={{0,2},{1,3},{2,0},{3,1},{4,6},{5,7},{6,4},{7,5},{8,10},{9,11},{10,... | collective-permute-start | bytes 98312 | tf_op jit(solution)/shard_map/ppermute | solution.py:588
  6.1 2.6 %collective-permute-start.2 = (bf16[128,128]{1,0:T(8,128)(2,1)S(1)}, bf16[128,128]{1,0:T(8,128)(2,1)S(1)}, u32[]{:S(2)}, u32[]{:S(2)}) collective-permute-start(bf16[128,128]{1,0:T(8,128)(2,1)S(1)} %shard_map.120.u0), channel_id=1, source_target_pairs={{0,8},{1,12},{2,0},{3,4},{4,9},{5,13},{6,1},{7,5},{8,10},{9,14},{1... | collective-permute-start | bytes 98312 | tf_op jit(solution)/shard_map/ppermute | solution.py:587
  8.7 0.7 %collective-permute-start.1 = (bf16[128,128]{1,0:T(8,128)(2,1)S(1)}, bf16[128,128]{1,0:T(8,128)(2,1)S(1)}, u32[]{:S(2)}, u32[]{:S(2)}) collective-permute-start(bf16[128,128]{1,0:T(8,128)(2,1)S(1)} %shard_map.120.u0), channel_id=1, source_target_pairs={{0,0},{1,4},{2,8},{3,12},{4,1},{5,5},{6,9},{7,13},{8,2},{9,6},{10,... | collective-permute-start | bytes 98312 | tf_op jit(solution)/shard_map/ppermute | solution.py:586
  9.4 0.9 %shard_map.121 = (bf16[128,2048]{1,0:T(8,128)(2,1)S(1)}, bf16[128,2048]{1,0:T(8,128)(2,1)S(1)}, bf16[256,128]{1,0:T(8,128)(2,1)S(1)}, bf16[4,512,128]{2,1,0:T(8,128)(2,1)S(1)}, bf16[512,512]{1,0:T(8,128)(2,1)S(1)}) custom-call(bf16[16,16,128]{2,1,0:T(8,128)(2,1)S(1)} %get-tuple-element.37.cot_ref, bf16[1024,128]{1,0:T(8,128)(2,1)S(1)} %get-tuple-element.38.final_ref, ...), custom_call_target="tpu_custom_call" | custom-call | flops 268435456 | tf_op jit(solution)/shard_map/pallas_call | solution.py:174
  10.3 0.0 collective-permute-done.3.u1
  10.3 0.8 %shard_map.122 = (bf16[128,128]{1,0:T(8,128)(2,1)S(1)}, bf16[128,256]{1,0:T(8,128)(2,1)S(1)}, f32[4,32,128]{2,1,0:T(8,128)S(1)}) custom-call(bf16[128,128]{1,0:T(8,128)(2,1)S(1)} %shard_map.120.u0, bf16[128,128]{1,0:T(8,128)(2,1)S(1)} %collective-permute-done.3.u1, bf16[4,512,128]{2,1,0:T(8,128)(2,1)S(1)} %get-tuple-element.41.weight_ref, ...), custom_call_target="tpu_custom_call" | custom-call | flops 100000000 | tf_op jit(solution)/shard_map/pallas_call | solution.py:174
  11.1 0.0 collective-permute-done.2.u1
  11.1 0.0 collective-permute-done.1.u0
  11.1 1.5 %shard_map.123 = (bf16[256,1024]{1,0:T(8,128)(2,1)S(1)}, f32[352,128]{1,0:T(8,128)S(1)}, bf16[352,128]{1,0:T(8,128)(2,1)S(1)}, bf16[352,128]{1,0:T(8,128)(2,1)S(1)}, bf16[352,128]{1,0:T(8,128)(2,1)S(1)}) custom-call(bf16[128,128]{1,0:T(8,128)(2,1)S(1)} %collective-permute-done.1.u0, bf16[128,128]{1,0:T(8,128)(2,1)S(1)} %collective-permute-done.2.u1, ...), custom_call_target="tpu_custom_call" | custom-call | tf_op jit(solution)/shard_map/pallas_call | solution.py:174
  12.6 5.7 %collective-permute-start.4 = (bf16[352,128]{1,0:T(8,128)(2,1)S(1)}, bf16[352,128]{1,0:T(8,128)(2,1)S(1)}, u32[]{:S(2)}, u32[]{:S(2)}) collective-permute-start(bf16[352,128]{1,0:T(8,128)(2,1)S(1)} %get-tuple-element.52), channel_id=1, source_target_pairs={{0,3},{1,2},{2,1},{3,0},{4,7},{5,6},{6,5},{7,4},{8,11},{9,10},{10,... | collective-permute-start | bytes 270344 | tf_op jit(solution)/shard_map/ppermute | solution.py:507
  18.3 0.0 collective-permute-start.5
  18.3 0.2 collective-permute-start.6
  18.5 2.8 %collective-permute-done.4.r3 = bf16[352,128]{1,0:T(8,128)(2,1)S(1)} collective-permute-done((bf16[352,128]{1,0:T(8,128)(2,1)S(1)}, bf16[352,128]{1,0:T(8,128)(2,1)S(1)}, u32[]{:S(2)}, u32[]{:S(2)}) %collective-permute-start.4) | collective-permute-done | bytes 90144 | tf_op jit(solution)/shard_map/ppermute | solution.py:507
  21.3 2.1 %collective-permute-done.5.r2 = bf16[352,128]{1,0:T(8,128)(2,1)S(1)} collective-permute-done((bf16[352,128]{1,0:T(8,128)(2,1)S(1)}, bf16[352,128]{1,0:T(8,128)(2,1)S(1)}, u32[]{:S(2)}, u32[]{:S(2)}) %collective-permute-start.5) | collective-permute-done | bytes 90144 | tf_op jit(solution)/shard_map/ppermute | solution.py:507
  23.4 0.0 collective-permute-done.6.r1
  23.4 0.1 shard_map.125
  23.5 1.7 %collective-permute-start.7 = (bf16[128,128]{1,0:T(8,128)(2,1)S(1)}, bf16[128,128]{1,0:T(8,128)(2,1)S(1)}, u32[]{:S(2)}, u32[]{:S(2)}) collective-permute-start(bf16[128,128]{1,0:T(8,128)(2,1)S(1)} %get-tuple-element.56), channel_id=1, source_target_pairs={{0,12},{4,8},{8,4},{12,0},{1,13},{5,9},{9,5},{13,1},{2,14},{6,10},... | collective-permute-start | bytes 98312 | tf_op jit(solution)/shard_map/ppermute | solution.py:507
  25.2 0.6 %collective-permute-start.8 = (bf16[128,128]{1,0:T(8,128)(2,1)S(1)}, bf16[128,128]{1,0:T(8,128)(2,1)S(1)}, u32[]{:S(2)}, u32[]{:S(2)}) collective-permute-start(bf16[128,128]{1,0:T(8,128)(2,1)S(1)} %get-tuple-element.57), channel_id=1, source_target_pairs={{0,8},{4,12},{8,0},{12,4},{1,9},{5,13},{9,1},{13,5},{2,10},{6,14},... | collective-permute-start | bytes 98312 | tf_op jit(solution)/shard_map/ppermute | solution.py:507
  25.8 2.2 %collective-permute-start.9 = (bf16[128,128]{1,0:T(8,128)(2,1)S(1)}, bf16[128,128]{1,0:T(8,128)(2,1)S(1)}, u32[]{:S(2)}, u32[]{:S(2)}) collective-permute-start(bf16[128,128]{1,0:T(8,128)(2,1)S(1)} %get-tuple-element.58), channel_id=1, source_target_pairs={{0,4},{4,0},{8,12},{12,8},{1,5},{5,1},{9,13},{13,9},{2,6},{6,2},{1... | collective-permute-start | bytes 98312 | tf_op jit(solution)/shard_map/ppermute | solution.py:507
  28.0 1.0 %shard_map.124 = bf16[16,16,128]{2,1,0:T(8,128)(2,1)} custom-call(bf16[256,1024]{1,0:T(8,128)(2,1)S(1)} %get-tuple-element.49.outer_ref, bf16[1024,128]{1,0:T(8,128)(2,1)S(1)} %get-tuple-element.38.final_ref, f32[1,128]{1,0:T(1,128)S(1)} %get-tuple-element.50.bias_ref), custom_call_target="tpu_custom_call" | custom-call | flops 100000000 | tf_op jit(solution)/shard_map/pallas_call | solution.py:174
  28.9 0.1 shard_map.126.unit_ref
  29.1 0.7 %collective-permute-done.7.r3 = bf16[128,128]{1,0:T(8,128)(2,1)S(1)} collective-permute-done((bf16[128,128]{1,0:T(8,128)(2,1)S(1)}, bf16[128,128]{1,0:T(8,128)(2,1)S(1)}, u32[]{:S(2)}, u32[]{:S(2)}) %collective-permute-start.7) | collective-permute-done | bytes 32800 | tf_op jit(solution)/shard_map/ppermute | solution.py:507
  29.7 0.4 %collective-permute-done.8.r2 = bf16[128,128]{1,0:T(8,128)(2,1)S(1)} collective-permute-done((bf16[128,128]{1,0:T(8,128)(2,1)S(1)}, bf16[128,128]{1,0:T(8,128)(2,1)S(1)}, u32[]{:S(2)}, u32[]{:S(2)}) %collective-permute-start.8) | collective-permute-done | bytes 32800 | tf_op jit(solution)/shard_map/ppermute | solution.py:507
  30.1 0.2 collective-permute-done.9.r1
  30.3 1.0 %shard_map.127 = (f32[64,128]{1,0:T(8,128)}, f32[32,64]{1,0:T(8,128)}, f32[32,64]{1,0:T(8,128)}, f32[16,8,64]{2,1,0:T(8,128)}) custom-call(f32[128,128]{1,0:T(8,128)S(1)} %get-tuple-element.55.own_ref, bf16[128,128]{1,0:T(8,128)(2,1)S(1)} %collective-permute-done.7.r3, bf16[128,128]{1,0:T(8,128)(2,1)S(1)} %collective-permute-done.8.r2, ...), custom_call_target="tpu_custom_call" | custom-call | tf_op jit(solution)/shard_map/pallas_call | solution.py:174
  (1 shorter events, 0.0 us)
Async XLA Ops:
  1.8 1.4 %collective-permute-start = (bf16[64,128]{1,0:T(8,128)(2,1)S(1)}, bf16[64,128]{1,0:T(8,128)(2,1)S(1)}, u32[]{:S(2)}, u32[]{:S(2)}) collective-permute-start(bf16[64,128]{1,0:T(8,128)(2,1)S(1)} %get-tuple-element.36.own_ref), channel_id=1, source_target_pairs={{0,1},{1,0},{2,3},{3,2},{4,5},{5,4},{6,7},{7,6},{8,9},{9,8},{10,11... | collective-permute-start | bytes 49160 | tf_op jit(solution)/shard_map/ppermute | solution.py:579
  3.2 7.0 %collective-permute-start.3 = (bf16[128,128]{1,0:T(8,128)(2,1)S(1)}, bf16[128,128]{1,0:T(8,128)(2,1)S(1)}, u32[]{:S(2)}, u32[]{:S(2)}) collective-permute-start(bf16[128,128]{1,0:T(8,128)(2,1)S(1)} %shard_map.120.u0), channel_id=1, source_target_pairs={{0,2},{1,3},{2,0},{3,1},{4,6},{5,7},{6,4},{7,5},{8,10},{9,11},{10,... | collective-permute-start | bytes 98312 | tf_op jit(solution)/shard_map/ppermute | solution.py:588
  6.1 5.0 %collective-permute-start.2 = (bf16[128,128]{1,0:T(8,128)(2,1)S(1)}, bf16[128,128]{1,0:T(8,128)(2,1)S(1)}, u32[]{:S(2)}, u32[]{:S(2)}) collective-permute-start(bf16[128,128]{1,0:T(8,128)(2,1)S(1)} %shard_map.120.u0), channel_id=1, source_target_pairs={{0,8},{1,12},{2,0},{3,4},{4,9},{5,13},{6,1},{7,5},{8,10},{9,14},{1... | collective-permute-start | bytes 98312 | tf_op jit(solution)/shard_map/ppermute | solution.py:587
  8.7 2.4 %collective-permute-start.1 = (bf16[128,128]{1,0:T(8,128)(2,1)S(1)}, bf16[128,128]{1,0:T(8,128)(2,1)S(1)}, u32[]{:S(2)}, u32[]{:S(2)}) collective-permute-start(bf16[128,128]{1,0:T(8,128)(2,1)S(1)} %shard_map.120.u0), channel_id=1, source_target_pairs={{0,0},{1,4},{2,8},{3,12},{4,1},{5,5},{6,9},{7,13},{8,2},{9,6},{10,... | collective-permute-start | bytes 98312 | tf_op jit(solution)/shard_map/ppermute | solution.py:586
  12.6 8.7 %collective-permute-start.4 = (bf16[352,128]{1,0:T(8,128)(2,1)S(1)}, bf16[352,128]{1,0:T(8,128)(2,1)S(1)}, u32[]{:S(2)}, u32[]{:S(2)}) collective-permute-start(bf16[352,128]{1,0:T(8,128)(2,1)S(1)} %get-tuple-element.52), channel_id=1, source_target_pairs={{0,3},{1,2},{2,1},{3,0},{4,7},{5,6},{6,5},{7,4},{8,11},{9,10},{10,... | collective-permute-start | bytes 270344 | tf_op jit(solution)/shard_map/ppermute | solution.py:507
  18.3 5.1 %collective-permute-start.5 = (bf16[352,128]{1,0:T(8,128)(2,1)S(1)}, bf16[352,128]{1,0:T(8,128)(2,1)S(1)}, u32[]{:S(2)}, u32[]{:S(2)}) collective-permute-start(bf16[352,128]{1,0:T(8,128)(2,1)S(1)} %get-tuple-element.53), channel_id=1, source_target_pairs={{0,2},{1,3},{2,0},{3,1},{4,6},{5,7},{6,4},{7,5},{8,10},{9,11},{10,... | collective-permute-start | bytes 270344 | tf_op jit(solution)/shard_map/ppermute | solution.py:507
  18.3 5.1 %collective-permute-start.6 = (bf16[352,128]{1,0:T(8,128)(2,1)S(1)}, bf16[352,128]{1,0:T(8,128)(2,1)S(1)}, u32[]{:S(2)}, u32[]{:S(2)}) collective-permute-start(bf16[352,128]{1,0:T(8,128)(2,1)S(1)} %get-tuple-element.54), channel_id=1, source_target_pairs={{0,1},{1,0},{2,3},{3,2},{4,5},{5,4},{6,7},{7,6},{8,9},{9,8},{10,11... | collective-permute-start | bytes 270344 | tf_op jit(solution)/shard_map/ppermute | solution.py:507
  23.5 6.2 %collective-permute-start.7 = (bf16[128,128]{1,0:T(8,128)(2,1)S(1)}, bf16[128,128]{1,0:T(8,128)(2,1)S(1)}, u32[]{:S(2)}, u32[]{:S(2)}) collective-permute-start(bf16[128,128]{1,0:T(8,128)(2,1)S(1)} %get-tuple-element.56), channel_id=1, source_target_pairs={{0,12},{4,8},{8,4},{12,0},{1,13},{5,9},{9,5},{13,1},{2,14},{6,10},... | collective-permute-start | bytes 98312 | tf_op jit(solution)/shard_map/ppermute | solution.py:507
  25.2 4.8 %collective-permute-start.8 = (bf16[128,128]{1,0:T(8,128)(2,1)S(1)}, bf16[128,128]{1,0:T(8,128)(2,1)S(1)}, u32[]{:S(2)}, u32[]{:S(2)}) collective-permute-start(bf16[128,128]{1,0:T(8,128)(2,1)S(1)} %get-tuple-element.57), channel_id=1, source_target_pairs={{0,8},{4,12},{8,0},{12,4},{1,9},{5,13},{9,1},{13,5},{2,10},{6,14},... | collective-permute-start | bytes 98312 | tf_op jit(solution)/shard_map/ppermute | solution.py:507
  25.8 4.5 %collective-permute-start.9 = (bf16[128,128]{1,0:T(8,128)(2,1)S(1)}, bf16[128,128]{1,0:T(8,128)(2,1)S(1)}, u32[]{:S(2)}, u32[]{:S(2)}) collective-permute-start(bf16[128,128]{1,0:T(8,128)(2,1)S(1)} %get-tuple-element.58), channel_id=1, source_target_pairs={{0,4},{4,0},{8,12},{12,8},{1,5},{5,1},{9,13},{13,9},{2,6},{6,2},{1... | collective-permute-start | bytes 98312 | tf_op jit(solution)/shard_map/ppermute | solution.py:507

commit v8 on v7

--- a/solution.py
+++ b/solution.py
@@ -1,5 +1,4 @@
 import functools
-import itertools
 
 import jax
 import jax.numpy as jnp
@@ -452,7 +451,9 @@
     left_ref[...] = total_f[first : first + span, :]
     slopes = total_f[last:, :]
     for k, ref in enumerate((next_ref, m1, m2, m3)):
-        peer = mine ^ k
+        place = (mine ^ (mine >> 1)) + k
+        place = place % rows
+        peer = place ^ (place >> 1)
         at = pl.multiple_of(peer * share, share)
         ref[0:share, :] = total_f[pl.ds(at, share), :].astype(ref.dtype)
         ref[share : share + span, :] = right_f[peer].astype(ref.dtype)
@@ -504,26 +505,27 @@
     size = lax.axis_size(axis)
     got = {}
     for k in order:
-        got[k] = lax.ppermute(messages[k], axis, [(p, p ^ k) for p in range(size)])
+        if axis == "cols":
+            pairs = [(p, p ^ k) for p in range(size)]
+        else:
+            cycle = [p ^ (p >> 1) for p in range(size)]
+            pairs = [(cycle[p], cycle[(p + k) % size]) for p in range(size)]
+        got[k] = lax.ppermute(messages[k], axis, pairs)
     return [got[k] for k in sorted(got)]
 
 
-def holders(rows, cols):
+ROUTES = (
+    ((3, 2, 0, 1), (1, 0, 2, 3)),
+    ((0, 3, 2, 1), (1, 2, 0, 3)),
+    ((0, 3, 1, 2), (2, 1, 0, 3)),
+    ((1, 0, 3, 2), (2, 3, 0, 1)),
+)
+
+
+def holders(cols):
     first, second, mask = [], [], 0
-    for r in range(rows):
-
-        def hops(to):
-            return [abs(z - r) + (q // 2 != r // 2) for q, z in enumerate(to) if z != r]
-
-        best = None
-        for a in itertools.permutations(range(rows)):
-            for b in itertools.permutations(range(rows)):
-                if any(a.index(z) // 2 == b.index(z) // 2 for z in range(rows)):
-                    continue
-                cost = (max(hops(a) + hops(b)), sum(hops(a) + hops(b)))
-                if best is None or cost < best[0]:
-                    best = cost, a, b
-        _, a, b = best
+    for r, (a, b) in enumerate(ROUTES):
+        assert all(a.index(z) // 2 != b.index(z) // 2 for z in a)
         first += [(r * cols + q, z * cols + r) for q, z in enumerate(a)]
         second += [(r * cols + q, z * cols + r) for q, z in enumerate(b)]
         for q, z in enumerate(a):
@@ -582,7 +584,7 @@
         shape((half * seqs // 2, 2 * width), BF16),
         [pltpu.VMEM((half, seqs // 2, 2 * width), F32)],
     )(unit, partner)
-    from_first, from_second, first_halves = holders(rows, cols)
+    from_first, from_second, first_halves = holders(cols)
     cols_a = lax.ppermute(halves, ("rows", "cols"), from_first)
     cols_b = lax.ppermute(halves, ("rows", "cols"), from_second)
     across = lax.ppermute(halves, "cols", [(p, p ^ 2) for p in range(cols)])
@@ -670,7 +672,7 @@
     width, chans = first_projector.shape
     per = LANES // chans
     return (
-        rows == cols == 4
+        rows == cols == len(ROUTES)
         and chans * per == LANES
         and chans % per == 0
         and chans // per == SUBLANES

time: 31.4 us -> 30.7 us (0.978)
  starting transfers between devices: 17.1 us -> 13.9 us
  waiting for transfers between devices: 7.03 us -> 9.43 us
    ppermute x6, starting transfers between devices: 10.4 us -> 6.87 us  [exchange(): got[k] = lax.ppermute(messages[k], axis, pairs)]
    ppermute x6, waiting for transfers between devices: 6.18 us -> 7.97 us  [exchange(): got[k] = lax.ppermute(messages[k], axis, pairs)]
    ppermute x1, starting transfers between devices: 0.65 us -> 2.03 us  [local_square_(): cols_a = lax.ppermute(halves, ('rows', 'cols'), from_first)]
    ppermute x1, starting transfers between devices: 2.59 us -> 1.58 us  [local_square_(): cols_b = lax.ppermute(halves, ('rows', 'cols'), from_second)]
    ppermute x1, waiting for transfers between devices: 0.01 us -> 0.61 us  [local_square_(): cols_a = lax.ppermute(halves, ('rows', 'cols'), from_first)]
  transfers between devices with their start and end apart: 10 -> 10, of which waited for: 6 -> 7; matrix products, arithmetic and copies ran while one was open for 0% -> 0% of each run, Pallas kernels for 9% -> 9%
where the time goes in v8:
time: 30.7 us; the launch traced here: 30.5 us
  starting transfers between devices  13.9 us (45%)
  waiting for transfers between devices  9.43 us (31%)
  Pallas kernels  6.46 us (21%)
  between operations  0.7 us (2%)
    ppermute x6, waiting for transfers between devices, exchange(): got[k] = lax.ppermute(messages[k], axis, pairs)  7.97 us
    ppermute x6, starting transfers between devices, exchange(): got[k] = lax.ppermute(messages[k], axis, pairs)  6.87 us
    pallas_call x9, Pallas kernels, run(): pl.pallas_call(kernel, out_shape=out_shape, in_specs=[place] * len(args),...  6.46 us
    ppermute x1, starting transfers between devices, local_square_(): across = lax.ppermute(halves, 'cols', [(p, p ^ 2) for p in range(cols)])  2.88 us
    ppermute x1, starting transfers between devices, local_square_(): cols_a = lax.ppermute(halves, ('rows', 'cols'), from_first)  2.03 us
    ppermute x1, starting transfers between devices, local_square_(): cols_b = lax.ppermute(halves, ('rows', 'cols'), from_second)  1.58 us
    ppermute x1, waiting for transfers between devices, local_square_(): partner = lax.ppermute(unit, 'cols', [(p, p ^ 1) for p in range(cols)])  0.84 us
  transfers between devices with their start and end apart: 10, of which 7 were waited for; matrix products, arithmetic and copies ran while one was open for 0% of the time, Pallas kernels for 9%

profile of v8, /device:TPU:0, one launch (start us, length us, event | category | flops | bytes accessed | tf_op | source)
XLA Modules:
  0.0 30.5 jit_solution(8722659294613032498)
XLA Ops:
  0.6 1.2 %shard_map.119 = (bf16[64,128]{1,0:T(8,128)(2,1)S(1)}, f32[128,64]{1,0:T(8,128)S(1)}, f32[128,64]{1,0:T(8,128)S(1)}, f32[1,64]{1,0:T(1,128)S(1)}, bf16[16,16,128...) custom-call(f32[16,8,64]{2,1,0:T(8,128)} %refs_0_.1, ...), custom_call_target="tpu_custom_call" | custom-call | tf_op jit(solution)/shard_map/pallas_call | solution.py:173
  1.8 0.6 %collective-permute-start = (bf16[64,128]{1,0:T(8,128)(2,1)S(1)}, bf16[64,128]{1,0:T(8,128)(2,1)S(1)}, u32[]{:S(2)}, u32[]{:S(2)}) collective-permute-start(bf16[64,128]{1,0:T(8,128)(2,1)S(1)} %get-tuple-element.36.own_ref), channel_id=1, source_target_pairs={{0,1},{1,0},{2,3},{3,2},{4,5},{5,4},{6,7},{7,6},{8,9},{9,8},{10,11... | collective-permute-start | bytes 49160 | tf_op jit(solution)/shard_map/ppermute | solution.py:581
  2.4 0.8 %collective-permute-done.other_ref = bf16[64,128]{1,0:T(8,128)(2,1)S(1)} collective-permute-done((bf16[64,128]{1,0:T(8,128)(2,1)S(1)}, bf16[64,128]{1,0:T(8,128)(2,1)S(1)}, u32[]{:S(2)}, u32[]{:S(2)}) %collective-permute-start) | collective-permute-done | bytes 16416 | tf_op jit(solution)/shard_map/ppermute | solution.py:581
  3.2 2.9 %collective-permute-start.3 = (bf16[128,128]{1,0:T(8,128)(2,1)S(1)}, bf16[128,128]{1,0:T(8,128)(2,1)S(1)}, u32[]{:S(2)}, u32[]{:S(2)}) collective-permute-start(bf16[128,128]{1,0:T(8,128)(2,1)S(1)} %shard_map.120.u0), channel_id=1, source_target_pairs={{0,2},{1,3},{2,0},{3,1},{4,6},{5,7},{6,4},{7,5},{8,10},{9,11},{10,... | collective-permute-start | bytes 98312 | tf_op jit(solution)/shard_map/ppermute | solution.py:590
  6.1 1.6 %collective-permute-start.2 = (bf16[128,128]{1,0:T(8,128)(2,1)S(1)}, bf16[128,128]{1,0:T(8,128)(2,1)S(1)}, u32[]{:S(2)}, u32[]{:S(2)}) collective-permute-start(bf16[128,128]{1,0:T(8,128)(2,1)S(1)} %shard_map.120.u0), channel_id=1, source_target_pairs={{0,4},{1,0},{2,8},{3,12},{4,5},{5,9},{6,1},{7,13},{8,10},{9,6},{10... | collective-permute-start | bytes 98312 | tf_op jit(solution)/shard_map/ppermute | solution.py:589
  7.7 2.0 %collective-permute-start.1 = (bf16[128,128]{1,0:T(8,128)(2,1)S(1)}, bf16[128,128]{1,0:T(8,128)(2,1)S(1)}, u32[]{:S(2)}, u32[]{:S(2)}) collective-permute-start(bf16[128,128]{1,0:T(8,128)(2,1)S(1)} %shard_map.120.u0), channel_id=1, source_target_pairs={{0,12},{1,8},{2,0},{3,4},{4,1},{5,13},{6,9},{7,5},{8,2},{9,14},{10... | collective-permute-start | bytes 98312 | tf_op jit(solution)/shard_map/ppermute | solution.py:588
  9.7 0.9 %shard_map.121 = (bf16[128,2048]{1,0:T(8,128)(2,1)S(1)}, bf16[128,2048]{1,0:T(8,128)(2,1)S(1)}, bf16[256,128]{1,0:T(8,128)(2,1)S(1)}, bf16[4,512,128]{2,1,0:T(8,128)(2,1)S(1)}, bf16[512,512]{1,0:T(8,128)(2,1)S(1)}) custom-call(bf16[16,16,128]{2,1,0:T(8,128)(2,1)S(1)} %get-tuple-element.37.cot_ref, bf16[1024,128]{1,0:T(8,128)(2,1)S(1)} %get-tuple-element.38.final_ref, ...), custom_call_target="tpu_custom_call" | custom-call | flops 268435456 | tf_op jit(solution)/shard_map/pallas_call | solution.py:173
  10.6 0.0 collective-permute-done.3.u1
  10.6 0.8 %shard_map.122 = (bf16[128,128]{1,0:T(8,128)(2,1)S(1)}, bf16[128,256]{1,0:T(8,128)(2,1)S(1)}, f32[4,32,128]{2,1,0:T(8,128)S(1)}) custom-call(bf16[128,128]{1,0:T(8,128)(2,1)S(1)} %shard_map.120.u0, bf16[128,128]{1,0:T(8,128)(2,1)S(1)} %collective-permute-done.3.u1, bf16[4,512,128]{2,1,0:T(8,128)(2,1)S(1)} %get-tuple-element.41.weight_ref, ...), custom_call_target="tpu_custom_call" | custom-call | flops 100000000 | tf_op jit(solution)/shard_map/pallas_call | solution.py:173
  11.4 0.0 collective-permute-done.2.u1
  11.4 0.6 %collective-permute-done.1.u0 = bf16[128,128]{1,0:T(8,128)(2,1)S(1)} collective-permute-done((bf16[128,128]{1,0:T(8,128)(2,1)S(1)}, bf16[128,128]{1,0:T(8,128)(2,1)S(1)}, u32[]{:S(2)}, u32[]{:S(2)}) %collective-permute-start.1) | collective-permute-done | bytes 32800 | tf_op jit(solution)/shard_map/ppermute | solution.py:588
  12.1 1.5 %shard_map.123 = (bf16[256,1024]{1,0:T(8,128)(2,1)S(1)}, f32[352,128]{1,0:T(8,128)S(1)}, bf16[352,128]{1,0:T(8,128)(2,1)S(1)}, bf16[352,128]{1,0:T(8,128)(2,1)S(1)}, bf16[352,128]{1,0:T(8,128)(2,1)S(1)}) custom-call(bf16[128,128]{1,0:T(8,128)(2,1)S(1)} %collective-permute-done.1.u0, bf16[128,128]{1,0:T(8,128)(2,1)S(1)} %collective-permute-done.2.u1, ...), custom_call_target="tpu_custom_call" | custom-call | tf_op jit(solution)/shard_map/pallas_call | solution.py:173
  13.5 4.4 %collective-permute-start.4 = (bf16[352,128]{1,0:T(8,128)(2,1)S(1)}, bf16[352,128]{1,0:T(8,128)(2,1)S(1)}, u32[]{:S(2)}, u32[]{:S(2)}) collective-permute-start(bf16[352,128]{1,0:T(8,128)(2,1)S(1)} %get-tuple-element.52), channel_id=1, source_target_pairs={{0,3},{1,2},{2,1},{3,0},{4,7},{5,6},{6,5},{7,4},{8,11},{9,10},{10,... | collective-permute-start | bytes 270344 | tf_op jit(solution)/shard_map/ppermute | solution.py:513
  17.9 0.0 collective-permute-start.5
  17.9 0.2 collective-permute-start.6
  18.1 2.8 %collective-permute-done.4.r3 = bf16[352,128]{1,0:T(8,128)(2,1)S(1)} collective-permute-done((bf16[352,128]{1,0:T(8,128)(2,1)S(1)}, bf16[352,128]{1,0:T(8,128)(2,1)S(1)}, u32[]{:S(2)}, u32[]{:S(2)}) %collective-permute-start.4) | collective-permute-done | bytes 90144 | tf_op jit(solution)/shard_map/ppermute | solution.py:513
  20.9 2.1 %collective-permute-done.5.r2 = bf16[352,128]{1,0:T(8,128)(2,1)S(1)} collective-permute-done((bf16[352,128]{1,0:T(8,128)(2,1)S(1)}, bf16[352,128]{1,0:T(8,128)(2,1)S(1)}, u32[]{:S(2)}, u32[]{:S(2)}) %collective-permute-start.5) | collective-permute-done | bytes 90144 | tf_op jit(solution)/shard_map/ppermute | solution.py:513
  23.0 0.0 collective-permute-done.6.r1
  23.0 0.1 shard_map.125
  23.1 0.1 collective-permute-start.7
  23.1 1.6 %collective-permute-start.8 = (bf16[128,128]{1,0:T(8,128)(2,1)S(1)}, bf16[128,128]{1,0:T(8,128)(2,1)S(1)}, u32[]{:S(2)}, u32[]{:S(2)}) collective-permute-start(bf16[128,128]{1,0:T(8,128)(2,1)S(1)} %get-tuple-element.57), channel_id=1, source_target_pairs={{0,12},{4,8},{12,0},{8,4},{1,13},{5,9},{13,1},{9,5},{2,14},{6,10},... | collective-permute-start | bytes 98312 | tf_op jit(solution)/shard_map/ppermute | solution.py:513
  24.7 0.7 %collective-permute-start.9 = (bf16[128,128]{1,0:T(8,128)(2,1)S(1)}, bf16[128,128]{1,0:T(8,128)(2,1)S(1)}, u32[]{:S(2)}, u32[]{:S(2)}) collective-permute-start(bf16[128,128]{1,0:T(8,128)(2,1)S(1)} %get-tuple-element.58), channel_id=1, source_target_pairs={{0,4},{4,12},{12,8},{8,0},{1,5},{5,13},{13,9},{9,1},{2,6},{6,14},{... | collective-permute-start | bytes 98312 | tf_op jit(solution)/shard_map/ppermute | solution.py:513
  25.4 1.0 %shard_map.124 = bf16[16,16,128]{2,1,0:T(8,128)(2,1)} custom-call(bf16[256,1024]{1,0:T(8,128)(2,1)S(1)} %get-tuple-element.49.outer_ref, bf16[1024,128]{1,0:T(8,128)(2,1)S(1)} %get-tuple-element.38.final_ref, f32[1,128]{1,0:T(1,128)S(1)} %get-tuple-element.50.bias_ref), custom_call_target="tpu_custom_call" | custom-call | flops 100000000 | tf_op jit(solution)/shard_map/pallas_call | solution.py:173
  26.3 0.1 shard_map.126.unit_ref
  26.5 0.6 %collective-permute-done.7.r3 = bf16[128,128]{1,0:T(8,128)(2,1)S(1)} collective-permute-done((bf16[128,128]{1,0:T(8,128)(2,1)S(1)}, bf16[128,128]{1,0:T(8,128)(2,1)S(1)}, u32[]{:S(2)}, u32[]{:S(2)}) %collective-permute-start.7) | collective-permute-done | bytes 32800 | tf_op jit(solution)/shard_map/ppermute | solution.py:513
  27.0 1.9 %collective-permute-done.8.r2 = bf16[128,128]{1,0:T(8,128)(2,1)S(1)} collective-permute-done((bf16[128,128]{1,0:T(8,128)(2,1)S(1)}, bf16[128,128]{1,0:T(8,128)(2,1)S(1)}, u32[]{:S(2)}, u32[]{:S(2)}) %collective-permute-start.8) | collective-permute-done | bytes 32800 | tf_op jit(solution)/shard_map/ppermute | solution.py:513
  28.9 0.6 %collective-permute-done.9.r1 = bf16[128,128]{1,0:T(8,128)(2,1)S(1)} collective-permute-done((bf16[128,128]{1,0:T(8,128)(2,1)S(1)}, bf16[128,128]{1,0:T(8,128)(2,1)S(1)}, u32[]{:S(2)}, u32[]{:S(2)}) %collective-permute-start.9) | collective-permute-done | bytes 32800 | tf_op jit(solution)/shard_map/ppermute | solution.py:513
  29.5 1.0 %shard_map.127 = (f32[64,128]{1,0:T(8,128)}, f32[32,64]{1,0:T(8,128)}, f32[32,64]{1,0:T(8,128)}, f32[16,8,64]{2,1,0:T(8,128)}) custom-call(f32[128,128]{1,0:T(8,128)S(1)} %get-tuple-element.55.own_ref, bf16[128,128]{1,0:T(8,128)(2,1)S(1)} %collective-permute-done.7.r3, bf16[128,128]{1,0:T(8,128)(2,1)S(1)} %collective-permute-done.8.r2, ...), custom_call_target="tpu_custom_call" | custom-call | tf_op jit(solution)/shard_map/pallas_call | solution.py:173
  (1 shorter events, 0.0 us)
Async XLA Ops:
  1.8 1.4 %collective-permute-start = (bf16[64,128]{1,0:T(8,128)(2,1)S(1)}, bf16[64,128]{1,0:T(8,128)(2,1)S(1)}, u32[]{:S(2)}, u32[]{:S(2)}) collective-permute-start(bf16[64,128]{1,0:T(8,128)(2,1)S(1)} %get-tuple-element.36.own_ref), channel_id=1, source_target_pairs={{0,1},{1,0},{2,3},{3,2},{4,5},{5,4},{6,7},{7,6},{8,9},{9,8},{10,11... | collective-permute-start | bytes 49160 | tf_op jit(solution)/shard_map/ppermute | solution.py:581
  3.2 7.4 %collective-permute-start.3 = (bf16[128,128]{1,0:T(8,128)(2,1)S(1)}, bf16[128,128]{1,0:T(8,128)(2,1)S(1)}, u32[]{:S(2)}, u32[]{:S(2)}) collective-permute-start(bf16[128,128]{1,0:T(8,128)(2,1)S(1)} %shard_map.120.u0), channel_id=1, source_target_pairs={{0,2},{1,3},{2,0},{3,1},{4,6},{5,7},{6,4},{7,5},{8,10},{9,11},{10,... | collective-permute-start | bytes 98312 | tf_op jit(solution)/shard_map/ppermute | solution.py:590
  6.1 5.3 %collective-permute-start.2 = (bf16[128,128]{1,0:T(8,128)(2,1)S(1)}, bf16[128,128]{1,0:T(8,128)(2,1)S(1)}, u32[]{:S(2)}, u32[]{:S(2)}) collective-permute-start(bf16[128,128]{1,0:T(8,128)(2,1)S(1)} %shard_map.120.u0), channel_id=1, source_target_pairs={{0,4},{1,0},{2,8},{3,12},{4,5},{5,9},{6,1},{7,13},{8,10},{9,6},{10... | collective-permute-start | bytes 98312 | tf_op jit(solution)/shard_map/ppermute | solution.py:589
  7.7 4.4 %collective-permute-start.1 = (bf16[128,128]{1,0:T(8,128)(2,1)S(1)}, bf16[128,128]{1,0:T(8,128)(2,1)S(1)}, u32[]{:S(2)}, u32[]{:S(2)}) collective-permute-start(bf16[128,128]{1,0:T(8,128)(2,1)S(1)} %shard_map.120.u0), channel_id=1, source_target_pairs={{0,12},{1,8},{2,0},{3,4},{4,1},{5,13},{6,9},{7,5},{8,2},{9,14},{10... | collective-permute-start | bytes 98312 | tf_op jit(solution)/shard_map/ppermute | solution.py:588
  13.5 7.4 %collective-permute-start.4 = (bf16[352,128]{1,0:T(8,128)(2,1)S(1)}, bf16[352,128]{1,0:T(8,128)(2,1)S(1)}, u32[]{:S(2)}, u32[]{:S(2)}) collective-permute-start(bf16[352,128]{1,0:T(8,128)(2,1)S(1)} %get-tuple-element.52), channel_id=1, source_target_pairs={{0,3},{1,2},{2,1},{3,0},{4,7},{5,6},{6,5},{7,4},{8,11},{9,10},{10,... | collective-permute-start | bytes 270344 | tf_op jit(solution)/shard_map/ppermute | solution.py:513
  17.9 5.1 %collective-permute-start.5 = (bf16[352,128]{1,0:T(8,128)(2,1)S(1)}, bf16[352,128]{1,0:T(8,128)(2,1)S(1)}, u32[]{:S(2)}, u32[]{:S(2)}) collective-permute-start(bf16[352,128]{1,0:T(8,128)(2,1)S(1)} %get-tuple-element.53), channel_id=1, source_target_pairs={{0,2},{1,3},{2,0},{3,1},{4,6},{5,7},{6,4},{7,5},{8,10},{9,11},{10,... | collective-permute-start | bytes 270344 | tf_op jit(solution)/shard_map/ppermute | solution.py:513
  17.9 5.1 %collective-permute-start.6 = (bf16[352,128]{1,0:T(8,128)(2,1)S(1)}, bf16[352,128]{1,0:T(8,128)(2,1)S(1)}, u32[]{:S(2)}, u32[]{:S(2)}) collective-permute-start(bf16[352,128]{1,0:T(8,128)(2,1)S(1)} %get-tuple-element.54), channel_id=1, source_target_pairs={{0,1},{1,0},{2,3},{3,2},{4,5},{5,4},{6,7},{7,6},{8,9},{9,8},{10,11... | collective-permute-start | bytes 270344 | tf_op jit(solution)/shard_map/ppermute | solution.py:513
  23.1 4.0 %collective-permute-start.7 = (bf16[128,128]{1,0:T(8,128)(2,1)S(1)}, bf16[128,128]{1,0:T(8,128)(2,1)S(1)}, u32[]{:S(2)}, u32[]{:S(2)}) collective-permute-start(bf16[128,128]{1,0:T(8,128)(2,1)S(1)} %get-tuple-element.56), channel_id=1, source_target_pairs={{0,8},{4,0},{12,4},{8,12},{1,9},{5,1},{13,5},{9,13},{2,10},{6,2},{... | collective-permute-start | bytes 98312 | tf_op jit(solution)/shard_map/ppermute | solution.py:513
  23.1 5.8 %collective-permute-start.8 = (bf16[128,128]{1,0:T(8,128)(2,1)S(1)}, bf16[128,128]{1,0:T(8,128)(2,1)S(1)}, u32[]{:S(2)}, u32[]{:S(2)}) collective-permute-start(bf16[128,128]{1,0:T(8,128)(2,1)S(1)} %get-tuple-element.57), channel_id=1, source_target_pairs={{0,12},{4,8},{12,0},{8,4},{1,13},{5,9},{13,1},{9,5},{2,14},{6,10},... | collective-permute-start | bytes 98312 | tf_op jit(solution)/shard_map/ppermute | solution.py:513
  24.7 4.8 %collective-permute-start.9 = (bf16[128,128]{1,0:T(8,128)(2,1)S(1)}, bf16[128,128]{1,0:T(8,128)(2,1)S(1)}, u32[]{:S(2)}, u32[]{:S(2)}) collective-permute-start(bf16[128,128]{1,0:T(8,128)(2,1)S(1)} %get-tuple-element.58), channel_id=1, source_target_pairs={{0,4},{4,12},{12,8},{8,0},{1,5},{5,13},{13,9},{9,1},{2,6},{6,14},{... | collective-permute-start | bytes 98312 | tf_op jit(solution)/shard_map/ppermute | solution.py:513
